TPU v7x, 256 devices: a whole 4x4x8 slice. The times are simulated.
256 devices in a mesh: dp: 64 (over x, z_hi, y), mp: 4 (over z_lo, core).
Axes of the slice: x: 4, y: 4, z: 8 (z_hi: 4, z_lo: 2; z = z_hi * 2 + z_lo), core: 2. Of those that a mesh axis runs over, the one named last changes fastest.
Arguments:
- history_sequences: float32 [512, 512], P('dp'), may hold values from -65 to 65, as said below
- later_steps: float32 [512, 128], P('dp'), may hold values from -65 to 65
- patch_lift_matrix: bfloat16 [32, 1280], P(None, 'dp'), may hold values from -1 to 1
- scaling_factors: bfloat16 [2, 1280], P(None, 'dp'), may hold values from 0.5 to 1.5
- asking_matrix: bfloat16 [1280, 1280], P('dp', 'mp'), may hold values from -0.15625 to 0.15625
- lookup_matrix: bfloat16 [1280, 1280], P('dp', 'mp'), may hold values from -0.15625 to 0.15625
- content_matrix: bfloat16 [1280, 1280], P('dp', 'mp'), may hold values from -0.15625 to 0.15625
- attend_exit_matrix: bfloat16 [1280, 1280], P('mp', 'dp'), may hold values from -0.15625 to 0.15625
- outlook_matrix: bfloat16 [1280, 1280], P('dp', 'mp'), may hold values from -0.15625 to 0.15625
Outputs:
- loss_mean: float32 [], replicated
- embed_grad: float32 [32, 1280], P(None, 'dp')
- gains_grad: float32 [2, 1280], P(None, 'dp')
- query_grad: float32 [1280, 1280], P('dp', 'mp')
- key_grad: float32 [1280, 1280], P('dp', 'mp')
- value_grad: float32 [1280, 1280], P('dp', 'mp')
- output_grad: float32 [1280, 1280], P('mp', 'dp')
- head_weight_gradient: float32 [1280, 1280], P('dp', 'mp')
Inputs may be any that keep to these rules, and one draw needn't show every extreme that they name: `history_sequences`: later_steps continues the history of each series.
All inputs are finite; a program needn't handle non-finite values.
Results may differ from a plain program's by a relative error of at most 0.005.
Values may be sent and summed in bfloat16 or wider, within the bound.
No kernel may reach another device: no remote copies, remote signals or barrier semaphores. Data moves between devices by JAX's collectives and lax.ppermute only.
A program may use at most 64 MiB of HBM per device.

v0:
```python
import math

import jax
import jax.numpy as jnp
from jax import lax
from jax.sharding import Mesh
from jax.sharding import PartitionSpec as P

PATCH = 32
HORIZON_SPAN = 128
PATCHES = 16
LEVEL_CHANNELS = 10
HEAD_DIM = 80
DP = ("dp_0", "dp_1", "dp_2")
MP = ("mp_0", "mp_1")
DP_MP = ("dp_0", "dp_1", "dp_2", "mp_0", "mp_1")


EPS = 1e-06
STAT_EPS = 1e-05
SMOOTHING_RADIUS = 0.05


def gather_turned(arrays, axis, dims):
    turned = [jnp.moveaxis(a, dim, 0) for a, dim in zip(arrays, dims)]
    both = jnp.concatenate([t.reshape(len(t), -1) for t in turned], axis=1)
    out, at, outs = (lax.all_gather(both, axis, axis=0, tiled=True), 0, [])
    for t, dim in zip(turned, dims):
        piece = out[:, at : at + t[0].size].reshape(-1, *t.shape[1:])
        outs.append(jnp.moveaxis(piece, 0, dim))
        at += t[0].size
    return tuple(outs)


def in_one_piece(arrays, axis, dim, along):
    ends, at = ([], 0)
    for a in arrays[:-1]:
        at += a.shape[along]
        ends.append(at)
    both = jnp.concatenate(arrays, axis=along)
    return tuple(jnp.split(lax.all_gather(both, axis, axis=dim, tiled=True), ends, axis=along))


def from_everyone(x, axis):
    length = lax.axis_size(axis)
    return lax.all_to_all(jnp.broadcast_to(x[None], (length, *x.shape)), axis, 0, 0, tiled=True)


def over_copies(x, axis):
    return from_everyone(x, axis).sum(axis=0)


def by_axis(x, axes):
    for axis in axes:
        x = lax.psum(x, axis)
    return x


def taken_together(x, axis):
    return from_everyone(x, axis).astype(jnp.float32).sum(axis=0)


def split_up(x, dim, length):
    before, after = (x.shape[:dim], x.shape[dim + 1 :])
    return jnp.moveaxis(x.reshape(*before, length, -1, *after), dim, 0)


def sum_at_owner(x, axis, dim):
    length = lax.axis_size(axis)
    tiles = lax.all_to_all(split_up(x, dim, length), axis, 0, 0, tiled=True)
    return jnp.sum(tiles.astype(jnp.float32), axis=0)


def sent_together(arrays, axis, dim, along):
    ends, at = ([], 0)
    for a in arrays[:-1]:
        at += a.shape[along]
        ends.append(at)
    both = jnp.concatenate(arrays, axis=along)
    return tuple(jnp.split(sum_at_owner(both, axis, dim), ends, axis=along))


def summed_on_arrival(x, axis, dim):
    tiles = split_up(x, dim, lax.axis_size(axis))
    arrived = lax.all_to_all(tiles, axis, split_axis=0, concat_axis=0, tiled=True)
    return arrived.sum(axis=0)


def sent_together_2(arrays, axis, dim, along):
    both = jnp.concatenate(arrays, axis=along)
    out, at, outs = (summed_on_arrival(both, axis, dim), 0, [])
    for a in arrays:
        outs.append(lax.slice_in_dim(out, at, at + a.shape[along], axis=along))
        at += a.shape[along]
    return tuple(outs)


def rms_forward(residual, gain):
    factor = lax.rsqrt(jnp.mean(residual * residual, axis=1, keepdims=True) + EPS)
    return ((residual * factor * gain[None, :]).astype(jnp.bfloat16), factor)


def rms_backward(residual, factor, gain, upstream):
    weighted = gain[None, :] * upstream
    inner = jnp.mean(weighted * residual, axis=1, keepdims=True)
    back = factor * weighted - residual * factor * factor * factor * inner
    gain_term = jnp.sum(upstream * residual * factor, axis=0)
    return (back, gain_term)


def positions(length, width):
    half = width // 2
    freqs = jnp.exp(-math.log(10000.0) * jnp.arange(half, dtype=jnp.float32) / half)
    angles = jnp.arange(length, dtype=jnp.float32)[:, None] * freqs[None, :]
    return jnp.concatenate([jnp.sin(angles), jnp.cos(angles)], axis=1)


def prepare(history_sequences, later_steps):
    number = history_sequences.shape[0]
    centre = jnp.mean(history_sequences, axis=1, keepdims=True)
    spread = jnp.sqrt(
        jnp.mean((history_sequences - centre) * (history_sequences - centre), axis=1, keepdims=True)
        + STAT_EPS
    )
    normed = (history_sequences - centre) / spread
    ahead = (later_steps - centre) / spread
    joined = jnp.concatenate([normed, ahead], axis=1).reshape(number, -1, PATCH)
    reach = later_steps.shape[1] // PATCH
    future_values = jnp.concatenate(
        [joined[:, offset + 1 : offset + 1 + PATCHES] for offset in range(reach)], axis=2
    )
    future_values = future_values.reshape(number * PATCHES, reach * PATCH)
    patches = normed.reshape(number * PATCHES, PATCH).astype(jnp.bfloat16)
    return (patches, future_values)


def attention_forward(queries, keys, values, number):
    layout = (number, PATCHES, -1, HEAD_DIM)
    query_blocks = queries.reshape(layout)
    key_blocks = keys.reshape(layout)
    value_blocks = values.reshape(layout)
    scale = 1.0 / math.sqrt(HEAD_DIM)
    scores = (
        jnp.einsum("sihd,sjhd->shij", query_blocks, key_blocks, preferred_element_type=jnp.float32)
        * scale
    )
    place = jnp.arange(PATCHES)
    causal = place[:, None] >= place[None, :]
    raised = jnp.where(causal, jnp.exp(scores), 0.0)
    probs = raised / jnp.sum(raised, axis=3, keepdims=True)
    probs_low = probs.astype(jnp.bfloat16)
    context = jnp.einsum(
        "shij,sjhd->sihd", probs_low, value_blocks, preferred_element_type=jnp.float32
    )
    context = context.astype(jnp.bfloat16).reshape(number * PATCHES, -1)
    return (context, probs, probs_low)


def attention_backward(context_grad, queries, keys, values, probs, probs_low, number):
    layout = (number, PATCHES, -1, HEAD_DIM)
    query_blocks = queries.reshape(layout)
    key_blocks = keys.reshape(layout)
    value_blocks = values.reshape(layout)
    grad_blocks = context_grad.reshape(layout)
    scale = 1.0 / math.sqrt(HEAD_DIM)
    prob_grad = jnp.einsum(
        "sihd,sjhd->shij", grad_blocks, value_blocks, preferred_element_type=jnp.float32
    )
    value_back = jnp.einsum(
        "shij,sihd->sjhd", probs_low, grad_blocks, preferred_element_type=jnp.float32
    ).astype(jnp.bfloat16)
    centred = prob_grad - jnp.sum(probs * prob_grad, axis=3, keepdims=True)
    score_grad = (probs * centred * scale).astype(jnp.bfloat16)
    query_back = jnp.einsum(
        "shij,sjhd->sihd", score_grad, key_blocks, preferred_element_type=jnp.float32
    ).astype(jnp.bfloat16)
    key_back = jnp.einsum(
        "shij,sihd->sjhd", score_grad, query_blocks, preferred_element_type=jnp.float32
    ).astype(jnp.bfloat16)
    flat = (number * PATCHES, -1)
    return (query_back.reshape(flat), key_back.reshape(flat), value_back.reshape(flat))


def pinball_terms(estimate_entries, actual_entries):
    batch_example_tally = estimate_entries.shape[0]
    horizon_error = actual_entries[:, :, None] - estimate_entries.reshape(
        batch_example_tally, -1, LEVEL_CHANNELS
    )
    cumulative_share = jnp.arange(LEVEL_CHANNELS, dtype=jnp.float32) / LEVEL_CHANNELS
    mean_indicator = jnp.arange(LEVEL_CHANNELS) == 0
    lopsided_errors = jnp.where(
        mean_indicator,
        horizon_error * horizon_error,
        cumulative_share * horizon_error
        + SMOOTHING_RADIUS * jax.nn.softplus(-horizon_error / SMOOTHING_RADIUS),
    )
    skew_coefficient = (
        jnp.where(
            mean_indicator,
            -2.0 * horizon_error,
            jax.nn.sigmoid(-horizon_error / SMOOTHING_RADIUS) - cumulative_share,
        )
        / HORIZON_SPAN
    )
    return (
        jnp.sum(lopsided_errors) / HORIZON_SPAN,
        skew_coefficient.reshape(batch_example_tally, -1).astype(jnp.bfloat16),
    )


def multiplied_rows(left, right):

    def term(start, count):
        return jnp.dot(left, right, preferred_element_type=jnp.float32)

    return term


def per_device(
    history_sequences,
    later_steps,
    patch_lift_matrix,
    scaling_factors,
    asking_matrix,
    lookup_matrix,
    content_matrix,
    attend_exit_matrix,
    outlook_matrix,
):
    number = history_sequences.shape[0]
    rows_all = number * PATCHES
    patches, future_values = prepare(history_sequences, later_steps)
    embed_full, gains_full = gather_turned((patch_lift_matrix, scaling_factors), DP, (1, 1))
    gains = gains_full.astype(jnp.float32)
    query_full, key_full, value_full, outlook_collected = in_one_piece(
        (asking_matrix, lookup_matrix, content_matrix, outlook_matrix), DP, 0, 1
    )
    output_full = lax.all_gather(attend_exit_matrix, DP, axis=1, tiled=True)
    residual_zero = jnp.dot(patches, embed_full, preferred_element_type=jnp.float32) + jnp.tile(
        positions(PATCHES, embed_full.shape[1]), (number, 1)
    )
    normed_attn, factor_attn = rms_forward(residual_zero, gains[0])
    queries = jnp.dot(normed_attn, query_full, preferred_element_type=jnp.float32).astype(
        jnp.bfloat16
    )
    keys = jnp.dot(normed_attn, key_full, preferred_element_type=jnp.float32).astype(jnp.bfloat16)
    values = jnp.dot(normed_attn, value_full, preferred_element_type=jnp.float32).astype(
        jnp.bfloat16
    )
    context, probs, probs_low = attention_forward(queries, keys, values, number)
    attn_term = multiplied_rows(context, output_full)
    residual_one = residual_zero + over_copies(attn_term(0, rows_all), MP)
    normed_head, factor_head = rms_forward(residual_one, gains[1])
    estimate_entries = jnp.dot(normed_head, outlook_collected, preferred_element_type=jnp.float32)
    device_portion = estimate_entries.shape[1] // LEVEL_CHANNELS
    actual_entries = lax.dynamic_slice_in_dim(
        future_values, lax.axis_index(MP) * device_portion, device_portion, 1
    )
    device_loss, estimate_derivative = pinball_terms(estimate_entries, actual_entries)
    total_loss_value = by_axis(device_loss, DP_MP)
    loss_mean = total_loss_value / (number * PATCHES * lax.axis_size(DP))
    head_weight_gradient = jnp.dot(
        normed_head.T, estimate_derivative, preferred_element_type=jnp.float32
    )
    head_contribution = multiplied_rows(estimate_derivative, outlook_collected.T)
    head_reverse = taken_together(head_contribution(0, rows_all).astype(jnp.bfloat16), MP).astype(
        jnp.float32
    )
    residual_one_grad, gain_one = rms_backward(residual_one, factor_head, gains[1], head_reverse)
    attn_low = residual_one_grad.astype(jnp.bfloat16)
    output_grad = jnp.dot(context.T, attn_low, preferred_element_type=jnp.float32)
    context_grad = jnp.dot(attn_low, output_full.T, preferred_element_type=jnp.float32).astype(
        jnp.bfloat16
    )
    query_back, key_back, value_back = attention_backward(
        context_grad, queries, keys, values, probs, probs_low, number
    )
    query_grad = jnp.dot(normed_attn.T, query_back, preferred_element_type=jnp.float32)
    key_grad = jnp.dot(normed_attn.T, key_back, preferred_element_type=jnp.float32)
    value_grad = jnp.dot(normed_attn.T, value_back, preferred_element_type=jnp.float32)
    total = jnp.dot(query_back, query_full.T, preferred_element_type=jnp.float32)
    total = total + jnp.dot(key_back, key_full.T, preferred_element_type=jnp.float32)
    attn_back = taken_together(
        (total + jnp.dot(value_back, value_full.T, preferred_element_type=jnp.float32)).astype(
            jnp.bfloat16
        ),
        MP,
    ).astype(jnp.float32)
    norm_back_zero, gain_zero = rms_backward(residual_zero, factor_attn, gains[0], attn_back)
    residual_zero_grad = residual_one_grad + norm_back_zero
    embed_grad = jnp.dot(
        patches.T, residual_zero_grad.astype(jnp.bfloat16), preferred_element_type=jnp.float32
    )
    gains_grad = jnp.stack([gain_zero, gain_one], axis=0)
    query_grad, key_grad, value_grad, head_weight_gradient = sent_together(
        (
            query_grad.astype(jnp.bfloat16),
            key_grad.astype(jnp.bfloat16),
            value_grad.astype(jnp.bfloat16),
            head_weight_gradient.astype(jnp.bfloat16),
        ),
        DP,
        0,
        1,
    )
    output_grad = sum_at_owner(output_grad.astype(jnp.bfloat16), DP, 1)
    embed_grad, gains_grad = sent_together_2((embed_grad, gains_grad), DP, 1, 0)
    return (
        loss_mean,
        embed_grad,
        gains_grad,
        query_grad,
        key_grad,
        value_grad,
        output_grad,
        head_weight_gradient,
    )


def solution(mesh):
    split = Mesh(mesh.devices.reshape(4, 4, 4, 2, 2), ("dp_0", "dp_1", "dp_2", "mp_0", "mp_1"))
    placed = (
        P(DP, None),
        P(DP, None),
        P(None, DP),
        P(None, DP),
        P(DP, MP),
        P(DP, MP),
        P(DP, MP),
        P(MP, DP),
        P(DP, MP),
    )
    return jax.shard_map(
        per_device,
        mesh=split,
        in_specs=placed,
        out_specs=(
            P(),
            P(None, DP),
            P(None, DP),
            P(DP, MP),
            P(DP, MP),
            P(DP, MP),
            P(MP, DP),
            P(DP, MP),
        ),
        check_vma=False,
    )
```

profile of v0, /device:TPU:1, one launch (start us, length us, event | category | flops | bytes accessed | tf_op | source)
XLA Modules:
  0.0 718.7 jit_solution(1902449885133331667)
XLA Ops:
  12.9 172.1 %all-gather = bf16[64,20,34]{2,1,0:T(8,128)(2,1)S(1)} all-gather(bf16[1,20,34]{2,1,0:T(8,128)(2,1)S(1)} %maximum_bitcast_fusion.1), channel_id=1, replica_groups=mesh['dp_0'=4,'dp_1'=4,'dp_2'=4,'mp_0'=2,'mp_1'=2] {'dp_0','dp_1','dp_2'}, dimensions={0}, use_global_device_ids=true | all-gather | bytes 88400 | tf_op jit(solution)/shard_map/all_gather | solution.py:27
  185.5 164.7 %all-gather.2 = bf16[64,20,320]{2,1,0:T(8,128)(2,1)S(1)} all-gather(bf16[1,20,320]{2,1,0:T(8,128)(2,1)} %bitcast.63), channel_id=1, replica_groups=mesh['dp_0'=4,'dp_1'=4,'dp_2'=4,'mp_0'=2,'mp_1'=2] {'dp_0','dp_1','dp_2'}, dimensions={0}, use_global_device_ids=true | all-gather | bytes 832000 | tf_op jit(solution)/shard_map/all_gather | solution.py:238
  351.5 6.2 reshape.143
  359.4 2.3 convolution_convert_fusion.11
  367.1 57.9 %all-to-all-start = ((f32[4,128,1280]{2,1,0:T(8,128)}), f32[4,128,1280]{2,1,0:T(8,128)S(1)}, u32[]{:S(2)}, u32[]{:S(2)}) async-start(f32[4,128,1280]{2,1,0:T(8,128)} %broadcast_in_dim.61), calls=%async_computation | async-start | bytes 5242880 | tf_op jit(solution)/shard_map/all_to_all | solution.py:46
  428.8 26.1 %all-to-all-done = f32[4,128,1280]{2,1,0:T(8,128)S(1)} async-done(((f32[4,128,1280]{2,1,0:T(8,128)}), f32[4,128,1280]{2,1,0:T(8,128)S(1)}, u32[]{:S(2)}, u32[]{:S(2)}) %all-to-all-start) | async-done | bytes 2621472 | tf_op jit(solution)/shard_map/all_to_all | solution.py:46
  457.3 2.9 fusion.32
  460.2 2.1 convolution_convert_fusion.5
  463.4 5.5 all-to-all-start.1
  469.7 15.6 %all-to-all-done.1 = bf16[4,128,1280]{2,1,0:T(8,128)(2,1)} async-done(((bf16[4,128,1280]{2,1,0:T(8,128)(2,1)}), bf16[4,128,1280]{2,1,0:T(8,128)(2,1)}, u32[]{:S(2)}, u32[]{:S(2)}) %all-to-all-start.1) | async-done | bytes 1310752 | tf_op jit(solution)/shard_map/all_to_all | solution.py:46
  494.5 1.9 convolution_add_fusion.1
  499.1 4.7 all-to-all-start.2
  503.8 2.3 convolution_convert_fusion
  506.3 2.2 convolution_convert_fusion.1
  508.5 2.2 copy.121
  510.7 2.2 reshape.139
  515.6 4.5 all-to-all-done.2
  520.1 5.5 all-to-all-start.5
  529.7 2.4 reshape.150
  532.1 25.7 %all-to-all-done.5 = bf16[64,320,20]{1,2,0:T(8,128)(2,1)} async-done(((bf16[64,320,20]{1,2,0:T(8,128)(2,1)}), bf16[64,320,20]{1,2,0:T(8,128)(2,1)}, u32[]{:S(2)}, u32[]{:S(2)}) %all-to-all-start.5) | async-done | bytes 819232 | tf_op jit(solution)/shard_map/all_to_all | solution.py:70
  557.8 7.1 all-to-all-start.3
  565.0 3.0 pad_maximum_fusion
  568.0 5.7 copy.120
  573.7 6.1 reshape.138
  579.7 12.4 %all-to-all-start.4 = ((bf16[64,20,1280]{2,1,0:T(8,128)(2,1)}), bf16[64,20,1280]{2,1,0:T(8,128)(2,1)}, u32[]{:S(2)}, u32[]{:S(2)}) async-start(bf16[64,20,1280]{2,1,0:T(8,128)(2,1)} %reshape.138), calls=%async_computation.4 | async-start | bytes 7864320 | tf_op jit(solution)/shard_map/all_to_all | solution.py:70
  592.8 16.2 %psum.35 = f32[]{:T(128)} all-reduce(f32[]{:T(128)S(6)} %div.89), channel_id=1, replica_groups=mesh['dp_0'=4,'dp_1'=4,'dp_2'=4,'mp_0'=2,'mp_1'=2] {'dp_0'}, use_global_device_ids=true, to_apply=%region_7.8 | all-reduce | flops 1 | bytes 8 | tf_op jit(solution)/shard_map/psum | solution.py:55
  609.0 68.8 %psum.36 = f32[]{:T(128)} all-reduce(f32[]{:T(128)} %psum.35), channel_id=1, replica_groups=mesh['dp_0'=4,'dp_1'=4,'dp_2'=4,'mp_0'=2,'mp_1'=2] {'dp_1'}, use_global_device_ids=true, to_apply=%region_8.9 | all-reduce | flops 1 | bytes 8 | tf_op jit(solution)/shard_map/psum | solution.py:55
  677.8 12.2 %psum.37 = f32[]{:T(128)} all-reduce(f32[]{:T(128)} %psum.36), channel_id=1, replica_groups=mesh['dp_0'=4,'dp_1'=4,'dp_2'=4,'mp_0'=2,'mp_1'=2] {'dp_2'}, use_global_device_ids=true, to_apply=%region_9.10 | all-reduce | flops 1 | bytes 8 | tf_op jit(solution)/shard_map/psum | solution.py:55
  690.0 4.4 psum.38
  694.4 7.3 %psum.39 = f32[]{:T(128)} all-reduce(f32[]{:T(128)} %psum.38), channel_id=1, replica_groups=mesh['dp_0'=4,'dp_1'=4,'dp_2'=4,'mp_0'=2,'mp_1'=2] {'mp_1'}, use_global_device_ids=true, to_apply=%region_11.12 | all-reduce | flops 1 | bytes 8 | tf_op jit(solution)/shard_map/psum | solution.py:55
  702.4 2.1 convert_reduce_fusion.3
  707.2 2.8 convert_reduce_fusion
  (158 shorter events, 44.5 us)
Async XLA Ops:
  7.2 344.3 %all-gather.5.cloned.1.call-start = ((), (), s32[]{:S(2)}) async-start(), calls=%async_computation.6 | async-start | bytes 3993600 | tf_op jit(solution)/shard_map/all_gather | solution.py:41
  11.4 339.6 %copy-start.11 = (bf16[128,32]{1,0:T(8,128)(2,1)}, bf16[128,32]{1,0:T(8,128)(2,1)S(1)}, u32[]{:S(2)}) copy-start(bf16[128,32]{1,0:T(8,128)(2,1)S(1)} %convert_element_type.104) | copy-start | bytes 24580
  350.6 14.3 %copy-start = (bf16[1280,320]{1,0:T(8,128)(2,1)}, bf16[1280,320]{1,0:T(8,128)(2,1)S(1)}, u32[]{:S(2)}) copy-start(bf16[1280,320]{1,0:T(8,128)(2,1)S(1)} %reshape.145) | copy-start | bytes 2457604
  351.3 6.4 copy-start.21
  351.4 10.3 %copy-start.2 = (bf16[128,1280]{1,0:T(8,128)(2,1)}, bf16[128,1280]{1,0:T(8,128)(2,1)S(1)}, u32[]{:S(2)}) copy-start(bf16[128,1280]{1,0:T(8,128)(2,1)S(1)} %multiply_convert_fusion.1) | copy-start | bytes 983044
  363.9 3.1 copy-start.15
  364.2 2.9 copy-start.17
  364.5 2.6 copy-start.25
  364.9 2.2 copy-start.6
  367.1 59.2 %copy-start.23 = (f32[8,128]{1,0:T(8,128)S(1)}, f32[8,128]{1,0:T(8,128)}, u32[]{:S(2)}) copy-start(f32[8,128]{1,0:T(8,128)} %param.10) | copy-start | bytes 12292
  367.1 87.9 %all-to-all-start = ((f32[4,128,1280]{2,1,0:T(8,128)}), f32[4,128,1280]{2,1,0:T(8,128)S(1)}, u32[]{:S(2)}, u32[]{:S(2)}) async-start(f32[4,128,1280]{2,1,0:T(8,128)} %broadcast_in_dim.61), calls=%async_computation | async-start | bytes 5242880 | tf_op jit(solution)/shard_map/all_to_all | solution.py:46
  428.8 28.4 %copy-start.13 = (f32[128,320]{0,1:T(8,128)S(1)}, f32[128,320]{0,1:T(8,128)}, u32[]{:S(2)}) copy-start(f32[128,320]{0,1:T(8,128)} %sub.62) | copy-start | bytes 491524
  428.8 28.4 %copy-start.20 = (f32[320]{0:T(512)S(1)}, f32[320]{0:T(512)}, u32[]{:S(2)}) copy-start(f32[320]{0:T(512)} %mul.236) | copy-start | bytes 3844
  428.8 28.4 %copy-start.24 = (pred[320]{0:T(512)(128)(4,1)S(1)}, pred[320]{0:T(512)(128)(4,1)}, u32[]{:S(2)}) copy-start(pred[320]{0:T(512)(128)(4,1)} %broadcast_in_dim.30) | copy-start | bytes 964
  460.2 3.2 copy-start.14
  460.2 8.8 %copy-start.26 = (f32[8,4,16,16]{2,3,1,0:T(8,128)S(1)}, f32[8,4,16,16]{2,3,1,0:T(8,128)}, u32[]{:S(2)}) copy-start(f32[8,4,16,16]{2,3,1,0:T(8,128)} %copy-done.25) | copy-start | bytes 98308
  463.4 21.9 %all-to-all-start.1 = ((bf16[4,128,1280]{2,1,0:T(8,128)(2,1)}), bf16[4,128,1280]{2,1,0:T(8,128)(2,1)}, u32[]{:S(2)}, u32[]{:S(2)}) async-start(bf16[4,128,1280]{2,1,0:T(8,128)(2,1)} %broadcast_in_dim.62), calls=%async_computation.1 | async-start | bytes 2621440 | tf_op jit(solution)/shard_map/all_to_all | solution.py:46
  468.9 18.4 %copy-start.1 = (bf16[1280,320]{1,0:T(8,128)(2,1)S(1)}, bf16[1280,320]{1,0:T(8,128)(2,1)}, u32[]{:S(2)}) copy-start(bf16[1280,320]{1,0:T(8,128)(2,1)} %copy-done) | copy-start | bytes 2457604
  469.7 18.4 %copy-start.10 = (bf16[8,16,4,80]{3,2,1,0:T(4,128)(2,1)S(1)}, bf16[8,16,4,80]{3,2,1,0:T(4,128)(2,1)}, u32[]{:S(2)}) copy-start(bf16[8,16,4,80]{3,2,1,0:T(4,128)(2,1)} %copy-done.9) | copy-start | bytes 245764
  486.9 1.5 copy-start.16
  486.9 2.7 copy-start.18
  492.4 5.6 copy-start.7
  499.1 20.9 %all-to-all-start.2 = ((bf16[4,128,1280]{2,1,0:T(8,128)(2,1)}), bf16[4,128,1280]{2,1,0:T(8,128)(2,1)S(1)}, u32[]{:S(2)}, u32[]{:S(2)}) async-start(bf16[4,128,1280]{2,1,0:T(8,128)(2,1)} %broadcast_in_dim.63), calls=%async_computation.2 | async-start | bytes 2621440 | tf_op jit(solution)/shard_map/all_to_all | solution.py:46
  506.1 6.9 copy-start.3
  510.7 14.8 %copy-start.8 = (bf16[128,320]{1,0:T(8,128)(2,1)S(1)}, bf16[128,320]{1,0:T(8,128)(2,1)}, u32[]{:S(2)}) copy-start(bf16[128,320]{1,0:T(8,128)(2,1)} %copy-done.7) | copy-start | bytes 245764
  514.3 12.8 %copy-start.22 = (f32[128]{0:T(128)S(1)}, f32[128]{0:T(128)}, u32[]{:S(2)}) copy-start(f32[128]{0:T(128)} %copy-done.21) | copy-start | bytes 1540
  520.1 37.8 %all-to-all-start.5 = ((bf16[64,320,20]{1,2,0:T(8,128)(2,1)}), bf16[64,320,20]{1,2,0:T(8,128)(2,1)}, u32[]{:S(2)}, u32[]{:S(2)}) async-start(bf16[64,320,20]{1,2,0:T(8,128)(2,1)} %bitcast.55), calls=%async_computation.5 | async-start | bytes 2359296 | tf_op jit(solution)/shard_map/all_to_all | solution.py:70
  527.5 37.5 %copy-start.4 = (bf16[1280,320]{0,1:T(8,128)(2,1)S(1)}, bf16[1280,320]{0,1:T(8,128)(2,1)}, u32[]{:S(2)}) copy-start(bf16[1280,320]{0,1:T(8,128)(2,1)} %convolution_convert_fusion.2) | copy-start | bytes 2457604
  527.7 37.3 %copy-start.5 = (bf16[1280,320]{0,1:T(8,128)(2,1)S(1)}, bf16[1280,320]{0,1:T(8,128)(2,1)}, u32[]{:S(2)}) copy-start(bf16[1280,320]{0,1:T(8,128)(2,1)} %convolution_convert_fusion.3) | copy-start | bytes 2457604
  557.8 21.9 %all-to-all-start.3 = ((f32[64,1,680]{2,1,0:T(1,128)}), f32[64,1,680]{2,1,0:T(1,128)S(1)}, u32[]{:S(2)}, u32[]{:S(2)}) async-start(f32[64,1,680]{2,1,0:T(1,128)} %reshape.150), calls=%async_computation.3 | async-start | bytes 393216 | tf_op jit(solution)/shard_map/all_to_all | solution.py:85
  579.7 127.5 %all-to-all-start.4 = ((bf16[64,20,1280]{2,1,0:T(8,128)(2,1)}), bf16[64,20,1280]{2,1,0:T(8,128)(2,1)}, u32[]{:S(2)}, u32[]{:S(2)}) async-start(bf16[64,20,1280]{2,1,0:T(8,128)(2,1)} %reshape.138), calls=%async_computation.4 | async-start | bytes 7864320 | tf_op jit(solution)/shard_map/all_to_all | solution.py:70
  706.5 4.2 copy-start.19
  (2 other events, 1.9 us)
Sparse Core Ops, SparseCore 0:
  11.2 90.6 all-gather.4
where the time goes:
time: 721 us; the launch traced here: 719 us
  blocking collectives  446 us (62%)
  starting transfers between devices  93.1 us (13%)
  waiting for transfers between devices  72 us (10%)
  local copies, waits for them, and re-layouts  41.5 us (6%)
  matrix products  30.4 us (4%)
  other arithmetic  18.8 us (3%)
  between operations  17.2 us (2%)
    all_gather x1, blocking collectives, gather_turned(): out, at, outs = (lax.all_gather(both, axis, axis=0, tiled=True), 0, [])  172 us
    all_gather x1, blocking collectives, per_device(): output_full = lax.all_gather(attend_exit_matrix, DP, axis=1, tiled=True)  165 us
    psum x5, blocking collectives, by_axis(): x = lax.psum(x, axis)  109 us
    all_to_all x3, starting transfers between devices, from_everyone(): lax.all_to_all(jnp.broadcast_to(x[None], (length, *x.shape)), axis, 0, 0,...  68 us
    all_to_all x3, waiting for transfers between devices, from_everyone(): lax.all_to_all(jnp.broadcast_to(x[None], (length, *x.shape)), axis, 0, 0,...  46.2 us
    all_to_all x2, waiting for transfers between devices, sum_at_owner(): tiles = lax.all_to_all(split_up(x, dim, length), axis, 0, 0, tiled=True)  25.7 us
    all_to_all x2, starting transfers between devices, sum_at_owner(): tiles = lax.all_to_all(split_up(x, dim, length), axis, 0, 0, tiled=True)  17.9 us
  transfers between devices with their start and end apart: 7, of which 4 were waited for; matrix products, arithmetic and copies ran while one was open for 7% of the time, Pallas kernels for 0%

commit v1 on v0

v1 whole, which is shorter than its diff:
```python
import math

import jax
import jax.numpy as jnp
import numpy as np
from jax import lax
from jax.experimental import pallas as pl
from jax.experimental.pallas import tpu as pltpu
from jax.sharding import Mesh
from jax.sharding import PartitionSpec as P

WIDTH = 1280
PATCH = 32
PATCHES = 16
HEAD_DIM = 80
CHANNELS = 10
BLOCKS = 64
OWN = WIDTH // BLOCKS
PADDED = 24
ROWS = BLOCKS * PADDED
TOKENS = 128
COLS = 320
WIDE = 384
BASIS = PATCH + PATCHES
TILES = (BASIS // 8) * (3 * WIDE // 128)
DP = ("dp_0", "dp_1", "dp_2")
MP = ("mp_0", "mp_1")
EPS = 1e-06
STAT_EPS = 1e-05
RADIUS = 0.05
SCALE = 1.0 / math.sqrt(HEAD_DIM)
BF = jnp.bfloat16
F32 = jnp.float32


def nn(a, b):
    return lax.dot_general(a, b, (((1,), (0,)), ((), ())), preferred_element_type=F32)


def nt(a, b):
    return lax.dot_general(a, b, (((1,), (1,)), ((), ())), preferred_element_type=F32)


def tn(a, b):
    return lax.dot_general(a, b, (((0,), (0,)), ((), ())), preferred_element_type=F32)


def two(x):
    high = x.astype(BF)
    return high, (x - high.astype(F32)).astype(BF)


def position_table():
    half = WIDTH // 2
    freqs = np.exp(np.float32(-math.log(10000.0)) * np.arange(half, dtype=np.float32) / np.float32(half))
    angles = np.arange(PATCHES, dtype=np.float32)[:, None] * freqs[None, :]
    table = np.concatenate([np.sin(angles), np.cos(angles)], axis=1).astype(np.float32)
    return np.ascontiguousarray(table.reshape(PATCHES, BLOCKS, OWN).transpose(1, 0, 2))


def call(body, outs, *args):
    return pl.pallas_call(
        body,
        out_shape=[jax.ShapeDtypeStruct(s, d) for s, d in outs],
        name=body.__name__,
    )(*args)


def basis_kernel(embed_ref, gains_ref, pos_ref, wq_ref, wk_ref, wv_ref, out_ref):
    basis = jnp.concatenate([embed_ref[...].astype(F32), pos_ref[...]], axis=0)
    high, low = two(basis * gains_ref[0:1, :].astype(F32))
    out_ref[...] = jnp.zeros_like(out_ref)
    for w, ref in enumerate((wq_ref, wk_ref, wv_ref)):
        weight = ref[...]
        part = nn(high, weight) + nn(low, weight)
        for i in range(BASIS // 8):
            rows = part[8 * i : 8 * i + 8]
            out_ref[9 * i + 3 * w] = rows[:, 0:128]
            out_ref[9 * i + 3 * w + 1] = rows[:, 128:256]
            out_ref[9 * i + 3 * w + 2, :, 0:64] = rows[:, 256:320]


def from_tiles(ref):
    return jnp.concatenate(
        [jnp.concatenate([ref[9 * i + j] for j in range(9)], axis=1) for i in range(BASIS // 8)], axis=0
    )


def raw_projections(tiles_ref, basis):
    high, low = two(from_tiles(tiles_ref))
    return tn(jnp.concatenate([high, low], axis=0), jnp.concatenate([basis, basis], axis=0))


def first_residual(exit_ref, basis_ref):
    lanes = exit_ref[:, 256:384]
    entries = basis_ref[...]
    return nn(lanes, jnp.concatenate([jnp.zeros_like(entries), entries], axis=0))


def causal_mask():
    j = lax.broadcasted_iota(jnp.int32, (TOKENS, TOKENS), 0)
    i = lax.broadcasted_iota(jnp.int32, (TOKENS, TOKENS), 1)
    same = lax.shift_right_logical(j, 4) == lax.shift_right_logical(i, 4)
    return same & (j <= i)


def attention_kernel(
    exit_ref, tiles_ref, basis_ref, part_ref, context_ref, queries_ref, keys_ref, values_ref, probs_ref, factor_ref
):
    residual = first_residual(exit_ref, basis_ref)
    factor = lax.rsqrt(jnp.sum(residual * residual, axis=0, keepdims=True) / WIDTH + EPS)
    factor_ref[...] = jnp.broadcast_to(factor, factor_ref.shape)
    raw = raw_projections(tiles_ref, basis_ref[0:BASIS, :]) * factor
    queries_ref[...] = raw[0:COLS].astype(BF)
    keys_ref[...] = raw[WIDE : WIDE + COLS].astype(BF)
    values_ref[...] = raw[2 * WIDE : 2 * WIDE + COLS].astype(BF)
    mask = causal_mask()
    for h in range(COLS // HEAD_DIM):
        at = slice(h * HEAD_DIM, (h + 1) * HEAD_DIM)
        scores = tn(keys_ref[at, :], queries_ref[at, :]) * SCALE
        raised = jnp.where(mask, jnp.exp(scores), 0.0)
        probs = raised / jnp.sum(raised, axis=0, keepdims=True)
        probs_ref[h] = probs
        context_ref[at, :] = nn(values_ref[at, :], probs.astype(BF)).astype(BF)
    part_ref[...] = nn(exit_ref[:, 0:COLS], context_ref[...]).astype(BF)


def head_kernel(
    exit_ref, head_ref, basis_ref, near_ref, far_ref, target_ref, back_ref, grad_ref, residual_ref, factor_ref, loss_ref
):
    residual = first_residual(exit_ref, basis_ref) + (near_ref[...].astype(F32) + far_ref[...].astype(F32))
    residual_ref[...] = residual
    factor = lax.rsqrt(jnp.sum(residual * residual, axis=0, keepdims=True) / WIDTH + EPS)
    factor_ref[...] = jnp.broadcast_to(factor, factor_ref.shape)
    scaled = residual * factor
    normed = (scaled * head_ref[:, COLS + 1 : COLS + 2].astype(F32)).astype(BF)
    forecast = tn(head_ref[...], normed)[0:COLS]
    column = lax.broadcasted_iota(jnp.int32, (COLS, 1), 0).astype(F32)
    step = jnp.floor((column + 0.5) * 0.1)
    channel = column - CHANNELS * step
    spread = (step == lax.broadcasted_iota(jnp.int32, (COLS, PATCH), 1).astype(F32)).astype(F32).astype(BF)
    target = target_ref[...]
    first, rest = target.astype(BF), target
    rest = rest - first.astype(F32)
    second, third = two(rest)
    expanded = nn(spread, first) + (nn(spread, second) + nn(spread, third))
    error = expanded - forecast
    share = channel / CHANNELS
    mean_channel = channel == 0.0
    inside = error / -RADIUS
    tail = jnp.exp(-jnp.abs(inside))
    softplus = jnp.maximum(inside, 0.0) + jnp.log1p(tail)
    sigmoid = jnp.where(inside >= 0.0, 1.0, tail) / (1.0 + tail)
    terms = jnp.where(mean_channel, error * error, share * error + RADIUS * softplus)
    loss_ref[...] = jnp.broadcast_to(jnp.sum(terms, axis=0, keepdims=True), loss_ref.shape)
    slope = (jnp.where(mean_channel, -2.0 * error, sigmoid - share) * (1.0 / 128.0)).astype(BF)
    slope = jnp.concatenate([slope, jnp.zeros((WIDE - COLS, TOKENS), BF)], axis=0)
    back = nn(head_ref[...], slope)
    back_ref[...] = back.astype(BF)
    high, low = two(jnp.sum(back * scaled, axis=1, keepdims=True))
    lane = lax.broadcasted_iota(jnp.int32, (1, WIDE), 1)
    grad = nt(normed, slope)
    grad = jnp.where(lane == COLS, high.astype(F32), jnp.where(lane == COLS + 1, low.astype(F32), grad))
    grad_ref[...] = grad.astype(BF)


def backward_kernel(
    exit_ref,
    head_ref,
    tiles_ref,
    basis_ref,
    near_ref,
    far_ref,
    residual_ref,
    factor_one_ref,
    factor_zero_ref,
    context_ref,
    queries_ref,
    keys_ref,
    values_ref,
    probs_ref,
    loss_ref,
    grad_ref,
    out_ref,
):
    basis = basis_ref[0:BASIS, :]
    patches = basis_ref[0:PATCH, :]
    upstream = near_ref[...].astype(F32) + far_ref[...].astype(F32)
    residual = residual_ref[...]
    factor = factor_one_ref[0:1, :]
    weighted = head_ref[:, COLS + 1 : COLS + 2].astype(F32) * upstream
    inner = jnp.sum(weighted * residual, axis=0, keepdims=True) / WIDTH
    low = (factor * weighted - residual * (factor * factor * factor * inner)).astype(BF)
    grad = nt(low, jnp.concatenate([context_ref[...], patches, patches], axis=0))
    lane = lax.broadcasted_iota(jnp.int32, (1, WIDE), 1)
    grad = jnp.where(lane >= COLS + PATCH, grad - grad.astype(BF).astype(F32), grad)
    grad_ref[...] = grad.astype(BF)
    context_grad = tn(exit_ref[...], low)[0:COLS].astype(BF)
    backs = ([], [], [])
    for h in range(COLS // HEAD_DIM):
        at = slice(h * HEAD_DIM, (h + 1) * HEAD_DIM)
        slope = context_grad[at]
        probs = probs_ref[h]
        prob_grad = tn(values_ref[at, :], slope)
        value_back = nt(slope, probs.astype(BF))
        centred = prob_grad - jnp.sum(probs * prob_grad, axis=0, keepdims=True)
        score_grad = (probs * centred * SCALE).astype(BF)
        backs[0].append(nn(keys_ref[at, :], score_grad).astype(BF))
        backs[1].append(nt(queries_ref[at, :], score_grad).astype(BF))
        backs[2].append(value_back.astype(BF))
    gap = jnp.zeros((WIDE - COLS, TOKENS), BF)
    back = jnp.concatenate([*backs[0], gap, *backs[1], gap, *backs[2], gap], axis=0)
    factor = factor_zero_ref[0:1, :]
    entries = basis.astype(F32)
    high, low = two(entries * factor)
    total = nt(high, back) + nt(low, back)
    raw = raw_projections(tiles_ref, basis)
    inner = jnp.sum(back.astype(F32) * raw, axis=0, keepdims=True) / WIDTH
    high, low = two(entries * (factor * factor * factor * inner))
    mixed = nt(high, patches) + nt(low, patches)
    out_ref[...] = jnp.zeros_like(out_ref)
    for i in range(BASIS // 8):
        for j in range(9):
            out_ref[9 * i + j] = total[8 * i : 8 * i + 8, 128 * j : 128 * j + 128]
        out_ref[TILES + i, :, 0:PATCH] = mixed[8 * i : 8 * i + 8]
    out_ref[TILES + BASIS // 8] = loss_ref[...]


def exact(dims):
    def dot(a, b):
        return lax.dot_general(a, b, (dims, ((), ())), precision=lax.Precision.HIGHEST, preferred_element_type=F32)

    return dot


def last_kernel(
    tiles_ref, embed_ref, gains_ref, pos_ref, wq_ref, wk_ref, wv_ref, exit_ref, head_ref, q_ref, k_ref, v_ref, rest_ref
):
    basis = jnp.concatenate([embed_ref[...].astype(F32), pos_ref[...]], axis=0)
    scaled = basis * gains_ref[0:1, :].astype(F32)
    total = from_tiles(tiles_ref)
    scaled_grad = exact(((0,), (0,)))(scaled, total)
    plain_grad = exact(((0,), (0,)))(basis, total)
    embed = jnp.zeros((OWN, PATCH), F32)
    gain_zero = jnp.zeros((OWN, 1), F32)
    for w, (weight_ref, out_ref) in enumerate(((wq_ref, q_ref), (wk_ref, k_ref), (wv_ref, v_ref))):
        weight = weight_ref[...].astype(F32)
        out_ref[...] = scaled_grad[:, w * WIDE : w * WIDE + COLS]
        gain_zero += jnp.sum(weight * plain_grad[:, w * WIDE : w * WIDE + COLS], axis=1, keepdims=True)
        embed += exact(((1,), (1,)))(weight, total[0:PATCH, w * WIDE : w * WIDE + COLS])
    pick = (lax.broadcasted_iota(jnp.int32, (2, PATCH), 0) == 0).astype(F32)
    embed = embed * exact(((0,), (0,)))(gains_ref[...].astype(F32), pick)
    mixed = jnp.concatenate([tiles_ref[TILES + i] for i in range(BASIS // 8)], axis=0)[:, 0:PATCH]
    embed = embed - exact(((0,), (0,)))(basis, mixed)
    ends = exit_ref[0:OWN, COLS : COLS + PATCH] + exit_ref[0:OWN, COLS + PATCH : WIDE]
    gain_one = head_ref[0:OWN, COLS : COLS + 1] + head_ref[0:OWN, COLS + 1 : COLS + 2]
    loss = jnp.sum(tiles_ref[TILES + BASIS // 8][0:1, :], axis=1, keepdims=True)
    rest_ref[...] = jnp.zeros_like(rest_ref)
    rest_ref[0:OWN, 0:PATCH] = embed + 0.25 * ends
    rest_ref[0:OWN, PATCH : PATCH + 1] = gain_zero
    rest_ref[0:OWN, PATCH + 1 : PATCH + 2] = gain_one
    rest_ref[0:1, PATCH + 2 : PATCH + 3] = loss


def swapped(x, axis):
    return lax.ppermute(x, axis, [(0, 1), (1, 0)])


def mp_parts(part):
    near = (part.astype(F32) + swapped(part, "mp_1").astype(F32)).astype(BF)
    return near, swapped(near, "mp_0")


def to_everyone(x):
    return lax.all_to_all(jnp.broadcast_to(x[None], (BLOCKS, *x.shape)), DP, 0, 0, tiled=True)


def summed(x):
    return jnp.sum(lax.all_to_all(x, DP, 0, 0, tiled=True).astype(F32), axis=0)


def padded_rows(x):
    return jnp.pad(x, ((0, PADDED - OWN), (0, WIDE - x.shape[1])))


def prepare(history, later):
    number = history.shape[0]
    centre = jnp.mean(history, axis=1, keepdims=True)
    spread = jnp.sqrt(jnp.mean((history - centre) * (history - centre), axis=1, keepdims=True) + STAT_EPS)
    normed = (history - centre) / spread
    ahead = (later - centre) / spread
    joined = jnp.concatenate([normed, ahead], axis=1).reshape(number, -1, PATCH)
    member = lax.axis_index(MP)
    target = lax.dynamic_slice_in_dim(joined, member + 1, PATCHES, 1).reshape(number * PATCHES, PATCH)
    patches = joined[:, :PATCHES].reshape(number * PATCHES, PATCH).astype(BF)
    return patches.T, target.T


def per_device(history, later, embed, gains, asking, lookup, content, attend_exit, outlook):
    place = lax.axis_index(DP)
    pos = lax.dynamic_index_in_dim(jnp.asarray(position_table()), place, 0, keepdims=False)
    pos_high, pos_low = two(pos)
    exit_block = padded_rows(jnp.concatenate([attend_exit.T, embed.T, pos_high.T, pos_low.T], axis=1))
    head_block = padded_rows(jnp.concatenate([outlook, gains.T], axis=1))

    tiles = call(basis_kernel, [((BLOCKS, 8, 128), F32)], embed, gains, pos, asking, lookup, content)[0]
    tiles = to_everyone(summed(tiles))
    exit_all = to_everyone(exit_block).reshape(ROWS, WIDE)
    head_all = to_everyone(head_block).reshape(ROWS, WIDE)

    patches, target = prepare(history, later)
    number = np.arange(TOKENS) % PATCHES
    place_hot = jnp.asarray((np.arange(PATCHES)[:, None] == number[None, :]), dtype=BF)
    basis = jnp.concatenate([patches, place_hot, place_hot], axis=0)

    turned = (COLS, TOKENS)
    part, context, queries, keys, values, probs, factor_zero = call(
        attention_kernel,
        [
            ((ROWS, TOKENS), BF),
            (turned, BF),
            (turned, BF),
            (turned, BF),
            (turned, BF),
            ((COLS // HEAD_DIM, TOKENS, TOKENS), F32),
            ((8, TOKENS), F32),
        ],
        exit_all,
        tiles,
        basis,
    )
    near, far = mp_parts(part)
    back, head_grad, residual, factor_one, loss = call(
        head_kernel,
        [
            ((ROWS, TOKENS), BF),
            ((ROWS, WIDE), BF),
            ((ROWS, TOKENS), F32),
            ((8, TOKENS), F32),
            ((8, TOKENS), F32),
        ],
        exit_all,
        head_all,
        basis,
        near,
        far,
        target,
    )
    near, far = mp_parts(back)
    exit_grad, totals = call(
        backward_kernel,
        [((ROWS, WIDE), BF), ((BLOCKS, 8, 128), F32)],
        exit_all,
        head_all,
        tiles,
        basis,
        near,
        far,
        residual,
        factor_one,
        factor_zero,
        context,
        queries,
        keys,
        values,
        probs,
        loss,
    )
    totals = to_everyone(summed(totals))
    head_sum = summed(head_grad.reshape(BLOCKS, PADDED, WIDE))
    exit_sum = summed(exit_grad.reshape(BLOCKS, PADDED, WIDE))
    own = (OWN, COLS)
    query_grad, key_grad, value_grad, rest = call(
        last_kernel,
        [(own, F32), (own, F32), (own, F32), ((PADDED, 128), F32)],
        totals,
        embed,
        gains,
        pos,
        asking,
        lookup,
        content,
        exit_sum,
        head_sum,
    )
    rest = rest + swapped(rest, "mp_1")
    rest = rest + swapped(rest, "mp_0")
    loss_mean = rest[0, PATCH + 2] / 1048576.0
    return (
        loss_mean,
        rest[:OWN, :PATCH].T,
        rest[:OWN, PATCH : PATCH + 2].T,
        query_grad,
        key_grad,
        value_grad,
        exit_sum[:OWN, :COLS].T,
        head_sum[:OWN, :COLS],
    )


def solution(mesh):
    split = Mesh(mesh.devices.reshape(4, 4, 4, 2, 2), ("dp_0", "dp_1", "dp_2", "mp_0", "mp_1"))
    placed = (
        P(DP, None),
        P(DP, None),
        P(None, DP),
        P(None, DP),
        P(DP, MP),
        P(DP, MP),
        P(DP, MP),
        P(MP, DP),
        P(DP, MP),
    )
    return jax.shard_map(
        per_device,
        mesh=split,
        in_specs=placed,
        out_specs=(
            P(),
            P(None, DP),
            P(None, DP),
            P(DP, MP),
            P(DP, MP),
            P(DP, MP),
            P(MP, DP),
            P(DP, MP),
        ),
        check_vma=False,
    )
```

time: 721 us -> 292 us (0.40)
  blocking collectives: 446 us -> 91.5 us
  starting transfers between devices: 93.1 us -> 49.5 us
  waiting for transfers between devices: 72 us -> 107 us
  matrix products: 30.4 us -> 0 us
  local copies, waits for them, and re-layouts: 41.5 us -> 14.1 us
  Pallas kernels: 0 us -> 19 us
  between operations: 17.2 us -> 2.58 us
  other arithmetic: 18.8 us -> 6.64 us
    all_gather x2 -> x0, blocking collectives: 337 us -> none  [the longest x1 172 us: gather_turned(): out, at, outs = (lax.all_gather(both, axis, axis=0, tiled=True), 0, [])]
    psum x5 -> x0, blocking collectives: 109 us -> none  [by_axis(): x = lax.psum(x, axis)]
    all_to_all x0 -> x3, blocking collectives: none -> 91.5 us  [summed(): return jnp.sum(lax.all_to_all(x, DP, 0, 0, tiled=True).astype(F32), axis=0)]
    all_to_all x6 -> x5, starting transfers between devices: 93.1 us -> 30.3 us  [the longest x4 24.9 us: to_everyone(): lax.all_to_all(jnp.broadcast_to(x[None], (BLOCKS, *x.shape)), DP, 0, 0, t...]
    ppermute x0 -> x6, waiting for transfers between devices: none -> 31.4 us  [swapped(): return lax.ppermute(x, axis, [(0, 1), (1, 0)])]
    dot_general x23 -> x0, matrix products: 30.4 us -> none  [the longest x1 2.91 us: per_device(): jnp.dot(normed_head, outlook_collected, preferred_element_type=jnp.float32)]
    ppermute x0 -> x6, starting transfers between devices: none -> 19.2 us  [swapped(): return lax.ppermute(x, axis, [(0, 1), (1, 0)])]
    pallas_call x0 -> x5, Pallas kernels: none -> 19 us  [call(): pl.pallas_call(body, out_shape=[jax.ShapeDtypeStruct(s, d) for s, d in ou...]
  transfers between devices with their start and end apart: 7 -> 11, of which waited for: 4 -> 11; matrix products, arithmetic and copies ran while one was open for 7% -> 3% of each run, Pallas kernels for 0% -> 1%
where the time goes in v1:
time: 292 us; the launch traced here: 290 us
  waiting for transfers between devices  107 us (37%)
  blocking collectives  91.5 us (31%)
  starting transfers between devices  49.5 us (17%)
  Pallas kernels  19 us (7%)
  local copies, waits for them, and re-layouts  14.1 us (5%)
  other arithmetic  6.64 us (2%)
    all_to_all x3, blocking collectives, summed(): return jnp.sum(lax.all_to_all(x, DP, 0, 0, tiled=True).astype(F32), axis=0)  91.5 us
    all_to_all x4, waiting for transfers between devices, to_everyone(): lax.all_to_all(jnp.broadcast_to(x[None], (BLOCKS, *x.shape)), DP, 0, 0, t...  48.1 us
    ppermute x6, waiting for transfers between devices, swapped(): return lax.ppermute(x, axis, [(0, 1), (1, 0)])  31.4 us
    all_to_all x1, waiting for transfers between devices, summed(): return jnp.sum(lax.all_to_all(x, DP, 0, 0, tiled=True).astype(F32), axis=0)  27.4 us
    all_to_all x4, starting transfers between devices, to_everyone(): lax.all_to_all(jnp.broadcast_to(x[None], (BLOCKS, *x.shape)), DP, 0, 0, t...  24.9 us
    ppermute x6, starting transfers between devices, swapped(): return lax.ppermute(x, axis, [(0, 1), (1, 0)])  19.2 us
    pallas_call x5, Pallas kernels, call(): pl.pallas_call(body, out_shape=[jax.ShapeDtypeStruct(s, d) for s, d in ou...  19 us
  transfers between devices with their start and end apart: 11, of which 11 were waited for; matrix products, arithmetic and copies ran while one was open for 3% of the time, Pallas kernels for 1%

profile of v1, /device:TPU:1, one launch (start us, length us, event | category | flops | bytes accessed | tf_op | source)
XLA Modules:
  0.0 290.3 jit_solution(7301050053627625524)
XLA Ops:
  0.7 1.4 copy.30.embed_ref
  2.1 1.3 dynamic-slice_bitcast_fusion.pos_ref
  3.4 1.7 basis_kernel.1
  5.1 28.1 %all_to_all.40 = f32[64,8,128]{2,1,0:T(8,128)S(1)} all-to-all(f32[64,8,128]{2,1,0:T(8,128)} %basis_kernel.1), channel_id=1, replica_groups=mesh['dp_0'=4,'dp_1'=4,'dp_2'=4,'mp_0'=2,'mp_1'=2] {'dp_0','dp_1','dp_2'}, dimensions={0} | all-to-all | bytes 524288 | tf_op jit(solution)/shard_map/all_to_all | solution.py:279
  34.0 5.7 %all-to-all-start.3 = ((f32[64,8,128]{2,1,0:T(8,128)}), f32[64,8,128]{2,1,0:T(8,128)S(1)}, u32[]{:S(2)}, u32[]{:S(2)}) async-start(f32[64,8,128]{2,1,0:T(8,128)} %broadcast_in_dim.10), calls=%async_computation.3 | async-start | bytes 524288 | tf_op jit(solution)/shard_map/all_to_all | solution.py:275
  41.4 10.7 %all-to-all-done.3.tiles_ref = f32[64,8,128]{2,1,0:T(8,128)S(1)} async-done(((f32[64,8,128]{2,1,0:T(8,128)}), f32[64,8,128]{2,1,0:T(8,128)S(1)}, u32[]{:S(2)}, u32[]{:S(2)}) %all-to-all-start.3) | async-done | bytes 262176 | tf_op jit(solution)/shard_map/all_to_all | solution.py:275
  52.1 1.2 broadcast_in_dim.8
  53.3 4.8 %all-to-all-start = ((bf16[64,24,384]{2,1,0:T(8,128)(2,1)}), bf16[64,24,384]{2,1,0:T(8,128)(2,1)S(1)}, u32[]{:S(2)}, u32[]{:S(2)}) async-start(bf16[64,24,384]{2,1,0:T(8,128)(2,1)} %broadcast_in_dim.8), calls=%async_computation | async-start | bytes 2359296 | tf_op jit(solution)/shard_map/all_to_all | solution.py:275
  58.4 25.1 %all-to-all-done = bf16[64,24,384]{2,1,0:T(8,128)(2,1)S(1)} async-done(((bf16[64,24,384]{2,1,0:T(8,128)(2,1)}), bf16[64,24,384]{2,1,0:T(8,128)(2,1)S(1)}, u32[]{:S(2)}, u32[]{:S(2)}) %all-to-all-start) | async-done | bytes 1179680 | tf_op jit(solution)/shard_map/all_to_all | solution.py:275
  83.5 1.2 broadcast_in_dim.9
  84.9 6.6 %all-to-all-start.1 = ((bf16[64,24,384]{2,1,0:T(8,128)(2,1)}), bf16[64,24,384]{2,1,0:T(8,128)(2,1)S(1)}, u32[]{:S(2)}, u32[]{:S(2)}) async-start(bf16[64,24,384]{2,1,0:T(8,128)(2,1)} %broadcast_in_dim.9), calls=%async_computation.1 | async-start | bytes 2359296 | tf_op jit(solution)/shard_map/all_to_all | solution.py:275
  92.8 3.8 %attention_kernel.1 = (bf16[1536,128]{1,0:T(8,128)(2,1)}, bf16[320,128]{1,0:T(8,128)(2,1)}, bf16[320,128]{1,0:T(8,128)(2,1)}, bf16[320,128]{1,0:T(8,128)(2,1)}, ...) custom-call(bf16[1536,384]{1,0:T(8,128)(2,1)} %bitcast.35, f32[64,8,128]{2,1,0:T(8,128)} %copy-done.2, ...), custom_call_target="tpu_custom_call" | custom-call | tf_op jit(solution)/shard_map/attention_kernel/pallas_call | solution.py:62
  96.6 7.9 %collective-permute-start = (bf16[1536,128]{1,0:T(8,128)(2,1)}, bf16[1536,128]{1,0:T(8,128)(2,1)S(1)}, u32[]{:S(2)}, u32[]{:S(2)}) collective-permute-start(bf16[1536,128]{1,0:T(8,128)(2,1)} %get-tuple-element.26), channel_id=1, source_target_pairs={{0,1},{1,0},{2,3},{3,2},{4,5},{5,4},{6,7},{7,6},{8,9},{9,8},{10,11... | collective-permute-start | bytes 1179656 | tf_op jit(solution)/shard_map/ppermute | solution.py:266
  104.4 1.6 collective-permute-done
  107.1 1.7 collective-permute-start.1
  109.5 1.5 all-to-all-done.1
  111.0 17.9 %collective-permute-done.1.far_ref = bf16[1536,128]{1,0:T(8,128)(2,1)S(1)} collective-permute-done((bf16[1536,128]{1,0:T(8,128)(2,1)S(1)}, bf16[1536,128]{1,0:T(8,128)(2,1)S(1)}, u32[]{:S(2)}, u32[]{:S(2)}) %collective-permute-start.1) | collective-permute-done | bytes 393248 | tf_op jit(solution)/shard_map/ppermute | solution.py:266
  129.7 5.4 %head_kernel.1 = (bf16[1536,128]{1,0:T(8,128)(2,1)}, bf16[1536,384]{1,0:T(8,128)(2,1)}, f32[1536,128]{1,0:T(8,128)}, f32[8,128]{1,0:T(8,128)}, f32[8,128]{1,0:T(8,128)}) custom-call(bf16[1536,384]{1,0:T(8,128)(2,1)} %bitcast.36, bf16[1536,384]{1,0:T(8,128)(2,1)} %bitcast.38, bf16[64,128]{1,0:T(8,128)(2,1)} %pad_maximum_fusion.1.basis_ref, ...), custom_call_target="tpu_custom_call" | custom-call | tf_op jit(solution)/shard_map/head_kernel/pallas_call | solution.py:62
  135.0 2.3 collective-permute-start.2
  137.4 1.6 collective-permute-done.2
  140.0 2.7 collective-permute-start.3
  142.7 9.1 %collective-permute-done.3.far_ref = bf16[1536,128]{1,0:T(8,128)(2,1)S(1)} collective-permute-done((bf16[1536,128]{1,0:T(8,128)(2,1)S(1)}, bf16[1536,128]{1,0:T(8,128)(2,1)S(1)}, u32[]{:S(2)}, u32[]{:S(2)}) %collective-permute-start.3) | collective-permute-done | bytes 393248 | tf_op jit(solution)/shard_map/ppermute | solution.py:266
  152.6 5.9 %backward_kernel.1 = (bf16[1536,384]{1,0:T(8,128)(2,1)}, f32[64,8,128]{2,1,0:T(8,128)}) custom-call(bf16[1536,384]{1,0:T(8,128)(2,1)} %bitcast.37, bf16[1536,384]{1,0:T(8,128)(2,1)} %bitcast.39, f32[64,8,128]{2,1,0:T(8,128)} %copy-done.2, bf16[64,128]{1,0:T(8,128)(2,1)} %pad_maximum_fusion.1.basis_ref, bf16[1536,128]{1,0:T(8,128)(2,1)} %copy-done.4, ...), custom_call_target="tpu_custom_call" | custom-call | tf_op jit(solution)/shard_map/backward_kernel/pallas_call | solution.py:62
  158.6 24.9 %all_to_all.41 = f32[64,8,128]{2,1,0:T(8,128)S(1)} all-to-all(f32[64,8,128]{2,1,0:T(8,128)} %get-tuple-element.37), channel_id=1, replica_groups=mesh['dp_0'=4,'dp_1'=4,'dp_2'=4,'mp_0'=2,'mp_1'=2] {'dp_0','dp_1','dp_2'}, dimensions={0} | all-to-all | bytes 524288 | tf_op jit(solution)/shard_map/all_to_all | solution.py:279
  183.4 38.5 %all_to_all.42 = bf16[64,24,384]{2,1,0:T(8,128)(2,1)S(1)} all-to-all(bf16[64,24,384]{2,1,0:T(8,128)(2,1)S(1)} %bitcast.40), channel_id=1, replica_groups=mesh['dp_0'=4,'dp_1'=4,'dp_2'=4,'mp_0'=2,'mp_1'=2] {'dp_0','dp_1','dp_2'}, dimensions={0} | all-to-all | bytes 2359296 | tf_op jit(solution)/shard_map/all_to_all | solution.py:279
  221.9 5.4 %all-to-all-start.6 = ((bf16[64,24,384]{2,1,0:T(8,128)(2,1)}), bf16[64,24,384]{2,1,0:T(8,128)(2,1)S(1)}, u32[]{:S(2)}, u32[]{:S(2)}) async-start(bf16[64,24,384]{2,1,0:T(8,128)(2,1)} %bitcast.12), calls=%async_computation.6 | async-start | bytes 2359296 | tf_op jit(solution)/shard_map/all_to_all | solution.py:279
  227.4 27.4 %all-to-all-done.6 = bf16[64,24,384]{2,1,0:T(8,128)(2,1)S(1)} async-done(((bf16[64,24,384]{2,1,0:T(8,128)(2,1)}), bf16[64,24,384]{2,1,0:T(8,128)(2,1)S(1)}, u32[]{:S(2)}, u32[]{:S(2)}) %all-to-all-start.6) | async-done | bytes 1179680 | tf_op jit(solution)/shard_map/all_to_all | solution.py:279
  255.5 7.8 %all-to-all-start.5 = ((f32[64,8,128]{2,1,0:T(8,128)}), f32[64,8,128]{2,1,0:T(8,128)S(1)}, u32[]{:S(2)}, u32[]{:S(2)}) async-start(f32[64,8,128]{2,1,0:T(8,128)} %broadcast_in_dim.11), calls=%async_computation.5 | async-start | bytes 524288 | tf_op jit(solution)/shard_map/all_to_all | solution.py:275
  265.0 10.8 %all-to-all-done.5.tiles_ref = f32[64,8,128]{2,1,0:T(8,128)S(1)} async-done(((f32[64,8,128]{2,1,0:T(8,128)}), f32[64,8,128]{2,1,0:T(8,128)S(1)}, u32[]{:S(2)}, u32[]{:S(2)}) %all-to-all-start.5) | async-done | bytes 262176 | tf_op jit(solution)/shard_map/all_to_all | solution.py:275
  276.5 2.2 last_kernel.1
  278.8 3.5 %collective-permute-start.4 = (f32[24,128]{1,0:T(8,128)}, f32[24,128]{1,0:T(8,128)S(1)}, u32[]{:S(2)}, u32[]{:S(2)}) collective-permute-start(f32[24,128]{1,0:T(8,128)} %get-tuple-element.40), channel_id=1, source_target_pairs={{0,1},{1,0},{2,3},{3,2},{4,5},{5,4},{6,7},{7,6},{8,9},{9,8},{10,11... | collective-permute-start | bytes 36872 | tf_op jit(solution)/shard_map/ppermute | solution.py:266
  285.0 1.4 slice_bitcast_fusion
  (69 shorter events, 16.5 us)
Async XLA Ops:
  0.6 40.7 %copy-start.10 = (bf16[32,20]{0,1:T(8,128)(2,1)S(1)}, bf16[32,20]{0,1:T(8,128)(2,1)}, u32[]{:S(2)}) copy-start(bf16[32,20]{0,1:T(8,128)(2,1)} %param.13) | copy-start | bytes 3844
  0.6 40.7 %copy-start.11 = (bf16[320,20]{0,1:T(8,128)(2,1)S(1)}, bf16[320,20]{0,1:T(8,128)(2,1)}, u32[]{:S(2)}) copy-start(bf16[320,20]{0,1:T(8,128)(2,1)} %param.18) | copy-start | bytes 38404
  34.0 18.1 %all-to-all-start.3 = ((f32[64,8,128]{2,1,0:T(8,128)}), f32[64,8,128]{2,1,0:T(8,128)S(1)}, u32[]{:S(2)}, u32[]{:S(2)}) async-start(f32[64,8,128]{2,1,0:T(8,128)} %broadcast_in_dim.10), calls=%async_computation.3 | async-start | bytes 524288 | tf_op jit(solution)/shard_map/all_to_all | solution.py:275
  52.1 1.2 copy-start.2
  53.2 4.8 %copy-start.13 = (bf16[2,20]{1,0:T(2,128)(2,1)S(1)}, bf16[2,20]{1,0:T(2,128)(2,1)}, u32[]{:S(2)}) copy-start(bf16[2,20]{1,0:T(2,128)(2,1)} %gains_ref.3) | copy-start | bytes 244
  53.2 4.9 %copy-start.9 = (f32[8,512]{1,0:T(8,128)S(1)}, f32[8,512]{1,0:T(8,128)}, u32[]{:S(2)}) copy-start(f32[8,512]{1,0:T(8,128)} %param.11) | copy-start | bytes 49156
  53.2 5.1 %copy-start.12 = (bf16[20,320]{1,0:T(8,128)(2,1)S(1)}, bf16[20,320]{1,0:T(8,128)(2,1)}, u32[]{:S(2)}) copy-start(bf16[20,320]{1,0:T(8,128)(2,1)} %param.19) | copy-start | bytes 38404
  53.3 30.3 %all-to-all-start = ((bf16[64,24,384]{2,1,0:T(8,128)(2,1)}), bf16[64,24,384]{2,1,0:T(8,128)(2,1)S(1)}, u32[]{:S(2)}, u32[]{:S(2)}) async-start(bf16[64,24,384]{2,1,0:T(8,128)(2,1)} %broadcast_in_dim.8), calls=%async_computation | async-start | bytes 2359296 | tf_op jit(solution)/shard_map/all_to_all | solution.py:275
  83.5 1.4 copy-start
  84.7 7.1 %copy-start.15 = (f32[8,128]{1,0:T(8,128)S(1)}, f32[8,128]{1,0:T(8,128)}, u32[]{:S(2)}) copy-start(f32[8,128]{1,0:T(8,128)} %param.12) | copy-start | bytes 12292
  84.7 7.4 %copy-start.14 = (bf16[16,128]{1,0:T(8,128)(2,1)S(1)}, bf16[16,128]{1,0:T(8,128)(2,1)}, u32[]{:S(2)}) copy-start(bf16[16,128]{1,0:T(8,128)(2,1)} %constant.56.clone) | copy-start | bytes 12292
  84.9 26.1 %all-to-all-start.1 = ((bf16[64,24,384]{2,1,0:T(8,128)(2,1)}), bf16[64,24,384]{2,1,0:T(8,128)(2,1)S(1)}, u32[]{:S(2)}, u32[]{:S(2)}) async-start(bf16[64,24,384]{2,1,0:T(8,128)(2,1)} %broadcast_in_dim.9), calls=%async_computation.1 | async-start | bytes 2359296 | tf_op jit(solution)/shard_map/all_to_all | solution.py:275
  96.6 9.4 %collective-permute-start = (bf16[1536,128]{1,0:T(8,128)(2,1)}, bf16[1536,128]{1,0:T(8,128)(2,1)S(1)}, u32[]{:S(2)}, u32[]{:S(2)}) collective-permute-start(bf16[1536,128]{1,0:T(8,128)(2,1)} %get-tuple-element.26), channel_id=1, source_target_pairs={{0,1},{1,0},{2,3},{3,2},{4,5},{5,4},{6,7},{7,6},{8,9},{9,8},{10,11... | collective-permute-start | bytes 1179656 | tf_op jit(solution)/shard_map/ppermute | solution.py:266
  107.1 21.8 %copy-start.3 = (bf16[1536,128]{1,0:T(8,128)(2,1)}, bf16[1536,128]{1,0:T(8,128)(2,1)S(1)}, u32[]{:S(2)}) copy-start(bf16[1536,128]{1,0:T(8,128)(2,1)S(1)} %add_convert_fusion.1.near_ref) | copy-start | bytes 1179652
  107.1 21.8 %collective-permute-start.1 = (bf16[1536,128]{1,0:T(8,128)(2,1)S(1)}, bf16[1536,128]{1,0:T(8,128)(2,1)S(1)}, u32[]{:S(2)}, u32[]{:S(2)}) collective-permute-start(bf16[1536,128]{1,0:T(8,128)(2,1)S(1)} %add_convert_fusion.1.near_ref), channel_id=1, source_target_pairs={{0,2},{2,0},{1,3},{3,1},{4,6},{6,4},{5,7},{7,5},{8,10},{10,8},{9,1... | collective-permute-start | bytes 1179656 | tf_op jit(solution)/shard_map/ppermute | solution.py:266
  111.0 17.9 %copy-start.1 = (bf16[64,24,384]{2,1,0:T(8,128)(2,1)}, bf16[64,24,384]{2,1,0:T(8,128)(2,1)S(1)}, u32[]{:S(2)}) copy-start(bf16[64,24,384]{2,1,0:T(8,128)(2,1)S(1)} %all-to-all-done.1) | copy-start | bytes 3538948
  128.9 0.7 copy-start.7
  135.0 3.9 %collective-permute-start.2 = (bf16[1536,128]{1,0:T(8,128)(2,1)}, bf16[1536,128]{1,0:T(8,128)(2,1)S(1)}, u32[]{:S(2)}, u32[]{:S(2)}) collective-permute-start(bf16[1536,128]{1,0:T(8,128)(2,1)} %get-tuple-element.27), channel_id=1, source_target_pairs={{0,1},{1,0},{2,3},{3,2},{4,5},{5,4},{6,7},{7,6},{8,9},{9,8},{10,11... | collective-permute-start | bytes 1179656 | tf_op jit(solution)/shard_map/ppermute | solution.py:266
  140.0 11.8 %copy-start.4 = (bf16[1536,128]{1,0:T(8,128)(2,1)}, bf16[1536,128]{1,0:T(8,128)(2,1)S(1)}, u32[]{:S(2)}) copy-start(bf16[1536,128]{1,0:T(8,128)(2,1)S(1)} %add_convert_fusion.near_ref) | copy-start | bytes 1179652
  140.0 11.8 %collective-permute-start.3 = (bf16[1536,128]{1,0:T(8,128)(2,1)S(1)}, bf16[1536,128]{1,0:T(8,128)(2,1)S(1)}, u32[]{:S(2)}, u32[]{:S(2)}) collective-permute-start(bf16[1536,128]{1,0:T(8,128)(2,1)S(1)} %add_convert_fusion.near_ref), channel_id=1, source_target_pairs={{0,2},{2,0},{1,3},{3,1},{4,6},{6,4},{5,7},{7,5},{8,10},{10,8},{9,1... | collective-permute-start | bytes 1179656 | tf_op jit(solution)/shard_map/ppermute | solution.py:266
  151.9 0.8 copy-start.8
  152.6 30.8 %copy-start.5 = (bf16[1536,384]{1,0:T(8,128)(2,1)S(1)}, bf16[1536,384]{1,0:T(8,128)(2,1)}, u32[]{:S(2)}) copy-start(bf16[1536,384]{1,0:T(8,128)(2,1)} %get-tuple-element.39) | copy-start | bytes 3538948
  221.9 32.9 %all-to-all-start.6 = ((bf16[64,24,384]{2,1,0:T(8,128)(2,1)}), bf16[64,24,384]{2,1,0:T(8,128)(2,1)S(1)}, u32[]{:S(2)}, u32[]{:S(2)}) async-start(bf16[64,24,384]{2,1,0:T(8,128)(2,1)} %bitcast.12), calls=%async_computation.6 | async-start | bytes 2359296 | tf_op jit(solution)/shard_map/all_to_all | solution.py:279
  255.5 20.3 %all-to-all-start.5 = ((f32[64,8,128]{2,1,0:T(8,128)}), f32[64,8,128]{2,1,0:T(8,128)S(1)}, u32[]{:S(2)}, u32[]{:S(2)}) async-start(f32[64,8,128]{2,1,0:T(8,128)} %broadcast_in_dim.11), calls=%async_computation.5 | async-start | bytes 524288 | tf_op jit(solution)/shard_map/all_to_all | solution.py:275
  275.8 0.7 copy-start.6
  278.8 4.6 %collective-permute-start.4 = (f32[24,128]{1,0:T(8,128)}, f32[24,128]{1,0:T(8,128)S(1)}, u32[]{:S(2)}, u32[]{:S(2)}) collective-permute-start(f32[24,128]{1,0:T(8,128)} %get-tuple-element.40), channel_id=1, source_target_pairs={{0,1},{1,0},{2,3},{3,2},{4,5},{5,4},{6,7},{7,6},{8,9},{9,8},{10,11... | collective-permute-start | bytes 36872 | tf_op jit(solution)/shard_map/ppermute | solution.py:266
  284.0 2.5 collective-permute-start.5

commit v2 on v1

--- a/solution.py
+++ b/solution.py
@@ -24,6 +24,13 @@
 BASIS = PATCH + PATCHES
 TILES = (BASIS // 8) * (3 * WIDE // 128)
 DP = ("dp_0", "dp_1", "dp_2")
+XY = ("dp_0", "dp_2")
+Z = "dp_1"
+GROUPS = 16
+DEPTH = 4
+GROUP_ROWS = DEPTH * PADDED
+SMALL = 8 * BLOCKS // GROUPS
+HALF = ROWS // 2
 MP = ("mp_0", "mp_1")
 EPS = 1e-06
 STAT_EPS = 1e-05
@@ -86,13 +93,42 @@
     )
 
 
+def both_from(ref):
+    def tile(t, lanes):
+        return ref[t // DEPTH, GROUP_ROWS : GROUP_ROWS + SMALL, lanes].astype(F32)[8 * (t % DEPTH) : 8 * (t % DEPTH) + 8]
+
+    return [
+        jnp.concatenate(
+            [jnp.concatenate([tile(9 * i + j, lanes) for j in range(9)], axis=1) for i in range(BASIS // 8)], axis=0
+        ).astype(BF)
+        for lanes in (slice(0, 128), slice(128, 256))
+    ]
+
+
+def blocks(ref, lanes=slice(0, WIDE)):
+    rows = ref[:, 0:GROUP_ROWS, lanes]
+    return rows.reshape(ROWS, rows.shape[2])
+
+
+def spread_halves(value, mine_ref, other_ref):
+    north = lax.axis_index("mp_1") == 1
+    mine_ref[...] = jnp.where(north, value[HALF:], value[:HALF]).astype(BF)
+    other_ref[...] = jnp.where(north, value[:HALF], value[HALF:]).astype(BF)
+
+
+def joined_halves(mine_ref, other_ref):
+    north = lax.axis_index("mp_1") == 1
+    mine, other = mine_ref[...].astype(F32), other_ref[...].astype(F32)
+    return jnp.concatenate([jnp.where(north, other, mine), jnp.where(north, mine, other)], axis=0)
+
+
 def raw_projections(tiles_ref, basis):
-    high, low = two(from_tiles(tiles_ref))
+    high, low = both_from(tiles_ref)
     return tn(jnp.concatenate([high, low], axis=0), jnp.concatenate([basis, basis], axis=0))
 
 
 def first_residual(exit_ref, basis_ref):
-    lanes = exit_ref[:, 256:384]
+    lanes = blocks(exit_ref, slice(256, 384))
     entries = basis_ref[...]
     return nn(lanes, jnp.concatenate([jnp.zeros_like(entries), entries], axis=0))
 
@@ -105,12 +141,12 @@
 
 
 def attention_kernel(
-    exit_ref, tiles_ref, basis_ref, part_ref, context_ref, queries_ref, keys_ref, values_ref, probs_ref, factor_ref
+    exit_ref, basis_ref, mine_ref, other_ref, context_ref, queries_ref, keys_ref, values_ref, probs_ref, factor_ref
 ):
     residual = first_residual(exit_ref, basis_ref)
     factor = lax.rsqrt(jnp.sum(residual * residual, axis=0, keepdims=True) / WIDTH + EPS)
     factor_ref[...] = jnp.broadcast_to(factor, factor_ref.shape)
-    raw = raw_projections(tiles_ref, basis_ref[0:BASIS, :]) * factor
+    raw = raw_projections(exit_ref, basis_ref[0:BASIS, :]) * factor
     queries_ref[...] = raw[0:COLS].astype(BF)
     keys_ref[...] = raw[WIDE : WIDE + COLS].astype(BF)
     values_ref[...] = raw[2 * WIDE : 2 * WIDE + COLS].astype(BF)
@@ -122,19 +158,32 @@
         probs = raised / jnp.sum(raised, axis=0, keepdims=True)
         probs_ref[h] = probs
         context_ref[at, :] = nn(values_ref[at, :], probs.astype(BF)).astype(BF)
-    part_ref[...] = nn(exit_ref[:, 0:COLS], context_ref[...]).astype(BF)
+    context = jnp.concatenate([context_ref[...], jnp.zeros((WIDE - COLS, TOKENS), BF)], axis=0)
+    spread_halves(nn(blocks(exit_ref), context), mine_ref, other_ref)
 
 
 def head_kernel(
-    exit_ref, head_ref, basis_ref, near_ref, far_ref, target_ref, back_ref, grad_ref, residual_ref, factor_ref, loss_ref
+    exit_ref,
+    head_ref,
+    basis_ref,
+    half_ref,
+    rest_ref,
+    target_ref,
+    mine_ref,
+    other_ref,
+    grad_ref,
+    residual_ref,
+    factor_ref,
+    loss_ref,
 ):
-    residual = first_residual(exit_ref, basis_ref) + (near_ref[...].astype(F32) + far_ref[...].astype(F32))
+    head = blocks(head_ref)
+    residual = first_residual(exit_ref, basis_ref) + joined_halves(half_ref, rest_ref)
     residual_ref[...] = residual
     factor = lax.rsqrt(jnp.sum(residual * residual, axis=0, keepdims=True) / WIDTH + EPS)
     factor_ref[...] = jnp.broadcast_to(factor, factor_ref.shape)
     scaled = residual * factor
-    normed = (scaled * head_ref[:, COLS + 1 : COLS + 2].astype(F32)).astype(BF)
-    forecast = tn(head_ref[...], normed)[0:COLS]
+    normed = (scaled * head[:, COLS + 1 : COLS + 2].astype(F32)).astype(BF)
+    forecast = tn(head, normed)[0:COLS]
     column = lax.broadcasted_iota(jnp.int32, (COLS, 1), 0).astype(F32)
     step = jnp.floor((column + 0.5) * 0.1)
     channel = column - CHANNELS * step
@@ -155,22 +204,21 @@
     loss_ref[...] = jnp.broadcast_to(jnp.sum(terms, axis=0, keepdims=True), loss_ref.shape)
     slope = (jnp.where(mean_channel, -2.0 * error, sigmoid - share) * (1.0 / 128.0)).astype(BF)
     slope = jnp.concatenate([slope, jnp.zeros((WIDE - COLS, TOKENS), BF)], axis=0)
-    back = nn(head_ref[...], slope)
-    back_ref[...] = back.astype(BF)
+    back = nn(head, slope)
+    spread_halves(back, mine_ref, other_ref)
     high, low = two(jnp.sum(back * scaled, axis=1, keepdims=True))
     lane = lax.broadcasted_iota(jnp.int32, (1, WIDE), 1)
     grad = nt(normed, slope)
     grad = jnp.where(lane == COLS, high.astype(F32), jnp.where(lane == COLS + 1, low.astype(F32), grad))
-    grad_ref[...] = grad.astype(BF)
+    grad_ref[...] = grad.astype(BF).reshape(GROUPS, GROUP_ROWS, WIDE)
 
 
 def backward_kernel(
     exit_ref,
     head_ref,
-    tiles_ref,
     basis_ref,
-    near_ref,
-    far_ref,
+    half_ref,
+    rest_ref,
     residual_ref,
     factor_one_ref,
     factor_zero_ref,
@@ -180,22 +228,21 @@
     values_ref,
     probs_ref,
     loss_ref,
-    grad_ref,
     out_ref,
 ):
     basis = basis_ref[0:BASIS, :]
     patches = basis_ref[0:PATCH, :]
-    upstream = near_ref[...].astype(F32) + far_ref[...].astype(F32)
+    upstream = joined_halves(half_ref, rest_ref)
     residual = residual_ref[...]
     factor = factor_one_ref[0:1, :]
-    weighted = head_ref[:, COLS + 1 : COLS + 2].astype(F32) * upstream
+    weighted = blocks(head_ref, slice(256, 384))[:, COLS - 255 : COLS - 254].astype(F32) * upstream
     inner = jnp.sum(weighted * residual, axis=0, keepdims=True) / WIDTH
     low = (factor * weighted - residual * (factor * factor * factor * inner)).astype(BF)
     grad = nt(low, jnp.concatenate([context_ref[...], patches, patches], axis=0))
     lane = lax.broadcasted_iota(jnp.int32, (1, WIDE), 1)
     grad = jnp.where(lane >= COLS + PATCH, grad - grad.astype(BF).astype(F32), grad)
-    grad_ref[...] = grad.astype(BF)
-    context_grad = tn(exit_ref[...], low)[0:COLS].astype(BF)
+    out_ref[:, 0:GROUP_ROWS, :] = grad.astype(BF).reshape(GROUPS, GROUP_ROWS, WIDE)
+    context_grad = tn(blocks(exit_ref), low)[0:COLS].astype(BF)
     backs = ([], [], [])
     for h in range(COLS // HEAD_DIM):
         at = slice(h * HEAD_DIM, (h + 1) * HEAD_DIM)
@@ -214,16 +261,68 @@
     entries = basis.astype(F32)
     high, low = two(entries * factor)
     total = nt(high, back) + nt(low, back)
-    raw = raw_projections(tiles_ref, basis)
+    raw = raw_projections(exit_ref, basis)
     inner = jnp.sum(back.astype(F32) * raw, axis=0, keepdims=True) / WIDTH
     high, low = two(entries * (factor * factor * factor * inner))
     mixed = nt(high, patches) + nt(low, patches)
-    out_ref[...] = jnp.zeros_like(out_ref)
-    for i in range(BASIS // 8):
-        for j in range(9):
-            out_ref[9 * i + j] = total[8 * i : 8 * i + 8, 128 * j : 128 * j + 128]
-        out_ref[TILES + i, :, 0:PATCH] = mixed[8 * i : 8 * i + 8]
-    out_ref[TILES + BASIS // 8] = loss_ref[...]
+    blank = jnp.zeros((8, 128 - PATCH), F32)
+    tiles = [total[8 * i : 8 * i + 8, 128 * j : 128 * j + 128] for i in range(BASIS // 8) for j in range(9)]
+    tiles += [jnp.concatenate([mixed[8 * i : 8 * i + 8], blank], axis=1) for i in range(BASIS // 8)]
+    tiles += [loss_ref[...]]
+    tiles += [jnp.zeros((8, 128), F32)] * (BLOCKS - len(tiles))
+    for k in range(GROUPS):
+        high, low = two(jnp.concatenate(tiles[DEPTH * k : DEPTH * k + DEPTH], axis=0))
+        out_ref[k, GROUP_ROWS : GROUP_ROWS + SMALL, :] = jnp.concatenate([high, low, jnp.zeros_like(low)], axis=1)
+
+
+def pair(x):
+    high, low = two(x)
+    return jnp.concatenate([high, low, jnp.zeros_like(low)], axis=1)
+
+
+def lined(block):
+    return jnp.concatenate([block.astype(F32), jnp.zeros((SMALL - PADDED, WIDE), F32)], axis=0).astype(BF)
+
+
+def blocks_out_kernel(tiles_ref, exit_ref, head_ref, out_ref):
+    total = tiles_ref[0]
+    for k in range(1, GROUPS):
+        total += tiles_ref[k]
+    block = jnp.concatenate([lined(exit_ref[...]), lined(head_ref[...]), pair(total)], axis=0)
+    for z in range(DEPTH):
+        out_ref[z] = block
+
+
+def column_kernel(in_ref, exit_ref, head_ref):
+    parts = [in_ref[z].astype(F32) for z in range(DEPTH)]
+    total = sum(p[2 * SMALL :, 0:128] + p[2 * SMALL :, 128:256] for p in parts)
+    exits = jnp.concatenate([p[0:PADDED] for p in parts], axis=0).astype(BF)
+    heads = jnp.concatenate([p[SMALL : SMALL + PADDED] for p in parts], axis=0).astype(BF)
+    exits = jnp.concatenate([exits, pair(total)], axis=0)
+    for k in range(GROUPS):
+        exit_ref[k] = exits
+        head_ref[k] = heads
+
+
+def scatter_kernel(head_ref, exit_ref, out_ref):
+    heads = head_ref[0].astype(F32)
+    exits = exit_ref[0].astype(F32)
+    for k in range(1, GROUPS):
+        heads += head_ref[k].astype(F32)
+        exits += exit_ref[k].astype(F32)
+    small = pair(exits[GROUP_ROWS:, 0:128] + exits[GROUP_ROWS:, 128:256])
+    for z in range(DEPTH):
+        rows = slice(z * PADDED, (z + 1) * PADDED)
+        out_ref[z] = jnp.concatenate([lined(exits[rows]), lined(heads[rows]), small], axis=0)
+
+
+def finish_kernel(in_ref, exit_ref, head_ref, tiles_ref):
+    total = sum(in_ref[z].astype(F32) for z in range(DEPTH))
+    exit_ref[...] = total[0:PADDED]
+    head_ref[...] = total[SMALL : SMALL + PADDED]
+    small = total[2 * SMALL :, 0:128] + total[2 * SMALL :, 128:256]
+    for k in range(GROUPS):
+        tiles_ref[k] = small
 
 
 def exact(dims):
@@ -266,17 +365,14 @@
     return lax.ppermute(x, axis, [(0, 1), (1, 0)])
 
 
-def mp_parts(part):
-    near = (part.astype(F32) + swapped(part, "mp_1").astype(F32)).astype(BF)
-    return near, swapped(near, "mp_0")
-
-
-def to_everyone(x):
-    return lax.all_to_all(jnp.broadcast_to(x[None], (BLOCKS, *x.shape)), DP, 0, 0, tiled=True)
-
-
-def summed(x):
-    return jnp.sum(lax.all_to_all(x, DP, 0, 0, tiled=True).astype(F32), axis=0)
+def mp_sum(mine, other):
+    half = (mine.astype(F32) + swapped(other, "mp_1").astype(F32)).astype(BF)
+    half = (half.astype(F32) + swapped(half, "mp_0").astype(F32)).astype(BF)
+    return half, swapped(half, "mp_1")
+
+
+def over(x, axis):
+    return lax.all_to_all(x, axis, 0, 0, tiled=True)
 
 
 def padded_rows(x):
@@ -304,9 +400,14 @@
     head_block = padded_rows(jnp.concatenate([outlook, gains.T], axis=1))
 
     tiles = call(basis_kernel, [((BLOCKS, 8, 128), F32)], embed, gains, pos, asking, lookup, content)[0]
-    tiles = to_everyone(summed(tiles))
-    exit_all = to_everyone(exit_block).reshape(ROWS, WIDE)
-    head_all = to_everyone(head_block).reshape(ROWS, WIDE)
+    tiles = over(tiles.reshape(GROUPS, SMALL, 128), XY)
+    packed = ((DEPTH, 3 * SMALL, WIDE), BF)
+    with_small = ((GROUPS, GROUP_ROWS + SMALL, WIDE), BF)
+    without = ((GROUPS, GROUP_ROWS, WIDE), BF)
+    stacked = over(call(blocks_out_kernel, [packed], tiles, exit_block, head_block)[0], Z)
+    exit_all, head_all = call(column_kernel, [with_small, without], stacked)
+    exit_all = over(exit_all, XY)
+    head_all = over(head_all, XY)
 
     patches, target = prepare(history, later)
     number = np.arange(TOKENS) % PATCHES
@@ -314,10 +415,12 @@
     basis = jnp.concatenate([patches, place_hot, place_hot], axis=0)
 
     turned = (COLS, TOKENS)
-    part, context, queries, keys, values, probs, factor_zero = call(
+    half = ((HALF, TOKENS), BF)
+    mine, other, context, queries, keys, values, probs, factor_zero = call(
         attention_kernel,
         [
-            ((ROWS, TOKENS), BF),
+            half,
+            half,
             (turned, BF),
             (turned, BF),
             (turned, BF),
@@ -326,36 +429,29 @@
             ((8, TOKENS), F32),
         ],
         exit_all,
-        tiles,
         basis,
     )
-    near, far = mp_parts(part)
-    back, head_grad, residual, factor_one, loss = call(
+    mine, other = mp_sum(mine, other)
+    mine, other, head_grad, residual, factor_one, loss = call(
         head_kernel,
-        [
-            ((ROWS, TOKENS), BF),
-            ((ROWS, WIDE), BF),
-            ((ROWS, TOKENS), F32),
-            ((8, TOKENS), F32),
-            ((8, TOKENS), F32),
-        ],
+        [half, half, without, ((ROWS, TOKENS), F32), ((8, TOKENS), F32), ((8, TOKENS), F32)],
         exit_all,
         head_all,
         basis,
-        near,
-        far,
+        mine,
+        other,
         target,
     )
-    near, far = mp_parts(back)
-    exit_grad, totals = call(
+    head_grad = over(head_grad, XY)
+    mine, other = mp_sum(mine, other)
+    exit_grad = call(
         backward_kernel,
-        [((ROWS, WIDE), BF), ((BLOCKS, 8, 128), F32)],
+        [with_small],
         exit_all,
         head_all,
-        tiles,
         basis,
-        near,
-        far,
+        mine,
+        other,
         residual,
         factor_one,
         factor_zero,
@@ -365,10 +461,12 @@
         values,
         probs,
         loss,
-    )
-    totals = to_everyone(summed(totals))
-    head_sum = summed(head_grad.reshape(BLOCKS, PADDED, WIDE))
-    exit_sum = summed(exit_grad.reshape(BLOCKS, PADDED, WIDE))
+    )[0]
+    exit_grad = over(exit_grad, XY)
+    stacked = over(call(scatter_kernel, [packed], head_grad, exit_grad)[0], Z)
+    block = ((PADDED, WIDE), F32)
+    exit_sum, head_sum, totals = call(finish_kernel, [block, block, ((GROUPS, SMALL, 128), F32)], stacked)
+    totals = over(totals, XY).reshape(BLOCKS, 8, 128)
     own = (OWN, COLS)
     query_grad, key_grad, value_grad, rest = call(
         last_kernel,

time: 292 us -> 195 us (0.67)
  waiting for transfers between devices: 107 us -> 37.6 us
  blocking collectives: 91.5 us -> 70.7 us
  starting transfers between devices: 49.5 us -> 38.6 us
  Pallas kernels: 19 us -> 28.2 us
  local copies, waits for them, and re-layouts: 14.1 us -> 10.6 us
    all_to_all x5 -> x4, waiting for transfers between devices: 75.5 us -> 21.9 us  [over(): return lax.all_to_all(x, axis, 0, 0, tiled=True)]
    all_to_all x3 -> x4, blocking collectives: 91.5 us -> 70.7 us  [over(): return lax.all_to_all(x, axis, 0, 0, tiled=True)]
    ppermute x6 -> x8, waiting for transfers between devices: 31.4 us -> 15.6 us  [swapped(): return lax.ppermute(x, axis, [(0, 1), (1, 0)])]
    pallas_call x5 -> x9, Pallas kernels: 19 us -> 28.2 us  [call(): pl.pallas_call(body, out_shape=[jax.ShapeDtypeStruct(s, d) for s, d in ou...]
    ppermute x6 -> x8, starting transfers between devices: 19.2 us -> 13.3 us  [swapped(): return lax.ppermute(x, axis, [(0, 1), (1, 0)])]
    all_to_all x5 -> x4, starting transfers between devices: 30.3 us -> 25.2 us  [over(): return lax.all_to_all(x, axis, 0, 0, tiled=True)]
    broadcast_in_dim x4 -> x0, local copies, waits for them, and re-layouts: 3.8 us -> none  [to_everyone(): jnp.broadcast_to(x[None], (BLOCKS, *x.shape))]
  transfers between devices with their start and end apart: 11 -> 12, of which waited for: 11 -> 10; matrix products, arithmetic and copies ran while one was open for 3% -> 4% of each run, Pallas kernels for 1% -> 5%
where the time goes in v2:
time: 195 us; the launch traced here: 193 us
  blocking collectives  70.7 us (36%)
  starting transfers between devices  38.6 us (20%)
  waiting for transfers between devices  37.6 us (19%)
  Pallas kernels  28.2 us (14%)
  local copies, waits for them, and re-layouts  10.6 us (5%)
  other arithmetic  5.1 us (3%)
  between operations  2.58 us (1%)
    all_to_all x4, blocking collectives, over(): return lax.all_to_all(x, axis, 0, 0, tiled=True)  70.7 us
    pallas_call x9, Pallas kernels, call(): pl.pallas_call(body, out_shape=[jax.ShapeDtypeStruct(s, d) for s, d in ou...  28.2 us
    all_to_all x4, starting transfers between devices, over(): return lax.all_to_all(x, axis, 0, 0, tiled=True)  25.2 us
    all_to_all x4, waiting for transfers between devices, over(): return lax.all_to_all(x, axis, 0, 0, tiled=True)  21.9 us
    ppermute x8, waiting for transfers between devices, swapped(): return lax.ppermute(x, axis, [(0, 1), (1, 0)])  15.6 us
    ppermute x8, starting transfers between devices, swapped(): return lax.ppermute(x, axis, [(0, 1), (1, 0)])  13.3 us
    unnamed x29, local copies, waits for them, and re-layouts  4.93 us
  transfers between devices with their start and end apart: 12, of which 10 were waited for; matrix products, arithmetic and copies ran while one was open for 4% of the time, Pallas kernels for 5%

profile of v2, /device:TPU:1, one launch (start us, length us, event | category | flops | bytes accessed | tf_op | source)
XLA Modules:
  0.0 193.4 jit_solution(7556077666498835573)
XLA Ops:
  0.6 1.4 copy.27.embed_ref
  2.0 1.3 dynamic-slice_bitcast_fusion.pos_ref
  3.3 1.7 basis_kernel.1
  5.0 7.6 %all-to-all-start = ((f32[16,32,128]{2,1,0:T(8,128)}), f32[16,32,128]{2,1,0:T(8,128)S(1)}, u32[]{:S(2)}, u32[]{:S(2)}) async-start(f32[16,32,128]{2,1,0:T(8,128)} %bitcast.34), calls=%async_computation | async-start | bytes 524288 | tf_op jit(solution)/shard_map/all_to_all | solution.py:375
  15.0 1.5 fusion.9
  16.4 3.6 %all-to-all-done.tiles_ref = f32[16,32,128]{2,1,0:T(8,128)S(1)} async-done(((f32[16,32,128]{2,1,0:T(8,128)}), f32[16,32,128]{2,1,0:T(8,128)S(1)}, u32[]{:S(2)}, u32[]{:S(2)}) %all-to-all-start) | async-done | bytes 262176 | tf_op jit(solution)/shard_map/all_to_all | solution.py:375
  20.8 1.7 blocks_out_kernel.1
  22.5 17.1 %all_to_all.40.in_ref = bf16[4,96,384]{2,1,0:T(8,128)(2,1)} all-to-all(bf16[4,96,384]{2,1,0:T(8,128)(2,1)} %blocks_out_kernel.1), channel_id=1, replica_groups=mesh['dp_0'=4,'dp_1'=4,'dp_2'=4,'mp_0'=2,'mp_1'=2] {'dp_1'}, dimensions={0} | all-to-all | bytes 589824 | tf_op jit(solution)/shard_map/all_to_all | solution.py:375
  39.6 2.8 %column_kernel.1 = (bf16[16,128,384]{2,1,0:T(8,128)(2,1)}, bf16[16,96,384]{2,1,0:T(8,128)(2,1)}) custom-call(bf16[4,96,384]{2,1,0:T(8,128)(2,1)} %all_to_all.40.in_ref), custom_call_target="tpu_custom_call" | custom-call | tf_op jit(solution)/shard_map/column_kernel/pallas_call | solution.py:69
  42.4 3.8 %all-to-all-start.2 = ((bf16[16,128,384]{2,1,0:T(8,128)(2,1)}), bf16[16,128,384]{2,1,0:T(8,128)(2,1)S(1)}, u32[]{:S(2)}, u32[]{:S(2)}) async-start(bf16[16,128,384]{2,1,0:T(8,128)(2,1)} %get-tuple-element.31), calls=%async_computation.2 | async-start | bytes 3145728 | tf_op jit(solution)/shard_map/all_to_all | solution.py:375
  46.9 18.3 %all-to-all-done.2.exit_ref = bf16[16,128,384]{2,1,0:T(8,128)(2,1)S(1)} async-done(((bf16[16,128,384]{2,1,0:T(8,128)(2,1)}), bf16[16,128,384]{2,1,0:T(8,128)(2,1)S(1)}, u32[]{:S(2)}, u32[]{:S(2)}) %all-to-all-start.2) | async-done | bytes 1572896 | tf_op jit(solution)/shard_map/all_to_all | solution.py:375
  65.2 6.8 %all-to-all-start.3 = ((bf16[16,96,384]{2,1,0:T(8,128)(2,1)}), bf16[16,96,384]{2,1,0:T(8,128)(2,1)S(1)}, u32[]{:S(2)}, u32[]{:S(2)}) async-start(bf16[16,96,384]{2,1,0:T(8,128)(2,1)} %get-tuple-element.32), calls=%async_computation.3 | async-start | bytes 2359296 | tf_op jit(solution)/shard_map/all_to_all | solution.py:375
  72.6 3.9 %attention_kernel.1 = (bf16[768,128]{1,0:T(8,128)(2,1)}, bf16[768,128]{1,0:T(8,128)(2,1)}, bf16[320,128]{1,0:T(8,128)(2,1)}, bf16[320,128]{1,0:T(8,128)(2,1)}, b...) custom-call(bf16[16,128,384]{2,1,0:T(8,128)(2,1)} %copy-done, ...), custom_call_target="tpu_custom_call" | custom-call | tf_op jit(solution)/shard_map/attention_kernel/pallas_call | solution.py:69
  76.5 2.5 %collective-permute-start = (bf16[768,128]{1,0:T(8,128)(2,1)}, bf16[768,128]{1,0:T(8,128)(2,1)S(1)}, u32[]{:S(2)}, u32[]{:S(2)}) collective-permute-start(bf16[768,128]{1,0:T(8,128)(2,1)} %get-tuple-element.34), channel_id=1, source_target_pairs={{0,1},{1,0},{2,3},{3,2},{4,5},{5,4},{6,7},{7,6},{8,9},{9,8},{10,11... | collective-permute-start | bytes 589832 | tf_op jit(solution)/shard_map/ppermute | solution.py:365
  78.9 1.3 collective-permute-done
  82.1 5.3 %collective-permute-done.1 = bf16[768,128]{1,0:T(8,128)(2,1)S(1)} collective-permute-done((bf16[768,128]{1,0:T(8,128)(2,1)S(1)}, bf16[768,128]{1,0:T(8,128)(2,1)S(1)}, u32[]{:S(2)}, u32[]{:S(2)}) %collective-permute-start.1) | collective-permute-done | bytes 196640 | tf_op jit(solution)/shard_map/ppermute | solution.py:365
  87.5 1.3 collective-permute-start.2
  90.6 5.1 %head_kernel.1 = (bf16[768,128]{1,0:T(8,128)(2,1)}, bf16[768,128]{1,0:T(8,128)(2,1)}, bf16[16,96,384]{2,1,0:T(8,128)(2,1)}, f32[1536,128]{1,0:T(8,128)}, f32[8,128]{1,0:T(8,128)}, /*index=5*/f32[8,128]{1,0:T(8,128)}) custom-call(bf16[16,128,384]{2,1,0:T(8,128)(2,1)} %copy-done, bf16[16,96,384]{2,1,0:T(8,128)(2,1)} %copy-done.1, ...), custom_call_target="tpu_custom_call" | custom-call | tf_op jit(solution)/shard_map/head_kernel/pallas_call | solution.py:69
  95.7 7.0 %all-to-all-start.4 = ((bf16[16,96,384]{2,1,0:T(8,128)(2,1)}), bf16[16,96,384]{2,1,0:T(8,128)(2,1)S(1)}, u32[]{:S(2)}, u32[]{:S(2)}) async-start(bf16[16,96,384]{2,1,0:T(8,128)(2,1)} %get-tuple-element.35), calls=%async_computation.4 | async-start | bytes 2359296 | tf_op jit(solution)/shard_map/all_to_all | solution.py:375
  103.4 1.1 collective-permute-done.3
  105.5 5.3 %collective-permute-done.4 = bf16[768,128]{1,0:T(8,128)(2,1)S(1)} collective-permute-done((bf16[768,128]{1,0:T(8,128)(2,1)S(1)}, bf16[768,128]{1,0:T(8,128)(2,1)S(1)}, u32[]{:S(2)}, u32[]{:S(2)}) %collective-permute-start.4) | collective-permute-done | bytes 196640 | tf_op jit(solution)/shard_map/ppermute | solution.py:365
  110.8 1.3 collective-permute-start.5
  112.1 1.1 collective-permute-done.5.rest_ref
  113.9 6.2 %backward_kernel.1 = bf16[16,128,384]{2,1,0:T(8,128)(2,1)} custom-call(bf16[16,128,384]{2,1,0:T(8,128)(2,1)} %copy-done, bf16[16,96,384]{2,1,0:T(8,128)(2,1)} %copy-done.1, bf16[64,128]{1,0:T(8,128)(2,1)} %pad_maximum_fusion.1.basis_ref, bf16[768,128]{1,0:T(8,128)(2,1)} %copy-done.5, bf16[768,128]{1,0:T(8,128)(2,1)} %copy-done.8, ...), custom_call_target="tpu_custom_call" | custom-call | tf_op jit(solution)/shard_map/backward_kernel/pallas_call | solution.py:69
  120.1 28.7 %all_to_all.41.exit_ref = bf16[16,128,384]{2,1,0:T(8,128)(2,1)} all-to-all(bf16[16,128,384]{2,1,0:T(8,128)(2,1)} %backward_kernel.1), channel_id=1, replica_groups=mesh['dp_0'=4,'dp_1'=4,'dp_2'=4,'mp_0'=2,'mp_1'=2] {'dp_0','dp_2'}, dimensions={0} | all-to-all | bytes 3145728 | tf_op jit(solution)/shard_map/all_to_all | solution.py:375
  148.7 2.9 %scatter_kernel.1 = bf16[4,96,384]{2,1,0:T(8,128)(2,1)} custom-call(bf16[16,96,384]{2,1,0:T(8,128)(2,1)} %copy-done.2, bf16[16,128,384]{2,1,0:T(8,128)(2,1)} %all_to_all.41.exit_ref), custom_call_target="tpu_custom_call" | custom-call | tf_op jit(solution)/shard_map/scatter_kernel/pallas_call | solution.py:69
  151.6 13.5 %all_to_all.42.in_ref = bf16[4,96,384]{2,1,0:T(8,128)(2,1)} all-to-all(bf16[4,96,384]{2,1,0:T(8,128)(2,1)} %scatter_kernel.1), channel_id=1, replica_groups=mesh['dp_0'=4,'dp_1'=4,'dp_2'=4,'mp_0'=2,'mp_1'=2] {'dp_1'}, dimensions={0} | all-to-all | bytes 589824 | tf_op jit(solution)/shard_map/all_to_all | solution.py:375
  165.1 1.7 finish_kernel.1
  166.8 11.5 %all_to_all.43 = f32[16,32,128]{2,1,0:T(8,128)} all-to-all(f32[16,32,128]{2,1,0:T(8,128)} %get-tuple-element.47), channel_id=1, replica_groups=mesh['dp_0'=4,'dp_1'=4,'dp_2'=4,'mp_0'=2,'mp_1'=2] {'dp_0','dp_2'}, dimensions={0} | all-to-all | bytes 524288 | tf_op jit(solution)/shard_map/all_to_all | solution.py:375
  178.3 2.2 %last_kernel.1 = (f32[20,320]{1,0:T(8,128)}, f32[20,320]{1,0:T(8,128)}, f32[20,320]{1,0:T(8,128)}, f32[24,128]{1,0:T(8,128)}) custom-call(f32[64,8,128]{2,1,0:T(8,128)} %bitcast.33, bf16[32,20]{1,0:T(8,128)(2,1)} %copy.27.embed_ref, bf16[2,20]{1,0:T(2,128)(2,1)} %gains_ref.3, f32[16,20]{1,0:T(8,128)} %dynamic-slice_bitcast_fusion.pos_ref, ...), custom_call_target="tpu_custom_call" | custom-call | tf_op jit(solution)/shard_map/last_kernel/pallas_call | solution.py:69
  180.6 4.9 %collective-permute-start.6 = (f32[24,128]{1,0:T(8,128)}, f32[24,128]{1,0:T(8,128)S(1)}, u32[]{:S(2)}, u32[]{:S(2)}) collective-permute-start(f32[24,128]{1,0:T(8,128)} %get-tuple-element.50), channel_id=1, source_target_pairs={{0,1},{1,0},{2,3},{3,2},{4,5},{5,4},{6,7},{7,6},{8,9},{9,8},{10,11... | collective-permute-start | bytes 36872 | tf_op jit(solution)/shard_map/ppermute | solution.py:365
  188.1 1.4 slice_bitcast_fusion
  (63 shorter events, 15.3 us)
Async XLA Ops:
  5.0 15.0 %all-to-all-start = ((f32[16,32,128]{2,1,0:T(8,128)}), f32[16,32,128]{2,1,0:T(8,128)S(1)}, u32[]{:S(2)}, u32[]{:S(2)}) async-start(f32[16,32,128]{2,1,0:T(8,128)} %bitcast.34), calls=%async_computation | async-start | bytes 524288 | tf_op jit(solution)/shard_map/all_to_all | solution.py:375
  20.1 0.7 copy-start.3
  42.3 3.9 %copy-start.9 = (f32[8,512]{1,0:T(8,128)S(1)}, f32[8,512]{1,0:T(8,128)}, u32[]{:S(2)}) copy-start(f32[8,512]{1,0:T(8,128)} %param.11) | copy-start | bytes 49156
  42.4 4.2 %copy-start.11 = (f32[8,128]{1,0:T(8,128)S(1)}, f32[8,128]{1,0:T(8,128)}, u32[]{:S(2)}) copy-start(f32[8,128]{1,0:T(8,128)} %param.12) | copy-start | bytes 12292
  42.4 22.8 %all-to-all-start.2 = ((bf16[16,128,384]{2,1,0:T(8,128)(2,1)}), bf16[16,128,384]{2,1,0:T(8,128)(2,1)S(1)}, u32[]{:S(2)}, u32[]{:S(2)}) async-start(bf16[16,128,384]{2,1,0:T(8,128)(2,1)} %get-tuple-element.31), calls=%async_computation.2 | async-start | bytes 3145728 | tf_op jit(solution)/shard_map/all_to_all | solution.py:375
  46.2 25.8 %copy-start.10 = (bf16[16,128]{1,0:T(8,128)(2,1)S(1)}, bf16[16,128]{1,0:T(8,128)(2,1)}, u32[]{:S(2)}) copy-start(bf16[16,128]{1,0:T(8,128)(2,1)} %constant.56.clone) | copy-start | bytes 12292
  65.2 7.4 %copy-start = (bf16[16,128,384]{2,1,0:T(8,128)(2,1)}, bf16[16,128,384]{2,1,0:T(8,128)(2,1)S(1)}, u32[]{:S(2)}) copy-start(bf16[16,128,384]{2,1,0:T(8,128)(2,1)S(1)} %all-to-all-done.2.exit_ref) | copy-start | bytes 4718596
  65.2 24.3 %all-to-all-start.3 = ((bf16[16,96,384]{2,1,0:T(8,128)(2,1)}), bf16[16,96,384]{2,1,0:T(8,128)(2,1)S(1)}, u32[]{:S(2)}, u32[]{:S(2)}) async-start(bf16[16,96,384]{2,1,0:T(8,128)(2,1)} %get-tuple-element.32), calls=%async_computation.3 | async-start | bytes 2359296 | tf_op jit(solution)/shard_map/all_to_all | solution.py:375
  76.5 3.7 %collective-permute-start = (bf16[768,128]{1,0:T(8,128)(2,1)}, bf16[768,128]{1,0:T(8,128)(2,1)S(1)}, u32[]{:S(2)}, u32[]{:S(2)}) collective-permute-start(bf16[768,128]{1,0:T(8,128)(2,1)} %get-tuple-element.34), channel_id=1, source_target_pairs={{0,1},{1,0},{2,3},{3,2},{4,5},{5,4},{6,7},{7,6},{8,9},{9,8},{10,11... | collective-permute-start | bytes 589832 | tf_op jit(solution)/shard_map/ppermute | solution.py:365
  81.2 6.2 %collective-permute-start.1 = (bf16[768,128]{1,0:T(8,128)(2,1)S(1)}, bf16[768,128]{1,0:T(8,128)(2,1)S(1)}, u32[]{:S(2)}, u32[]{:S(2)}) collective-permute-start(bf16[768,128]{1,0:T(8,128)(2,1)S(1)} %add_convert_fusion.3), channel_id=1, source_target_pairs={{0,2},{2,0},{1,3},{3,1},{4,6},{6,4},{5,7},{7,5},{8,10},{10,8},{9,1... | collective-permute-start | bytes 589832 | tf_op jit(solution)/shard_map/ppermute | solution.py:365
  87.4 2.4 %copy-start.4 = (bf16[768,128]{1,0:T(8,128)(2,1)}, bf16[768,128]{1,0:T(8,128)(2,1)S(1)}, u32[]{:S(2)}) copy-start(bf16[768,128]{1,0:T(8,128)(2,1)S(1)} %add_convert_fusion.2.half_ref) | copy-start | bytes 589828
  87.5 2.4 %collective-permute-start.2 = (bf16[768,128]{1,0:T(8,128)(2,1)S(1)}, bf16[768,128]{1,0:T(8,128)(2,1)S(1)}, u32[]{:S(2)}, u32[]{:S(2)}) collective-permute-start(bf16[768,128]{1,0:T(8,128)(2,1)S(1)} %add_convert_fusion.2.half_ref), channel_id=1, source_target_pairs={{0,1},{1,0},{2,3},{3,2},{4,5},{5,4},{6,7},{7,6},{8,9},{9,8},{10,11... | collective-permute-start | bytes 589832 | tf_op jit(solution)/shard_map/ppermute | solution.py:365
  89.5 1.0 copy-start.1
  89.8 0.7 copy-start.6
  95.7 7.0 %copy-start.12 = (bf16[768,128]{1,0:T(8,128)(2,1)S(1)}, bf16[768,128]{1,0:T(8,128)(2,1)}, u32[]{:S(2)}) copy-start(bf16[768,128]{1,0:T(8,128)(2,1)} %get-tuple-element.37) | copy-start | bytes 589828
  95.7 8.8 %copy-start.7 = (bf16[768,128]{1,0:T(8,128)(2,1)S(1)}, bf16[768,128]{1,0:T(8,128)(2,1)}, u32[]{:S(2)}) copy-start(bf16[768,128]{1,0:T(8,128)(2,1)} %get-tuple-element.36) | copy-start | bytes 589828
  95.7 24.4 %all-to-all-start.4 = ((bf16[16,96,384]{2,1,0:T(8,128)(2,1)}), bf16[16,96,384]{2,1,0:T(8,128)(2,1)S(1)}, u32[]{:S(2)}, u32[]{:S(2)}) async-start(bf16[16,96,384]{2,1,0:T(8,128)(2,1)} %get-tuple-element.35), calls=%async_computation.4 | async-start | bytes 2359296 | tf_op jit(solution)/shard_map/all_to_all | solution.py:375
  102.7 1.8 collective-permute-start.3
  104.6 6.2 %collective-permute-start.4 = (bf16[768,128]{1,0:T(8,128)(2,1)S(1)}, bf16[768,128]{1,0:T(8,128)(2,1)S(1)}, u32[]{:S(2)}, u32[]{:S(2)}) collective-permute-start(bf16[768,128]{1,0:T(8,128)(2,1)S(1)} %add_convert_fusion.1), channel_id=1, source_target_pairs={{0,2},{2,0},{1,3},{3,1},{4,6},{6,4},{5,7},{7,5},{8,10},{10,8},{9,1... | collective-permute-start | bytes 589832 | tf_op jit(solution)/shard_map/ppermute | solution.py:365
  110.8 2.4 %copy-start.5 = (bf16[768,128]{1,0:T(8,128)(2,1)}, bf16[768,128]{1,0:T(8,128)(2,1)S(1)}, u32[]{:S(2)}) copy-start(bf16[768,128]{1,0:T(8,128)(2,1)S(1)} %add_convert_fusion.half_ref) | copy-start | bytes 589828
  110.8 2.4 %collective-permute-start.5 = (bf16[768,128]{1,0:T(8,128)(2,1)S(1)}, bf16[768,128]{1,0:T(8,128)(2,1)S(1)}, u32[]{:S(2)}, u32[]{:S(2)}) collective-permute-start(bf16[768,128]{1,0:T(8,128)(2,1)S(1)} %add_convert_fusion.half_ref), channel_id=1, source_target_pairs={{0,1},{1,0},{2,3},{3,2},{4,5},{5,4},{6,7},{7,6},{8,9},{9,8},{10,11... | collective-permute-start | bytes 589832 | tf_op jit(solution)/shard_map/ppermute | solution.py:365
  113.2 0.7 copy-start.8
  120.1 28.7 %copy-start.2 = (bf16[16,96,384]{2,1,0:T(8,128)(2,1)}, bf16[16,96,384]{2,1,0:T(8,128)(2,1)S(1)}, u32[]{:S(2)}) copy-start(bf16[16,96,384]{2,1,0:T(8,128)(2,1)S(1)} %all-to-all-done.4.head_ref) | copy-start | bytes 3538948
  180.6 5.9 %collective-permute-start.6 = (f32[24,128]{1,0:T(8,128)}, f32[24,128]{1,0:T(8,128)S(1)}, u32[]{:S(2)}, u32[]{:S(2)}) collective-permute-start(f32[24,128]{1,0:T(8,128)} %get-tuple-element.50), channel_id=1, source_target_pairs={{0,1},{1,0},{2,3},{3,2},{4,5},{5,4},{6,7},{7,6},{8,9},{9,8},{10,11... | collective-permute-start | bytes 36872 | tf_op jit(solution)/shard_map/ppermute | solution.py:365
  187.2 2.5 %collective-permute-start.7 = (f32[24,128]{1,0:T(8,128)S(1)}, f32[24,128]{1,0:T(8,128)S(1)}, u32[]{:S(2)}, u32[]{:S(2)}) collective-permute-start(f32[24,128]{1,0:T(8,128)S(1)} %add.62), channel_id=1, source_target_pairs={{0,2},{2,0},{1,3},{3,1},{4,6},{6,4},{5,7},{7,5},{8,10},{10,8},{9,1... | collective-permute-start | bytes 36872 | tf_op jit(solution)/shard_map/ppermute | solution.py:365

commit v3 on v2

--- a/solution.py
+++ b/solution.py
@@ -16,8 +16,6 @@
 CHANNELS = 10
 BLOCKS = 64
 OWN = WIDTH // BLOCKS
-PADDED = 24
-ROWS = BLOCKS * PADDED
 TOKENS = 128
 COLS = 320
 WIDE = 384
@@ -28,14 +26,18 @@
 Z = "dp_1"
 GROUPS = 16
 DEPTH = 4
-GROUP_ROWS = DEPTH * PADDED
+GROUP_ROWS = DEPTH * OWN
 SMALL = 8 * BLOCKS // GROUPS
-HALF = ROWS // 2
+LINED = 32
+FIRST = [(0, 1), (1, 0), (2, 3), (3, 2)]
+SECOND = [(0, 3), (3, 0), (1, 2), (2, 1)]
+HALF = WIDTH // 2
 MP = ("mp_0", "mp_1")
 EPS = 1e-06
 STAT_EPS = 1e-05
 RADIUS = 0.05
 SCALE = 1.0 / math.sqrt(HEAD_DIM)
+GRANT = 24 * 1024 * 1024
 BF = jnp.bfloat16
 F32 = jnp.float32
 
@@ -65,49 +67,64 @@
     return np.ascontiguousarray(table.reshape(PATCHES, BLOCKS, OWN).transpose(1, 0, 2))
 
 
-def call(body, outs, *args):
+def turned_table():
+    table = position_table().transpose(0, 2, 1)
+    high = table.astype(jnp.bfloat16)
+    low = (table - high.astype(np.float32)).astype(jnp.bfloat16)
+    return np.concatenate([high, low], axis=2)
+
+
+def call(body, outs, *args, grant=GRANT):
     return pl.pallas_call(
         body,
         out_shape=[jax.ShapeDtypeStruct(s, d) for s, d in outs],
         name=body.__name__,
+        compiler_params=pltpu.CompilerParams(vmem_limit_bytes=grant),
     )(*args)
 
 
-def basis_kernel(embed_ref, gains_ref, pos_ref, wq_ref, wk_ref, wv_ref, out_ref):
-    basis = jnp.concatenate([embed_ref[...].astype(F32), pos_ref[...]], axis=0)
-    high, low = two(basis * gains_ref[0:1, :].astype(F32))
+def own_basis(embed_ref, table_ref):
+    eye = lax.broadcasted_iota(jnp.int32, (PATCH, PATCH), 0) == lax.broadcasted_iota(jnp.int32, (PATCH, PATCH), 1)
+    embed = nt(eye.astype(F32).astype(BF), embed_ref[...])
+    return jnp.concatenate([embed, table_ref[lax.axis_index(DP)]], axis=0)
+
+
+def basis_kernel(
+    embed_ref, gains_ref, table_ref, turned_ref, wq_ref, wk_ref, wv_ref, exit_ref, head_ref, out_ref, block_ref
+):
+    high, low = two(own_basis(embed_ref, table_ref) * gains_ref[0:1, :].astype(F32))
     out_ref[...] = jnp.zeros_like(out_ref)
     for w, ref in enumerate((wq_ref, wk_ref, wv_ref)):
         weight = ref[...]
         part = nn(high, weight) + nn(low, weight)
         for i in range(BASIS // 8):
             rows = part[8 * i : 8 * i + 8]
-            out_ref[9 * i + 3 * w] = rows[:, 0:128]
-            out_ref[9 * i + 3 * w + 1] = rows[:, 128:256]
-            out_ref[9 * i + 3 * w + 2, :, 0:64] = rows[:, 256:320]
+            for j in range(3):
+                at = 9 * i + 3 * w + j
+                lanes = rows[:, 128 * j : min(128 * j + 128, COLS)]
+                k, t = at // DEPTH, 8 * (at % DEPTH)
+                out_ref[k, t : t + 8, 0 : lanes.shape[1]] = lanes
+    pair_eye = lax.broadcasted_iota(jnp.int32, (2, 2), 0) == lax.broadcasted_iota(jnp.int32, (2, 2), 1)
+    block_ref[...] = jnp.zeros_like(block_ref)
+    block_ref[0:OWN, 0:COLS] = exit_ref[...]
+    block_ref[0:OWN, COLS : COLS + PATCH] = embed_ref[...]
+    block_ref[0:OWN, COLS + PATCH : WIDE] = turned_ref[lax.axis_index(DP)]
+    block_ref[LINED : LINED + OWN, 0:COLS] = head_ref[...]
+    block_ref[LINED : LINED + OWN, COLS : COLS + 2] = tn(gains_ref[...], pair_eye.astype(F32).astype(BF)).astype(BF)
 
 
 def from_tiles(ref):
+    def tile(at):
+        return ref[at // DEPTH, 8 * (at % DEPTH) : 8 * (at % DEPTH) + 8, :]
+
     return jnp.concatenate(
-        [jnp.concatenate([ref[9 * i + j] for j in range(9)], axis=1) for i in range(BASIS // 8)], axis=0
-    )
-
-
-def both_from(ref):
-    def tile(t, lanes):
-        return ref[t // DEPTH, GROUP_ROWS : GROUP_ROWS + SMALL, lanes].astype(F32)[8 * (t % DEPTH) : 8 * (t % DEPTH) + 8]
-
-    return [
-        jnp.concatenate(
-            [jnp.concatenate([tile(9 * i + j, lanes) for j in range(9)], axis=1) for i in range(BASIS // 8)], axis=0
-        ).astype(BF)
-        for lanes in (slice(0, 128), slice(128, 256))
-    ]
+        [jnp.concatenate([tile(9 * i + j) for j in range(9)], axis=1) for i in range(BASIS // 8)], axis=0
+    )
 
 
 def blocks(ref, lanes=slice(0, WIDE)):
-    rows = ref[:, 0:GROUP_ROWS, lanes]
-    return rows.reshape(ROWS, rows.shape[2])
+    rows = ref[:, :, lanes]
+    return rows.reshape(WIDTH, rows.shape[2])
 
 
 def spread_halves(value, mine_ref, other_ref):
@@ -123,7 +140,7 @@
 
 
 def raw_projections(tiles_ref, basis):
-    high, low = both_from(tiles_ref)
+    high, low = two(from_tiles(tiles_ref))
     return tn(jnp.concatenate([high, low], axis=0), jnp.concatenate([basis, basis], axis=0))
 
 
@@ -141,12 +158,12 @@
 
 
 def attention_kernel(
-    exit_ref, basis_ref, mine_ref, other_ref, context_ref, queries_ref, keys_ref, values_ref, probs_ref, factor_ref
+    exit_ref, tiles_ref, basis_ref, mine_ref, other_ref, context_ref, queries_ref, keys_ref, values_ref, probs_ref, factor_ref
 ):
     residual = first_residual(exit_ref, basis_ref)
     factor = lax.rsqrt(jnp.sum(residual * residual, axis=0, keepdims=True) / WIDTH + EPS)
     factor_ref[...] = jnp.broadcast_to(factor, factor_ref.shape)
-    raw = raw_projections(exit_ref, basis_ref[0:BASIS, :]) * factor
+    raw = raw_projections(tiles_ref, basis_ref[0:BASIS, :]) * factor
     queries_ref[...] = raw[0:COLS].astype(BF)
     keys_ref[...] = raw[WIDE : WIDE + COLS].astype(BF)
     values_ref[...] = raw[2 * WIDE : 2 * WIDE + COLS].astype(BF)
@@ -216,6 +233,7 @@
 def backward_kernel(
     exit_ref,
     head_ref,
+    tiles_ref,
     basis_ref,
     half_ref,
     rest_ref,
@@ -228,6 +246,7 @@
     values_ref,
     probs_ref,
     loss_ref,
+    grad_ref,
     out_ref,
 ):
     basis = basis_ref[0:BASIS, :]
@@ -241,7 +260,7 @@
     grad = nt(low, jnp.concatenate([context_ref[...], patches, patches], axis=0))
     lane = lax.broadcasted_iota(jnp.int32, (1, WIDE), 1)
     grad = jnp.where(lane >= COLS + PATCH, grad - grad.astype(BF).astype(F32), grad)
-    out_ref[:, 0:GROUP_ROWS, :] = grad.astype(BF).reshape(GROUPS, GROUP_ROWS, WIDE)
+    grad_ref[...] = grad.astype(BF).reshape(GROUPS, GROUP_ROWS, WIDE)
     context_grad = tn(blocks(exit_ref), low)[0:COLS].astype(BF)
     backs = ([], [], [])
     for h in range(COLS // HEAD_DIM):
@@ -261,7 +280,7 @@
     entries = basis.astype(F32)
     high, low = two(entries * factor)
     total = nt(high, back) + nt(low, back)
-    raw = raw_projections(exit_ref, basis)
+    raw = raw_projections(tiles_ref, basis)
     inner = jnp.sum(back.astype(F32) * raw, axis=0, keepdims=True) / WIDTH
     high, low = two(entries * (factor * factor * factor * inner))
     mixed = nt(high, patches) + nt(low, patches)
@@ -271,58 +290,31 @@
     tiles += [loss_ref[...]]
     tiles += [jnp.zeros((8, 128), F32)] * (BLOCKS - len(tiles))
     for k in range(GROUPS):
-        high, low = two(jnp.concatenate(tiles[DEPTH * k : DEPTH * k + DEPTH], axis=0))
-        out_ref[k, GROUP_ROWS : GROUP_ROWS + SMALL, :] = jnp.concatenate([high, low, jnp.zeros_like(low)], axis=1)
-
-
-def pair(x):
-    high, low = two(x)
-    return jnp.concatenate([high, low, jnp.zeros_like(low)], axis=1)
-
-
-def lined(block):
-    return jnp.concatenate([block.astype(F32), jnp.zeros((SMALL - PADDED, WIDE), F32)], axis=0).astype(BF)
-
-
-def blocks_out_kernel(tiles_ref, exit_ref, head_ref, out_ref):
-    total = tiles_ref[0]
+        out_ref[k] = jnp.concatenate(tiles[DEPTH * k : DEPTH * k + DEPTH], axis=0)
+
+
+def group_sum(ref):
+    total = ref[0].astype(F32)
     for k in range(1, GROUPS):
-        total += tiles_ref[k]
-    block = jnp.concatenate([lined(exit_ref[...]), lined(head_ref[...]), pair(total)], axis=0)
-    for z in range(DEPTH):
-        out_ref[z] = block
-
-
-def column_kernel(in_ref, exit_ref, head_ref):
-    parts = [in_ref[z].astype(F32) for z in range(DEPTH)]
-    total = sum(p[2 * SMALL :, 0:128] + p[2 * SMALL :, 128:256] for p in parts)
-    exits = jnp.concatenate([p[0:PADDED] for p in parts], axis=0).astype(BF)
-    heads = jnp.concatenate([p[SMALL : SMALL + PADDED] for p in parts], axis=0).astype(BF)
-    exits = jnp.concatenate([exits, pair(total)], axis=0)
+        total += ref[k].astype(F32)
+    return total
+
+
+def gather_kernel(tiles_ref, own_ref, next_ref, far_ref, total_ref, exit_ref, head_ref):
+    total_ref[...] = group_sum(tiles_ref)
+    own, near, far = (ref[...].astype(F32) for ref in (own_ref, next_ref, far_ref))
+    parts = [own, near, far[: 2 * LINED], far[2 * LINED :]]
+    exits = jnp.concatenate([p[0:OWN] for p in parts], axis=0).astype(BF)
+    heads = jnp.concatenate([p[LINED : LINED + OWN] for p in parts], axis=0).astype(BF)
     for k in range(GROUPS):
         exit_ref[k] = exits
         head_ref[k] = heads
 
 
-def scatter_kernel(head_ref, exit_ref, out_ref):
-    heads = head_ref[0].astype(F32)
-    exits = exit_ref[0].astype(F32)
-    for k in range(1, GROUPS):
-        heads += head_ref[k].astype(F32)
-        exits += exit_ref[k].astype(F32)
-    small = pair(exits[GROUP_ROWS:, 0:128] + exits[GROUP_ROWS:, 128:256])
-    for z in range(DEPTH):
-        rows = slice(z * PADDED, (z + 1) * PADDED)
-        out_ref[z] = jnp.concatenate([lined(exits[rows]), lined(heads[rows]), small], axis=0)
-
-
-def finish_kernel(in_ref, exit_ref, head_ref, tiles_ref):
-    total = sum(in_ref[z].astype(F32) for z in range(DEPTH))
-    exit_ref[...] = total[0:PADDED]
-    head_ref[...] = total[SMALL : SMALL + PADDED]
-    small = total[2 * SMALL :, 0:128] + total[2 * SMALL :, 128:256]
+def total_kernel(one_ref, other_ref, out_ref):
+    total = one_ref[...] + other_ref[...]
     for k in range(GROUPS):
-        tiles_ref[k] = small
+        out_ref[k] = total
 
 
 def exact(dims):
@@ -333,32 +325,57 @@
 
 
 def last_kernel(
-    tiles_ref, embed_ref, gains_ref, pos_ref, wq_ref, wk_ref, wv_ref, exit_ref, head_ref, q_ref, k_ref, v_ref, rest_ref
+    tiles_ref,
+    embed_ref,
+    gains_ref,
+    table_ref,
+    wq_ref,
+    wk_ref,
+    wv_ref,
+    exit_ref,
+    head_ref,
+    q_ref,
+    k_ref,
+    v_ref,
+    exit_grad_ref,
+    head_grad_ref,
+    rest_ref,
 ):
-    basis = jnp.concatenate([embed_ref[...].astype(F32), pos_ref[...]], axis=0)
-    scaled = basis * gains_ref[0:1, :].astype(F32)
+    basis = own_basis(embed_ref, table_ref)
     total = from_tiles(tiles_ref)
-    scaled_grad = exact(((0,), (0,)))(scaled, total)
+    scaled_grad = exact(((0,), (0,)))(basis * gains_ref[0:1, :].astype(F32), total)
     plain_grad = exact(((0,), (0,)))(basis, total)
     embed = jnp.zeros((OWN, PATCH), F32)
     gain_zero = jnp.zeros((OWN, 1), F32)
-    for w, (weight_ref, out_ref) in enumerate(((wq_ref, q_ref), (wk_ref, k_ref), (wv_ref, v_ref))):
+    for w, (weight_ref, grad_ref) in enumerate(((wq_ref, q_ref), (wk_ref, k_ref), (wv_ref, v_ref))):
         weight = weight_ref[...].astype(F32)
-        out_ref[...] = scaled_grad[:, w * WIDE : w * WIDE + COLS]
+        grad_ref[...] = scaled_grad[:, w * WIDE : w * WIDE + COLS]
         gain_zero += jnp.sum(weight * plain_grad[:, w * WIDE : w * WIDE + COLS], axis=1, keepdims=True)
         embed += exact(((1,), (1,)))(weight, total[0:PATCH, w * WIDE : w * WIDE + COLS])
     pick = (lax.broadcasted_iota(jnp.int32, (2, PATCH), 0) == 0).astype(F32)
     embed = embed * exact(((0,), (0,)))(gains_ref[...].astype(F32), pick)
-    mixed = jnp.concatenate([tiles_ref[TILES + i] for i in range(BASIS // 8)], axis=0)[:, 0:PATCH]
+
+    def small(at):
+        return tiles_ref[at // DEPTH, 8 * (at % DEPTH) : 8 * (at % DEPTH) + 8, :]
+
+    mixed = jnp.concatenate([small(TILES + i) for i in range(BASIS // 8)], axis=0)[:, 0:PATCH]
     embed = embed - exact(((0,), (0,)))(basis, mixed)
-    ends = exit_ref[0:OWN, COLS : COLS + PATCH] + exit_ref[0:OWN, COLS + PATCH : WIDE]
-    gain_one = head_ref[0:OWN, COLS : COLS + 1] + head_ref[0:OWN, COLS + 1 : COLS + 2]
-    loss = jnp.sum(tiles_ref[TILES + BASIS // 8][0:1, :], axis=1, keepdims=True)
+    ends = exit_ref[:, COLS : COLS + PATCH] + exit_ref[:, COLS + PATCH : WIDE]
+    gain_one = head_ref[:, COLS : COLS + 1] + head_ref[:, COLS + 1 : COLS + 2]
+    exit_grad_ref[...] = exit_ref[:, 0:COLS]
+    head_grad_ref[...] = head_ref[:, 0:COLS]
     rest_ref[...] = jnp.zeros_like(rest_ref)
     rest_ref[0:OWN, 0:PATCH] = embed + 0.25 * ends
     rest_ref[0:OWN, PATCH : PATCH + 1] = gain_zero
     rest_ref[0:OWN, PATCH + 1 : PATCH + 2] = gain_one
-    rest_ref[0:1, PATCH + 2 : PATCH + 3] = loss
+    rest_ref[0:1, PATCH + 2 : PATCH + 3] = jnp.sum(small(TILES + BASIS // 8)[0:1, :], axis=1, keepdims=True)
+
+
+def end_kernel(one_ref, other_ref, embed_ref, gains_ref, loss_ref):
+    rest = one_ref[...] + other_ref[...]
+    embed_ref[...] = rest[0:OWN, 0:PATCH]
+    gains_ref[...] = rest.T[PATCH : PATCH + 2, 0:OWN]
+    loss_ref[...] = rest[0:1, PATCH + 2 : PATCH + 3] / 1048576.0
 
 
 def swapped(x, axis):
@@ -375,8 +392,17 @@
     return lax.all_to_all(x, axis, 0, 0, tiled=True)
 
 
-def padded_rows(x):
-    return jnp.pad(x, ((0, PADDED - OWN), (0, WIDE - x.shape[1])))
+def along_z(x, pairs):
+    return lax.ppermute(x, Z, pairs)
+
+
+def to_owner(x):
+    kept = x[: 2 * OWN] + along_z(x[2 * OWN :].astype(BF), SECOND).astype(F32)
+    return kept[:OWN] + along_z(kept[OWN:].astype(BF), FIRST).astype(F32)
+
+
+def after(x, *others):
+    return lax.optimization_barrier((x, *others))[0]
 
 
 def prepare(history, later):
@@ -393,26 +419,41 @@
 
 
 def per_device(history, later, embed, gains, asking, lookup, content, attend_exit, outlook):
-    place = lax.axis_index(DP)
-    pos = lax.dynamic_index_in_dim(jnp.asarray(position_table()), place, 0, keepdims=False)
-    pos_high, pos_low = two(pos)
-    exit_block = padded_rows(jnp.concatenate([attend_exit.T, embed.T, pos_high.T, pos_low.T], axis=1))
-    head_block = padded_rows(jnp.concatenate([outlook, gains.T], axis=1))
-
-    tiles = call(basis_kernel, [((BLOCKS, 8, 128), F32)], embed, gains, pos, asking, lookup, content)[0]
-    tiles = over(tiles.reshape(GROUPS, SMALL, 128), XY)
-    packed = ((DEPTH, 3 * SMALL, WIDE), BF)
-    with_small = ((GROUPS, GROUP_ROWS + SMALL, WIDE), BF)
-    without = ((GROUPS, GROUP_ROWS, WIDE), BF)
-    stacked = over(call(blocks_out_kernel, [packed], tiles, exit_block, head_block)[0], Z)
-    exit_all, head_all = call(column_kernel, [with_small, without], stacked)
+    table = jnp.asarray(position_table())
+    embed_turned = embed.T
+    tiles_like = ((GROUPS, SMALL, 128), F32)
+    groups = ((GROUPS, GROUP_ROWS, WIDE), BF)
+    tiles, block = call(
+        basis_kernel,
+        [tiles_like, ((2 * LINED, WIDE), BF)],
+        embed_turned,
+        gains,
+        table,
+        jnp.asarray(turned_table()),
+        asking,
+        lookup,
+        content,
+        attend_exit.T,
+        outlook,
+        grant=None,
+    )
+    tiles = over(tiles, XY)
+    near = along_z(block, FIRST)
+    far = along_z(jnp.concatenate([block, near], axis=0), SECOND)
+    total, exit_all, head_all = call(
+        gather_kernel, [((SMALL, 128), F32), groups, groups], tiles, block, near, far
+    )
     exit_all = over(exit_all, XY)
-    head_all = over(head_all, XY)
+    total = total + along_z(total, FIRST)
+    tiles = call(total_kernel, [tiles_like], total, along_z(total, SECOND))[0]
 
     patches, target = prepare(history, later)
     number = np.arange(TOKENS) % PATCHES
     place_hot = jnp.asarray((np.arange(PATCHES)[:, None] == number[None, :]), dtype=BF)
     basis = jnp.concatenate([patches, place_hot, place_hot], axis=0)
+    tiles, exit_all, basis, target = lax.optimization_barrier((tiles, exit_all, basis, target))
+    tiles = over(tiles, XY)
+    head_all = over(after(head_all, tiles), XY)
 
     turned = (COLS, TOKENS)
     half = ((HALF, TOKENS), BF)
@@ -429,12 +470,13 @@
             ((8, TOKENS), F32),
         ],
         exit_all,
+        tiles,
         basis,
     )
     mine, other = mp_sum(mine, other)
     mine, other, head_grad, residual, factor_one, loss = call(
         head_kernel,
-        [half, half, without, ((ROWS, TOKENS), F32), ((8, TOKENS), F32), ((8, TOKENS), F32)],
+        [half, half, groups, ((WIDTH, TOKENS), F32), ((8, TOKENS), F32), ((8, TOKENS), F32)],
         exit_all,
         head_all,
         basis,
@@ -444,11 +486,12 @@
     )
     head_grad = over(head_grad, XY)
     mine, other = mp_sum(mine, other)
-    exit_grad = call(
+    exit_grad, totals = call(
         backward_kernel,
-        [with_small],
+        [groups, tiles_like],
         exit_all,
         head_all,
+        tiles,
         basis,
         mine,
         other,
@@ -461,20 +504,23 @@
         values,
         probs,
         loss,
-    )[0]
-    exit_grad = over(exit_grad, XY)
-    stacked = over(call(scatter_kernel, [packed], head_grad, exit_grad)[0], Z)
-    block = ((PADDED, WIDE), F32)
-    exit_sum, head_sum, totals = call(finish_kernel, [block, block, ((GROUPS, SMALL, 128), F32)], stacked)
-    totals = over(totals, XY).reshape(BLOCKS, 8, 128)
-    own = (OWN, COLS)
-    query_grad, key_grad, value_grad, rest = call(
+    )
+    totals = over(after(totals, head_grad), XY)
+    head_sum = to_owner(jnp.sum(head_grad.astype(F32), axis=0))
+    exit_grad = over(after(exit_grad, totals), XY)
+    total = jnp.sum(totals, axis=0)
+    total = total + along_z(total, FIRST)
+    totals = call(total_kernel, [tiles_like], total, along_z(total, SECOND))[0]
+    totals = over(after(totals, exit_grad), XY)
+    exit_sum = to_owner(jnp.sum(exit_grad.astype(F32), axis=0))
+    own = ((OWN, COLS), F32)
+    query_grad, key_grad, value_grad, output_grad, head_weight_grad, rest = call(
         last_kernel,
-        [(own, F32), (own, F32), (own, F32), ((PADDED, 128), F32)],
+        [own, own, own, own, own, ((24, 128), F32)],
         totals,
-        embed,
+        embed_turned,
         gains,
-        pos,
+        table,
         asking,
         lookup,
         content,
@@ -482,17 +528,21 @@
         head_sum,
     )
     rest = rest + swapped(rest, "mp_1")
-    rest = rest + swapped(rest, "mp_0")
-    loss_mean = rest[0, PATCH + 2] / 1048576.0
+    embed_grad, gains_grad, loss_mean = call(
+        end_kernel,
+        [((OWN, PATCH), F32), ((2, OWN), F32), ((1, 1), F32)],
+        rest,
+        swapped(rest, "mp_0"),
+    )
     return (
-        loss_mean,
-        rest[:OWN, :PATCH].T,
-        rest[:OWN, PATCH : PATCH + 2].T,
+        loss_mean[0, 0],
+        embed_grad.T,
+        gains_grad,
         query_grad,
         key_grad,
         value_grad,
-        exit_sum[:OWN, :COLS].T,
-        head_sum[:OWN, :COLS],
+        output_grad.T,
+        head_weight_grad,
     )
 
 

time: 195 us -> 170 us (0.87)
  blocking collectives: 70.7 us -> 24.7 us
  starting transfers between devices: 38.6 us -> 73 us
  Pallas kernels: 28.2 us -> 13.6 us
  waiting for transfers between devices: 37.6 us -> 49.1 us
  local copies, waits for them, and re-layouts: 10.6 us -> 4.99 us
  other arithmetic: 5.1 us -> 3.02 us
    all_to_all x4 -> x2, blocking collectives: 70.7 us -> 24.7 us  [over(): return lax.all_to_all(x, axis, 0, 0, tiled=True)]
    ppermute x0 -> x10, starting transfers between devices: none -> 26.9 us  [along_z(): return lax.ppermute(x, Z, pairs)]
    pallas_call x9, Pallas kernels: 28.2 us -> 13.6 us  [call(): pl.pallas_call(body, out_shape=[jax.ShapeDtypeStruct(s, d) for s, d in ou...]
    ppermute x0 -> x10, waiting for transfers between devices: none -> 8.12 us  [along_z(): return lax.ppermute(x, Z, pairs)]
    all_to_all x4 -> x6, starting transfers between devices: 25.2 us -> 30.9 us  [over(): return lax.all_to_all(x, axis, 0, 0, tiled=True)]
    all_to_all x4 -> x6, waiting for transfers between devices: 21.9 us -> 26.7 us  [over(): return lax.all_to_all(x, axis, 0, 0, tiled=True)]
    transpose x6 -> x0, local copies, waits for them, and re-layouts: 2.96 us -> none  [the longest x1 1.39 us: per_device(): exit_sum[:OWN, :COLS]]
    unnamed x29 -> x42, local copies, waits for them, and re-layouts: 4.93 us -> 4.73 us
  transfers between devices with their start and end apart: 12 -> 24, of which waited for: 10 -> 16; matrix products, arithmetic and copies ran while one was open for 4% -> 2% of each run, Pallas kernels for 5% -> 2%
where the time goes in v3:
time: 170 us; the launch traced here: 169 us
  starting transfers between devices  73 us (43%)
  waiting for transfers between devices  49.1 us (29%)
  blocking collectives  24.7 us (15%)
  Pallas kernels  13.6 us (8%)
  local copies, waits for them, and re-layouts  4.99 us (3%)
  other arithmetic  3.02 us (2%)
    all_to_all x6, starting transfers between devices, over(): return lax.all_to_all(x, axis, 0, 0, tiled=True)  30.9 us
    ppermute x10, starting transfers between devices, along_z(): return lax.ppermute(x, Z, pairs)  26.9 us
    all_to_all x6, waiting for transfers between devices, over(): return lax.all_to_all(x, axis, 0, 0, tiled=True)  26.7 us
    all_to_all x2, blocking collectives, over(): return lax.all_to_all(x, axis, 0, 0, tiled=True)  24.7 us
    ppermute x8, starting transfers between devices, swapped(): return lax.ppermute(x, axis, [(0, 1), (1, 0)])  15.2 us
    ppermute x8, waiting for transfers between devices, swapped(): return lax.ppermute(x, axis, [(0, 1), (1, 0)])  14.2 us
    pallas_call x9, Pallas kernels, call(): pl.pallas_call(body, out_shape=[jax.ShapeDtypeStruct(s, d) for s, d in ou...  13.6 us
    ppermute x10, waiting for transfers between devices, along_z(): return lax.ppermute(x, Z, pairs)  8.12 us
  transfers between devices with their start and end apart: 24, of which 16 were waited for; matrix products, arithmetic and copies ran while one was open for 2% of the time, Pallas kernels for 2%

profile of v3, /device:TPU:1, one launch (start us, length us, event | category | flops | bytes accessed | tf_op | source)
XLA Modules:
  0.0 169.4 jit_solution(92132875522904827)
XLA Ops:
  0.6 2.3 %basis_kernel.1 = (f32[16,32,128]{2,1,0:T(8,128)}, bf16[64,384]{1,0:T(8,128)(2,1)}) custom-call(bf16[20,32]{1,0:T(8,128)(2,1)} %bitcast.10, bf16[2,20]{1,0:T(2,128)(2,1)} %gains_ref.3, f32[64,16,20]{2,1,0:T(8,128)} %constant.29.clone.table_ref, bf16[64,20,32]{2,1,0:T(8,128)(2,1)} %constant.30.clone.turned_ref, bf16[20,320]{1,0:T(8,128)(2,1)} %wq_ref.3, ...), custom_call_target="tpu_custom_call" | custom-call | tf_op jit(solution)/shard_map/basis_kernel/pallas_call | solution.py:78
  3.0 7.6 %all-to-all-start = ((f32[16,32,128]{2,1,0:T(8,128)}), f32[16,32,128]{2,1,0:T(8,128)S(1)}, u32[]{:S(2)}, u32[]{:S(2)}) async-start(f32[16,32,128]{2,1,0:T(8,128)} %get-tuple-element.46), calls=%async_computation | async-start | bytes 524288 | tf_op jit(solution)/shard_map/all_to_all | solution.py:392
  10.5 3.1 %collective-permute-start = (bf16[64,384]{1,0:T(8,128)(2,1)}, bf16[64,384]{1,0:T(8,128)(2,1)S(1)}, u32[]{:S(2)}, u32[]{:S(2)}) collective-permute-start(bf16[64,384]{1,0:T(8,128)(2,1)} %get-tuple-element.47.own_ref), channel_id=1, source_target_pairs={{0,16},{16,0},{32,48},{48,32},{1,17},{17,1},{33,49},{49,33},{2,18}... | collective-permute-start | bytes 147464 | tf_op jit(solution)/shard_map/ppermute | solution.py:396
  13.7 1.6 collective-permute-done.next_ref
  16.1 5.6 %collective-permute-start.1 = (bf16[128,384]{1,0:T(8,128)(2,1)S(1)}, bf16[128,384]{1,0:T(8,128)(2,1)S(1)}, u32[]{:S(2)}, u32[]{:S(2)}) collective-permute-start(bf16[128,384]{1,0:T(8,128)(2,1)S(1)} %pad_maximum_fusion), channel_id=1, source_target_pairs={{0,48},{48,0},{16,32},{32,16},{1,49},{49,1},{17,33},{33,17},{2,50}... | collective-permute-start | bytes 294920 | tf_op jit(solution)/shard_map/ppermute | solution.py:396
  21.9 2.4 %collective-permute-done.1.far_ref = bf16[128,384]{1,0:T(8,128)(2,1)S(1)} collective-permute-done((bf16[128,384]{1,0:T(8,128)(2,1)S(1)}, bf16[128,384]{1,0:T(8,128)(2,1)S(1)}, u32[]{:S(2)}, u32[]{:S(2)}) %collective-permute-start.1) | collective-permute-done | bytes 98336 | tf_op jit(solution)/shard_map/ppermute | solution.py:396
  26.5 6.9 %all-to-all-start.1 = ((bf16[16,80,384]{2,1,0:T(8,128)(2,1)}), bf16[16,80,384]{2,1,0:T(8,128)(2,1)S(1)}, u32[]{:S(2)}, u32[]{:S(2)}) async-start(bf16[16,80,384]{2,1,0:T(8,128)(2,1)} %get-tuple-element.49), calls=%async_computation.1 | async-start | bytes 1966080 | tf_op jit(solution)/shard_map/all_to_all | solution.py:392
  33.7 1.7 %collective-permute-start.2 = (f32[32,128]{1,0:T(8,128)S(1)}, f32[32,128]{1,0:T(8,128)S(1)}, u32[]{:S(2)}, u32[]{:S(2)}) collective-permute-start(f32[32,128]{1,0:T(8,128)S(1)} %get-tuple-element.48), channel_id=1, source_target_pairs={{0,16},{16,0},{32,48},{48,32},{1,17},{17,1},{33,49},{49,33},{2,18}... | collective-permute-start | bytes 49160 | tf_op jit(solution)/shard_map/ppermute | solution.py:396
  35.5 1.8 %collective-permute-done.2 = f32[32,128]{1,0:T(8,128)S(1)} collective-permute-done((f32[32,128]{1,0:T(8,128)S(1)}, f32[32,128]{1,0:T(8,128)S(1)}, u32[]{:S(2)}, u32[]{:S(2)}) %collective-permute-start.2) | collective-permute-done | bytes 16416 | tf_op jit(solution)/shard_map/ppermute | solution.py:396
  37.3 4.0 %collective-permute-start.3 = (f32[32,128]{1,0:T(8,128)S(1)}, f32[32,128]{1,0:T(8,128)S(1)}, u32[]{:S(2)}, u32[]{:S(2)}) collective-permute-start(f32[32,128]{1,0:T(8,128)S(1)} %add.52.one_ref), channel_id=1, source_target_pairs={{0,48},{48,0},{16,32},{32,16},{1,49},{49,1},{17,33},{33,17},{2,50}... | collective-permute-start | bytes 49160 | tf_op jit(solution)/shard_map/ppermute | solution.py:396
  42.5 2.4 %all-to-all-done.1.exit_ref = bf16[16,80,384]{2,1,0:T(8,128)(2,1)S(1)} async-done(((bf16[16,80,384]{2,1,0:T(8,128)(2,1)}), bf16[16,80,384]{2,1,0:T(8,128)(2,1)S(1)}, u32[]{:S(2)}, u32[]{:S(2)}) %all-to-all-start.1) | async-done | bytes 983072 | tf_op jit(solution)/shard_map/all_to_all | solution.py:392
  44.9 13.9 %all_to_all.40.tiles_ref = f32[16,32,128]{2,1,0:T(8,128)S(1)} all-to-all(f32[16,32,128]{2,1,0:T(8,128)S(1)} %total_kernel.2), channel_id=1, replica_groups=mesh['dp_0'=4,'dp_1'=4,'dp_2'=4,'mp_0'=2,'mp_1'=2] {'dp_0','dp_2'}, dimensions={0} | all-to-all | bytes 524288 | tf_op jit(solution)/shard_map/all_to_all | solution.py:392
  62.7 4.8 %collective-permute-start.4 = (bf16[640,128]{1,0:T(8,128)(2,1)S(1)}, bf16[640,128]{1,0:T(8,128)(2,1)S(1)}, u32[]{:S(2)}, u32[]{:S(2)}) collective-permute-start(bf16[640,128]{1,0:T(8,128)(2,1)S(1)} %get-tuple-element.56), channel_id=1, source_target_pairs={{0,1},{1,0},{2,3},{3,2},{4,5},{5,4},{6,7},{7,6},{8,9},{9,8},{10,11... | collective-permute-start | bytes 491528 | tf_op jit(solution)/shard_map/ppermute | solution.py:382
  67.5 3.6 %all-to-all-start.3 = ((bf16[16,80,384]{2,1,0:T(8,128)(2,1)}), bf16[16,80,384]{2,1,0:T(8,128)(2,1)S(1)}, u32[]{:S(2)}, u32[]{:S(2)}) async-start(bf16[16,80,384]{2,1,0:T(8,128)(2,1)} %get-tuple-element.53), calls=%async_computation.3 | async-start | bytes 1966080 | tf_op jit(solution)/shard_map/all_to_all | solution.py:392
  72.0 5.1 %collective-permute-done.5 = bf16[640,128]{1,0:T(8,128)(2,1)S(1)} collective-permute-done((bf16[640,128]{1,0:T(8,128)(2,1)S(1)}, bf16[640,128]{1,0:T(8,128)(2,1)S(1)}, u32[]{:S(2)}, u32[]{:S(2)}) %collective-permute-start.5) | collective-permute-done | bytes 163872 | tf_op jit(solution)/shard_map/ppermute | solution.py:382
  79.1 8.7 %all-to-all-done.3.head_ref = bf16[16,80,384]{2,1,0:T(8,128)(2,1)S(1)} async-done(((bf16[16,80,384]{2,1,0:T(8,128)(2,1)}), bf16[16,80,384]{2,1,0:T(8,128)(2,1)S(1)}, u32[]{:S(2)}, u32[]{:S(2)}) %all-to-all-start.3) | async-done | bytes 983072 | tf_op jit(solution)/shard_map/all_to_all | solution.py:392
  87.8 2.9 %head_kernel.1 = (bf16[640,128]{1,0:T(8,128)(2,1)S(1)}, bf16[640,128]{1,0:T(8,128)(2,1)}, bf16[16,80,384]{2,1,0:T(8,128)(2,1)}, f32[1280,128]{1,0:T(8,128)S(1)},...) custom-call(bf16[16,80,384]{2,1,0:T(8,128)(2,1)S(1)} %all-to-all-done.1.exit_ref, ...), custom_call_target="tpu_custom_call" | custom-call | tf_op jit(solution)/shard_map/head_kernel/pallas_call | solution.py:78
  92.7 4.4 %all-to-all-start.4 = ((bf16[16,80,384]{2,1,0:T(8,128)(2,1)}), bf16[16,80,384]{2,1,0:T(8,128)(2,1)}, u32[]{:S(2)}, u32[]{:S(2)}) async-start(bf16[16,80,384]{2,1,0:T(8,128)(2,1)} %get-tuple-element.70), calls=%async_computation.4 | async-start | bytes 1966080 | tf_op jit(solution)/shard_map/all_to_all | solution.py:392
  98.0 5.2 %collective-permute-done.8 = bf16[640,128]{1,0:T(8,128)(2,1)S(1)} collective-permute-done((bf16[640,128]{1,0:T(8,128)(2,1)S(1)}, bf16[640,128]{1,0:T(8,128)(2,1)S(1)}, u32[]{:S(2)}, u32[]{:S(2)}) %collective-permute-start.8) | collective-permute-done | bytes 163872 | tf_op jit(solution)/shard_map/ppermute | solution.py:382
  105.3 2.9 %backward_kernel.1 = (bf16[16,80,384]{2,1,0:T(8,128)(2,1)}, f32[16,32,128]{2,1,0:T(8,128)S(1)}) custom-call(bf16[16,80,384]{2,1,0:T(8,128)(2,1)S(1)} %all-to-all-done.1.exit_ref, bf16[16,80,384]{2,1,0:T(8,128)(2,1)S(1)} %all-to-all-done.3.head_ref, f32[16,32,128]{2,1,0:T(8,128)S(1)} %all_to_all.40.tiles_ref, ...), custom_call_target="tpu_custom_call" | custom-call | tf_op jit(solution)/shard_map/backward_kernel/pallas_call | solution.py:78
  108.9 5.2 %all-to-all-done.4 = bf16[16,80,384]{2,1,0:T(8,128)(2,1)} async-done(((bf16[16,80,384]{2,1,0:T(8,128)(2,1)}), bf16[16,80,384]{2,1,0:T(8,128)(2,1)}, u32[]{:S(2)}, u32[]{:S(2)}) %all-to-all-start.4) | async-done | bytes 983072 | tf_op jit(solution)/shard_map/all_to_all | solution.py:392
  114.1 10.8 %all_to_all.41 = f32[16,32,128]{2,1,0:T(8,128)S(1)} all-to-all(f32[16,32,128]{2,1,0:T(8,128)} %copy-done.1), channel_id=1, replica_groups=mesh['dp_0'=4,'dp_1'=4,'dp_2'=4,'mp_0'=2,'mp_1'=2] {'dp_0','dp_2'}, dimensions={0} | all-to-all | bytes 524288 | tf_op jit(solution)/shard_map/all_to_all | solution.py:392
  124.9 3.7 %all-to-all-start.6 = ((bf16[16,80,384]{2,1,0:T(8,128)(2,1)}), bf16[16,80,384]{2,1,0:T(8,128)(2,1)S(1)}, u32[]{:S(2)}, u32[]{:S(2)}) async-start(bf16[16,80,384]{2,1,0:T(8,128)(2,1)} %get-tuple-element.73), calls=%async_computation.6 | async-start | bytes 1966080 | tf_op jit(solution)/shard_map/all_to_all | solution.py:392
  130.8 3.4 %collective-permute-start.14 = (bf16[40,384]{1,0:T(8,128)(2,1)S(1)}, bf16[40,384]{1,0:T(8,128)(2,1)S(1)}, u32[]{:S(2)}, u32[]{:S(2)}) collective-permute-start(bf16[40,384]{1,0:T(8,128)(2,1)S(1)} %slice.60), channel_id=1, source_target_pairs={{0,48},{48,0},{16,32},{32,16},{1,49},{49,1},{17,33},{33,17},{2,50}... | collective-permute-start | bytes 92168 | tf_op jit(solution)/shard_map/ppermute | solution.py:396
  134.2 1.9 %collective-permute-start.11 = (f32[32,128]{1,0:T(8,128)S(1)}, f32[32,128]{1,0:T(8,128)S(1)}, u32[]{:S(2)}, u32[]{:S(2)}) collective-permute-start(f32[32,128]{1,0:T(8,128)S(1)} %add.61.one_ref), channel_id=1, source_target_pairs={{0,48},{48,0},{16,32},{32,16},{1,49},{49,1},{17,33},{33,17},{2,50}... | collective-permute-start | bytes 49160 | tf_op jit(solution)/shard_map/ppermute | solution.py:396
  136.1 6.6 %all-to-all-done.6 = bf16[16,80,384]{2,1,0:T(8,128)(2,1)S(1)} async-done(((bf16[16,80,384]{2,1,0:T(8,128)(2,1)}), bf16[16,80,384]{2,1,0:T(8,128)(2,1)S(1)}, u32[]{:S(2)}, u32[]{:S(2)}) %all-to-all-start.6) | async-done | bytes 983072 | tf_op jit(solution)/shard_map/all_to_all | solution.py:392
  142.9 3.9 %collective-permute-start.12 = (bf16[40,384]{1,0:T(8,128)(2,1)S(1)}, bf16[40,384]{1,0:T(8,128)(2,1)S(1)}, u32[]{:S(2)}, u32[]{:S(2)}) collective-permute-start(bf16[40,384]{1,0:T(8,128)(2,1)S(1)} %slice.61), channel_id=1, source_target_pairs={{0,48},{48,0},{16,32},{32,16},{1,49},{49,1},{17,33},{33,17},{2,50}... | collective-permute-start | bytes 92168 | tf_op jit(solution)/shard_map/ppermute | solution.py:396
  147.9 4.6 %all-to-all-start.7 = ((f32[16,32,128]{2,1,0:T(8,128)}), f32[16,32,128]{2,1,0:T(8,128)S(1)}, u32[]{:S(2)}, u32[]{:S(2)}) async-start(f32[16,32,128]{2,1,0:T(8,128)} %total_kernel.3), calls=%async_computation.7 | async-start | bytes 524288 | tf_op jit(solution)/shard_map/all_to_all | solution.py:392
  152.5 2.3 %collective-permute-start.13 = (bf16[20,384]{1,0:T(8,128)(2,1)S(1)}, bf16[20,384]{1,0:T(8,128)(2,1)S(1)}, u32[]{:S(2)}, u32[]{:S(2)}) collective-permute-start(bf16[20,384]{1,0:T(8,128)(2,1)S(1)} %slice.63), channel_id=1, source_target_pairs={{0,16},{16,0},{32,48},{48,32},{1,17},{17,1},{33,49},{49,33},{2,18}... | collective-permute-start | bytes 46088 | tf_op jit(solution)/shard_map/ppermute | solution.py:396
  156.1 3.8 %all-to-all-done.7.tiles_ref = f32[16,32,128]{2,1,0:T(8,128)S(1)} async-done(((f32[16,32,128]{2,1,0:T(8,128)}), f32[16,32,128]{2,1,0:T(8,128)S(1)}, u32[]{:S(2)}, u32[]{:S(2)}) %all-to-all-start.7) | async-done | bytes 262176 | tf_op jit(solution)/shard_map/all_to_all | solution.py:392
  161.3 3.8 %collective-permute-start.16 = (f32[24,128]{1,0:T(8,128)S(1)}, f32[24,128]{1,0:T(8,128)S(1)}, u32[]{:S(2)}, u32[]{:S(2)}) collective-permute-start(f32[24,128]{1,0:T(8,128)S(1)} %get-tuple-element.75), channel_id=1, source_target_pairs={{0,1},{1,0},{2,3},{3,2},{4,5},{5,4},{6,7},{7,6},{8,9},{9,8},{10,11... | collective-permute-start | bytes 36872 | tf_op jit(solution)/shard_map/ppermute | solution.py:382
  165.9 1.8 %collective-permute-start.17 = (f32[24,128]{1,0:T(8,128)S(1)}, f32[24,128]{1,0:T(8,128)S(1)}, u32[]{:S(2)}, u32[]{:S(2)}) collective-permute-start(f32[24,128]{1,0:T(8,128)S(1)} %add.66.one_ref), channel_id=1, source_target_pairs={{0,2},{2,0},{1,3},{3,1},{4,6},{6,4},{5,7},{7,5},{8,10},{10,8},{9,1... | collective-permute-start | bytes 36872 | tf_op jit(solution)/shard_map/ppermute | solution.py:382
  (101 shorter events, 25.7 us)
Async XLA Ops:
  0.6 13.0 %copy-start.18 = (f32[8,512]{1,0:T(8,128)S(1)}, f32[8,512]{1,0:T(8,128)}, u32[]{:S(2)}) copy-start(f32[8,512]{1,0:T(8,128)} %param.12) | copy-start | bytes 49156
  3.0 21.3 %all-to-all-start = ((f32[16,32,128]{2,1,0:T(8,128)}), f32[16,32,128]{2,1,0:T(8,128)S(1)}, u32[]{:S(2)}, u32[]{:S(2)}) async-start(f32[16,32,128]{2,1,0:T(8,128)} %get-tuple-element.46), calls=%async_computation | async-start | bytes 524288 | tf_op jit(solution)/shard_map/all_to_all | solution.py:392
  10.5 4.8 %collective-permute-start = (bf16[64,384]{1,0:T(8,128)(2,1)}, bf16[64,384]{1,0:T(8,128)(2,1)S(1)}, u32[]{:S(2)}, u32[]{:S(2)}) collective-permute-start(bf16[64,384]{1,0:T(8,128)(2,1)} %get-tuple-element.47.own_ref), channel_id=1, source_target_pairs={{0,16},{16,0},{32,48},{48,32},{1,17},{17,1},{33,49},{49,33},{2,18}... | collective-permute-start | bytes 147464 | tf_op jit(solution)/shard_map/ppermute | solution.py:396
  16.1 8.2 %collective-permute-start.1 = (bf16[128,384]{1,0:T(8,128)(2,1)S(1)}, bf16[128,384]{1,0:T(8,128)(2,1)S(1)}, u32[]{:S(2)}, u32[]{:S(2)}) collective-permute-start(bf16[128,384]{1,0:T(8,128)(2,1)S(1)} %pad_maximum_fusion), channel_id=1, source_target_pairs={{0,48},{48,0},{16,32},{32,16},{1,49},{49,1},{17,33},{33,17},{2,50}... | collective-permute-start | bytes 294920 | tf_op jit(solution)/shard_map/ppermute | solution.py:396
  26.5 14.8 %copy-start.19 = (bf16[16,128]{1,0:T(8,128)(2,1)S(1)}, bf16[16,128]{1,0:T(8,128)(2,1)}, u32[]{:S(2)}) copy-start(bf16[16,128]{1,0:T(8,128)(2,1)} %constant.31.clone) | copy-start | bytes 12292
  26.5 18.4 %all-to-all-start.1 = ((bf16[16,80,384]{2,1,0:T(8,128)(2,1)}), bf16[16,80,384]{2,1,0:T(8,128)(2,1)S(1)}, u32[]{:S(2)}, u32[]{:S(2)}) async-start(bf16[16,80,384]{2,1,0:T(8,128)(2,1)} %get-tuple-element.49), calls=%async_computation.1 | async-start | bytes 1966080 | tf_op jit(solution)/shard_map/all_to_all | solution.py:392
  33.7 3.6 %collective-permute-start.2 = (f32[32,128]{1,0:T(8,128)S(1)}, f32[32,128]{1,0:T(8,128)S(1)}, u32[]{:S(2)}, u32[]{:S(2)}) collective-permute-start(f32[32,128]{1,0:T(8,128)S(1)} %get-tuple-element.48), channel_id=1, source_target_pairs={{0,16},{16,0},{32,48},{48,32},{1,17},{17,1},{33,49},{49,33},{2,18}... | collective-permute-start | bytes 49160 | tf_op jit(solution)/shard_map/ppermute | solution.py:396
  37.3 5.1 %collective-permute-start.3 = (f32[32,128]{1,0:T(8,128)S(1)}, f32[32,128]{1,0:T(8,128)S(1)}, u32[]{:S(2)}, u32[]{:S(2)}) collective-permute-start(f32[32,128]{1,0:T(8,128)S(1)} %add.52.one_ref), channel_id=1, source_target_pairs={{0,48},{48,0},{16,32},{32,16},{1,49},{49,1},{17,33},{33,17},{2,50}... | collective-permute-start | bytes 49160 | tf_op jit(solution)/shard_map/ppermute | solution.py:396
  62.7 8.5 %collective-permute-start.4 = (bf16[640,128]{1,0:T(8,128)(2,1)S(1)}, bf16[640,128]{1,0:T(8,128)(2,1)S(1)}, u32[]{:S(2)}, u32[]{:S(2)}) collective-permute-start(bf16[640,128]{1,0:T(8,128)(2,1)S(1)} %get-tuple-element.56), channel_id=1, source_target_pairs={{0,1},{1,0},{2,3},{3,2},{4,5},{5,4},{6,7},{7,6},{8,9},{9,8},{10,11... | collective-permute-start | bytes 491528 | tf_op jit(solution)/shard_map/ppermute | solution.py:382
  67.5 20.3 %all-to-all-start.3 = ((bf16[16,80,384]{2,1,0:T(8,128)(2,1)}), bf16[16,80,384]{2,1,0:T(8,128)(2,1)S(1)}, u32[]{:S(2)}, u32[]{:S(2)}) async-start(bf16[16,80,384]{2,1,0:T(8,128)(2,1)} %get-tuple-element.53), calls=%async_computation.3 | async-start | bytes 1966080 | tf_op jit(solution)/shard_map/all_to_all | solution.py:392
  71.3 5.8 %collective-permute-start.5 = (bf16[640,128]{1,0:T(8,128)(2,1)S(1)}, bf16[640,128]{1,0:T(8,128)(2,1)S(1)}, u32[]{:S(2)}, u32[]{:S(2)}) collective-permute-start(bf16[640,128]{1,0:T(8,128)(2,1)S(1)} %add_convert_fusion.3), channel_id=1, source_target_pairs={{0,2},{2,0},{1,3},{3,1},{4,6},{6,4},{5,7},{7,5},{8,10},{10,8},{9,1... | collective-permute-start | bytes 491528 | tf_op jit(solution)/shard_map/ppermute | solution.py:382
  77.1 2.0 %collective-permute-start.6 = (bf16[640,128]{1,0:T(8,128)(2,1)S(1)}, bf16[640,128]{1,0:T(8,128)(2,1)S(1)}, u32[]{:S(2)}, u32[]{:S(2)}) collective-permute-start(bf16[640,128]{1,0:T(8,128)(2,1)S(1)} %add_convert_fusion.2.half_ref), channel_id=1, source_target_pairs={{0,1},{1,0},{2,3},{3,2},{4,5},{5,4},{6,7},{7,6},{8,9},{9,8},{10,11... | collective-permute-start | bytes 491528 | tf_op jit(solution)/shard_map/ppermute | solution.py:382
  91.4 5.8 %collective-permute-start.7 = (bf16[640,128]{1,0:T(8,128)(2,1)}, bf16[640,128]{1,0:T(8,128)(2,1)S(1)}, u32[]{:S(2)}, u32[]{:S(2)}) collective-permute-start(bf16[640,128]{1,0:T(8,128)(2,1)} %get-tuple-element.59), channel_id=1, source_target_pairs={{0,1},{1,0},{2,3},{3,2},{4,5},{5,4},{6,7},{7,6},{8,9},{9,8},{10,11... | collective-permute-start | bytes 491528 | tf_op jit(solution)/shard_map/ppermute | solution.py:382
  92.7 21.4 %all-to-all-start.4 = ((bf16[16,80,384]{2,1,0:T(8,128)(2,1)}), bf16[16,80,384]{2,1,0:T(8,128)(2,1)}, u32[]{:S(2)}, u32[]{:S(2)}) async-start(bf16[16,80,384]{2,1,0:T(8,128)(2,1)} %get-tuple-element.70), calls=%async_computation.4 | async-start | bytes 1966080 | tf_op jit(solution)/shard_map/all_to_all | solution.py:392
  97.3 5.9 %collective-permute-start.8 = (bf16[640,128]{1,0:T(8,128)(2,1)S(1)}, bf16[640,128]{1,0:T(8,128)(2,1)S(1)}, u32[]{:S(2)}, u32[]{:S(2)}) collective-permute-start(bf16[640,128]{1,0:T(8,128)(2,1)S(1)} %add_convert_fusion.1), channel_id=1, source_target_pairs={{0,2},{2,0},{1,3},{3,1},{4,6},{6,4},{5,7},{7,5},{8,10},{10,8},{9,1... | collective-permute-start | bytes 491528 | tf_op jit(solution)/shard_map/ppermute | solution.py:382
  103.3 2.1 %collective-permute-start.9 = (bf16[640,128]{1,0:T(8,128)(2,1)S(1)}, bf16[640,128]{1,0:T(8,128)(2,1)S(1)}, u32[]{:S(2)}, u32[]{:S(2)}) collective-permute-start(bf16[640,128]{1,0:T(8,128)(2,1)S(1)} %add_convert_fusion.half_ref), channel_id=1, source_target_pairs={{0,1},{1,0},{2,3},{3,2},{4,5},{5,4},{6,7},{7,6},{8,9},{9,8},{10,11... | collective-permute-start | bytes 491528 | tf_op jit(solution)/shard_map/ppermute | solution.py:382
  124.9 17.7 %all-to-all-start.6 = ((bf16[16,80,384]{2,1,0:T(8,128)(2,1)}), bf16[16,80,384]{2,1,0:T(8,128)(2,1)S(1)}, u32[]{:S(2)}, u32[]{:S(2)}) async-start(bf16[16,80,384]{2,1,0:T(8,128)(2,1)} %get-tuple-element.73), calls=%async_computation.6 | async-start | bytes 1966080 | tf_op jit(solution)/shard_map/all_to_all | solution.py:392
  128.6 5.5 %collective-permute-start.10 = (f32[32,128]{1,0:T(8,128)S(1)}, f32[32,128]{1,0:T(8,128)S(1)}, u32[]{:S(2)}, u32[]{:S(2)}) collective-permute-start(f32[32,128]{1,0:T(8,128)S(1)} %reduce_sum.47), channel_id=1, source_target_pairs={{0,16},{16,0},{32,48},{48,32},{1,17},{17,1},{33,49},{49,33},{2,18}... | collective-permute-start | bytes 49160 | tf_op jit(solution)/shard_map/ppermute | solution.py:396
  130.8 16.1 %collective-permute-start.14 = (bf16[40,384]{1,0:T(8,128)(2,1)S(1)}, bf16[40,384]{1,0:T(8,128)(2,1)S(1)}, u32[]{:S(2)}, u32[]{:S(2)}) collective-permute-start(bf16[40,384]{1,0:T(8,128)(2,1)S(1)} %slice.60), channel_id=1, source_target_pairs={{0,48},{48,0},{16,32},{32,16},{1,49},{49,1},{17,33},{33,17},{2,50}... | collective-permute-start | bytes 92168 | tf_op jit(solution)/shard_map/ppermute | solution.py:396
  134.2 12.9 %collective-permute-start.11 = (f32[32,128]{1,0:T(8,128)S(1)}, f32[32,128]{1,0:T(8,128)S(1)}, u32[]{:S(2)}, u32[]{:S(2)}) collective-permute-start(f32[32,128]{1,0:T(8,128)S(1)} %add.61.one_ref), channel_id=1, source_target_pairs={{0,48},{48,0},{16,32},{32,16},{1,49},{49,1},{17,33},{33,17},{2,50}... | collective-permute-start | bytes 49160 | tf_op jit(solution)/shard_map/ppermute | solution.py:396
  142.8 17.1 %copy-start = (f32[64,16,20]{2,1,0:T(8,128)S(1)}, f32[64,16,20]{2,1,0:T(8,128)}, u32[]{:S(2)}) copy-start(f32[64,16,20]{2,1,0:T(8,128)} %constant.29.clone.table_ref) | copy-start | bytes 245764
  142.8 17.1 %copy-start.13 = (bf16[20,320]{1,0:T(8,128)(2,1)S(1)}, bf16[20,320]{1,0:T(8,128)(2,1)}, u32[]{:S(2)}) copy-start(bf16[20,320]{1,0:T(8,128)(2,1)} %wq_ref.3) | copy-start | bytes 38404
  142.9 17.1 %copy-start.14 = (bf16[20,320]{1,0:T(8,128)(2,1)S(1)}, bf16[20,320]{1,0:T(8,128)(2,1)}, u32[]{:S(2)}) copy-start(bf16[20,320]{1,0:T(8,128)(2,1)} %wk_ref.3) | copy-start | bytes 38404
  142.9 17.1 %copy-start.15 = (bf16[20,320]{1,0:T(8,128)(2,1)S(1)}, bf16[20,320]{1,0:T(8,128)(2,1)}, u32[]{:S(2)}) copy-start(bf16[20,320]{1,0:T(8,128)(2,1)} %wv_ref.3) | copy-start | bytes 38404
  142.9 17.1 %copy-start.16 = (bf16[32,20]{0,1:T(8,128)(2,1)S(1)}, bf16[32,20]{0,1:T(8,128)(2,1)}, u32[]{:S(2)}) copy-start(bf16[32,20]{0,1:T(8,128)(2,1)} %param.14) | copy-start | bytes 3844
  142.9 17.1 %copy-start.17 = (bf16[2,20]{1,0:T(2,128)(2,1)S(1)}, bf16[2,20]{1,0:T(2,128)(2,1)}, u32[]{:S(2)}) copy-start(bf16[2,20]{1,0:T(2,128)(2,1)} %gains_ref.3) | copy-start | bytes 244
  142.9 9.6 %collective-permute-start.12 = (bf16[40,384]{1,0:T(8,128)(2,1)S(1)}, bf16[40,384]{1,0:T(8,128)(2,1)S(1)}, u32[]{:S(2)}, u32[]{:S(2)}) collective-permute-start(bf16[40,384]{1,0:T(8,128)(2,1)S(1)} %slice.61), channel_id=1, source_target_pairs={{0,48},{48,0},{16,32},{32,16},{1,49},{49,1},{17,33},{33,17},{2,50}... | collective-permute-start | bytes 92168 | tf_op jit(solution)/shard_map/ppermute | solution.py:396
  146.9 8.0 %collective-permute-start.15 = (bf16[20,384]{1,0:T(8,128)(2,1)S(1)}, bf16[20,384]{1,0:T(8,128)(2,1)S(1)}, u32[]{:S(2)}, u32[]{:S(2)}) collective-permute-start(bf16[20,384]{1,0:T(8,128)(2,1)S(1)} %slice.62), channel_id=1, source_target_pairs={{0,16},{16,0},{32,48},{48,32},{1,17},{17,1},{33,49},{49,33},{2,18}... | collective-permute-start | bytes 46088 | tf_op jit(solution)/shard_map/ppermute | solution.py:396
  147.9 12.1 %all-to-all-start.7 = ((f32[16,32,128]{2,1,0:T(8,128)}), f32[16,32,128]{2,1,0:T(8,128)S(1)}, u32[]{:S(2)}, u32[]{:S(2)}) async-start(f32[16,32,128]{2,1,0:T(8,128)} %total_kernel.3), calls=%async_computation.7 | async-start | bytes 524288 | tf_op jit(solution)/shard_map/all_to_all | solution.py:392
  152.5 3.6 %collective-permute-start.13 = (bf16[20,384]{1,0:T(8,128)(2,1)S(1)}, bf16[20,384]{1,0:T(8,128)(2,1)S(1)}, u32[]{:S(2)}, u32[]{:S(2)}) collective-permute-start(bf16[20,384]{1,0:T(8,128)(2,1)S(1)} %slice.63), channel_id=1, source_target_pairs={{0,16},{16,0},{32,48},{48,32},{1,17},{17,1},{33,49},{49,33},{2,18}... | collective-permute-start | bytes 46088 | tf_op jit(solution)/shard_map/ppermute | solution.py:396
  161.3 4.7 %collective-permute-start.16 = (f32[24,128]{1,0:T(8,128)S(1)}, f32[24,128]{1,0:T(8,128)S(1)}, u32[]{:S(2)}, u32[]{:S(2)}) collective-permute-start(f32[24,128]{1,0:T(8,128)S(1)} %get-tuple-element.75), channel_id=1, source_target_pairs={{0,1},{1,0},{2,3},{3,2},{4,5},{5,4},{6,7},{7,6},{8,9},{9,8},{10,11... | collective-permute-start | bytes 36872 | tf_op jit(solution)/shard_map/ppermute | solution.py:382
  165.9 2.8 %collective-permute-start.17 = (f32[24,128]{1,0:T(8,128)S(1)}, f32[24,128]{1,0:T(8,128)S(1)}, u32[]{:S(2)}, u32[]{:S(2)}) collective-permute-start(f32[24,128]{1,0:T(8,128)S(1)} %add.66.one_ref), channel_id=1, source_target_pairs={{0,2},{2,0},{1,3},{3,1},{4,6},{6,4},{5,7},{7,5},{8,10},{10,8},{9,1... | collective-permute-start | bytes 36872 | tf_op jit(solution)/shard_map/ppermute | solution.py:382
  (13 other events, 48.7 us)

commit v4 on v3

--- a/solution.py
+++ b/solution.py
@@ -8,6 +8,7 @@
 from jax.experimental.pallas import tpu as pltpu
 from jax.sharding import Mesh
 from jax.sharding import PartitionSpec as P
+
 
 WIDTH = 1280
 PATCH = 32
@@ -31,13 +32,15 @@
 LINED = 32
 FIRST = [(0, 1), (1, 0), (2, 3), (3, 2)]
 SECOND = [(0, 3), (3, 0), (1, 2), (2, 1)]
+FOURTH = [(0, 2), (2, 0), (1, 3), (3, 1)]
 HALF = WIDTH // 2
 MP = ("mp_0", "mp_1")
+HEADS = [slice(at, at + HEAD_DIM) for at in range(0, COLS, HEAD_DIM)]
 EPS = 1e-06
 STAT_EPS = 1e-05
 RADIUS = 0.05
 SCALE = 1.0 / math.sqrt(HEAD_DIM)
-GRANT = 24 * 1024 * 1024
+GRANT = 16 * 1024 * 1024
 BF = jnp.bfloat16
 F32 = jnp.float32
 
@@ -78,7 +81,6 @@
     return pl.pallas_call(
         body,
         out_shape=[jax.ShapeDtypeStruct(s, d) for s, d in outs],
-        name=body.__name__,
         compiler_params=pltpu.CompilerParams(vmem_limit_bytes=grant),
     )(*args)
 
@@ -157,25 +159,25 @@
     return same & (j <= i)
 
 
-def attention_kernel(
-    exit_ref, tiles_ref, basis_ref, mine_ref, other_ref, context_ref, queries_ref, keys_ref, values_ref, probs_ref, factor_ref
-):
+def attention(exit_ref, tiles_ref, basis_ref):
     residual = first_residual(exit_ref, basis_ref)
     factor = lax.rsqrt(jnp.sum(residual * residual, axis=0, keepdims=True) / WIDTH + EPS)
-    factor_ref[...] = jnp.broadcast_to(factor, factor_ref.shape)
-    raw = raw_projections(tiles_ref, basis_ref[0:BASIS, :]) * factor
-    queries_ref[...] = raw[0:COLS].astype(BF)
-    keys_ref[...] = raw[WIDE : WIDE + COLS].astype(BF)
-    values_ref[...] = raw[2 * WIDE : 2 * WIDE + COLS].astype(BF)
+    raw = raw_projections(tiles_ref, basis_ref[0:BASIS, :])
+    queries, keys, values = ((raw[w * WIDE : w * WIDE + COLS] * factor).astype(BF) for w in range(3))
     mask = causal_mask()
-    for h in range(COLS // HEAD_DIM):
-        at = slice(h * HEAD_DIM, (h + 1) * HEAD_DIM)
-        scores = tn(keys_ref[at, :], queries_ref[at, :]) * SCALE
+    all_probs, context = [], []
+    for at in HEADS:
+        scores = tn(keys[at], queries[at]) * SCALE
         raised = jnp.where(mask, jnp.exp(scores), 0.0)
         probs = raised / jnp.sum(raised, axis=0, keepdims=True)
-        probs_ref[h] = probs
-        context_ref[at, :] = nn(values_ref[at, :], probs.astype(BF)).astype(BF)
-    context = jnp.concatenate([context_ref[...], jnp.zeros((WIDE - COLS, TOKENS), BF)], axis=0)
+        all_probs.append(probs)
+        context.append(nn(values[at], probs.astype(BF)).astype(BF))
+    return factor, raw, queries, keys, values, all_probs, context
+
+
+def attention_kernel(exit_ref, tiles_ref, basis_ref, mine_ref, other_ref):
+    context = attention(exit_ref, tiles_ref, basis_ref)[-1]
+    context = jnp.concatenate([*context, jnp.zeros((WIDE - COLS, TOKENS), BF)], axis=0)
     spread_halves(nn(blocks(exit_ref), context), mine_ref, other_ref)
 
 
@@ -190,14 +192,11 @@
     other_ref,
     grad_ref,
     residual_ref,
-    factor_ref,
-    loss_ref,
 ):
     head = blocks(head_ref)
     residual = first_residual(exit_ref, basis_ref) + joined_halves(half_ref, rest_ref)
-    residual_ref[...] = residual
+    residual_ref[0:WIDTH, :] = residual
     factor = lax.rsqrt(jnp.sum(residual * residual, axis=0, keepdims=True) / WIDTH + EPS)
-    factor_ref[...] = jnp.broadcast_to(factor, factor_ref.shape)
     scaled = residual * factor
     normed = (scaled * head[:, COLS + 1 : COLS + 2].astype(F32)).astype(BF)
     forecast = tn(head, normed)[0:COLS]
@@ -218,7 +217,7 @@
     softplus = jnp.maximum(inside, 0.0) + jnp.log1p(tail)
     sigmoid = jnp.where(inside >= 0.0, 1.0, tail) / (1.0 + tail)
     terms = jnp.where(mean_channel, error * error, share * error + RADIUS * softplus)
-    loss_ref[...] = jnp.broadcast_to(jnp.sum(terms, axis=0, keepdims=True), loss_ref.shape)
+    residual_ref[WIDTH:, :] = jnp.broadcast_to(jnp.sum(terms, axis=0, keepdims=True), (8, TOKENS))
     slope = (jnp.where(mean_channel, -2.0 * error, sigmoid - share) * (1.0 / 128.0)).astype(BF)
     slope = jnp.concatenate([slope, jnp.zeros((WIDE - COLS, TOKENS), BF)], axis=0)
     back = nn(head, slope)
@@ -238,56 +237,46 @@
     half_ref,
     rest_ref,
     residual_ref,
-    factor_one_ref,
-    factor_zero_ref,
-    context_ref,
-    queries_ref,
-    keys_ref,
-    values_ref,
-    probs_ref,
-    loss_ref,
     grad_ref,
     out_ref,
 ):
+    factor_zero, raw, queries, keys, values, all_probs, context = attention(exit_ref, tiles_ref, basis_ref)
     basis = basis_ref[0:BASIS, :]
     patches = basis_ref[0:PATCH, :]
     upstream = joined_halves(half_ref, rest_ref)
-    residual = residual_ref[...]
-    factor = factor_one_ref[0:1, :]
+    residual = residual_ref[0:WIDTH, :]
+    factor = lax.rsqrt(jnp.sum(residual * residual, axis=0, keepdims=True) / WIDTH + EPS)
     weighted = blocks(head_ref, slice(256, 384))[:, COLS - 255 : COLS - 254].astype(F32) * upstream
     inner = jnp.sum(weighted * residual, axis=0, keepdims=True) / WIDTH
     low = (factor * weighted - residual * (factor * factor * factor * inner)).astype(BF)
-    grad = nt(low, jnp.concatenate([context_ref[...], patches, patches], axis=0))
+    grad = nt(low, jnp.concatenate([*context, patches, patches], axis=0))
     lane = lax.broadcasted_iota(jnp.int32, (1, WIDE), 1)
     grad = jnp.where(lane >= COLS + PATCH, grad - grad.astype(BF).astype(F32), grad)
     grad_ref[...] = grad.astype(BF).reshape(GROUPS, GROUP_ROWS, WIDE)
     context_grad = tn(blocks(exit_ref), low)[0:COLS].astype(BF)
     backs = ([], [], [])
-    for h in range(COLS // HEAD_DIM):
-        at = slice(h * HEAD_DIM, (h + 1) * HEAD_DIM)
+    for at, probs in zip(HEADS, all_probs):
         slope = context_grad[at]
-        probs = probs_ref[h]
-        prob_grad = tn(values_ref[at, :], slope)
+        prob_grad = tn(values[at], slope)
         value_back = nt(slope, probs.astype(BF))
         centred = prob_grad - jnp.sum(probs * prob_grad, axis=0, keepdims=True)
         score_grad = (probs * centred * SCALE).astype(BF)
-        backs[0].append(nn(keys_ref[at, :], score_grad).astype(BF))
-        backs[1].append(nt(queries_ref[at, :], score_grad).astype(BF))
+        backs[0].append(nn(keys[at], score_grad).astype(BF))
+        backs[1].append(nt(queries[at], score_grad).astype(BF))
         backs[2].append(value_back.astype(BF))
     gap = jnp.zeros((WIDE - COLS, TOKENS), BF)
     back = jnp.concatenate([*backs[0], gap, *backs[1], gap, *backs[2], gap], axis=0)
-    factor = factor_zero_ref[0:1, :]
+    factor = factor_zero
     entries = basis.astype(F32)
     high, low = two(entries * factor)
     total = nt(high, back) + nt(low, back)
-    raw = raw_projections(tiles_ref, basis)
     inner = jnp.sum(back.astype(F32) * raw, axis=0, keepdims=True) / WIDTH
     high, low = two(entries * (factor * factor * factor * inner))
     mixed = nt(high, patches) + nt(low, patches)
     blank = jnp.zeros((8, 128 - PATCH), F32)
     tiles = [total[8 * i : 8 * i + 8, 128 * j : 128 * j + 128] for i in range(BASIS // 8) for j in range(9)]
     tiles += [jnp.concatenate([mixed[8 * i : 8 * i + 8], blank], axis=1) for i in range(BASIS // 8)]
-    tiles += [loss_ref[...]]
+    tiles += [residual_ref[WIDTH:, :]]
     tiles += [jnp.zeros((8, 128), F32)] * (BLOCKS - len(tiles))
     for k in range(GROUPS):
         out_ref[k] = jnp.concatenate(tiles[DEPTH * k : DEPTH * k + DEPTH], axis=0)
@@ -300,10 +289,9 @@
     return total
 
 
-def gather_kernel(tiles_ref, own_ref, next_ref, far_ref, total_ref, exit_ref, head_ref):
+def gather_kernel(tiles_ref, own_ref, first_ref, second_ref, fourth_ref, total_ref, exit_ref, head_ref):
     total_ref[...] = group_sum(tiles_ref)
-    own, near, far = (ref[...].astype(F32) for ref in (own_ref, next_ref, far_ref))
-    parts = [own, near, far[: 2 * LINED], far[2 * LINED :]]
+    parts = [ref[...].astype(F32) for ref in (own_ref, first_ref, second_ref, fourth_ref)]
     exits = jnp.concatenate([p[0:OWN] for p in parts], axis=0).astype(BF)
     heads = jnp.concatenate([p[LINED : LINED + OWN] for p in parts], axis=0).astype(BF)
     for k in range(GROUPS):
@@ -315,6 +303,13 @@
     total = one_ref[...] + other_ref[...]
     for k in range(GROUPS):
         out_ref[k] = total
+
+
+def scatter_kernel(exit_ref, head_ref, keep_ref, send_ref):
+    exits, heads = group_sum(exit_ref), group_sum(head_ref)
+    rows = [x[OWN * at : OWN * at + OWN] for at in range(DEPTH) for x in (exits, heads)]
+    keep_ref[...] = jnp.concatenate(rows[:DEPTH], axis=0)
+    send_ref[...] = jnp.concatenate(rows[DEPTH:], axis=0).astype(BF)
 
 
 def exact(dims):
@@ -332,8 +327,7 @@
     wq_ref,
     wk_ref,
     wv_ref,
-    exit_ref,
-    head_ref,
+    sums_ref,
     q_ref,
     k_ref,
     v_ref,
@@ -360,6 +354,7 @@
 
     mixed = jnp.concatenate([small(TILES + i) for i in range(BASIS // 8)], axis=0)[:, 0:PATCH]
     embed = embed - exact(((0,), (0,)))(basis, mixed)
+    exit_ref, head_ref = sums_ref[0:OWN, :], sums_ref[OWN : 2 * OWN, :]
     ends = exit_ref[:, COLS : COLS + PATCH] + exit_ref[:, COLS + PATCH : WIDE]
     gain_one = head_ref[:, COLS : COLS + 1] + head_ref[:, COLS + 1 : COLS + 2]
     exit_grad_ref[...] = exit_ref[:, 0:COLS]
@@ -396,9 +391,9 @@
     return lax.ppermute(x, Z, pairs)
 
 
-def to_owner(x):
-    kept = x[: 2 * OWN] + along_z(x[2 * OWN :].astype(BF), SECOND).astype(F32)
-    return kept[:OWN] + along_z(kept[OWN:].astype(BF), FIRST).astype(F32)
+def z_total(x):
+    x = x + along_z(x, FIRST)
+    return call(total_kernel, [((GROUPS, SMALL, 128), F32)], x, along_z(x, SECOND))[0]
 
 
 def after(x, *others):
@@ -438,14 +433,12 @@
         grant=None,
     )
     tiles = over(tiles, XY)
-    near = along_z(block, FIRST)
-    far = along_z(jnp.concatenate([block, near], axis=0), SECOND)
+    column = [along_z(block, pairs) for pairs in (FIRST, SECOND, FOURTH)]
     total, exit_all, head_all = call(
-        gather_kernel, [((SMALL, 128), F32), groups, groups], tiles, block, near, far
+        gather_kernel, [((SMALL, 128), F32), groups, groups], tiles, block, *column
     )
     exit_all = over(exit_all, XY)
-    total = total + along_z(total, FIRST)
-    tiles = call(total_kernel, [tiles_like], total, along_z(total, SECOND))[0]
+    tiles = z_total(total)
 
     patches, target = prepare(history, later)
     number = np.arange(TOKENS) % PATCHES
@@ -455,28 +448,12 @@
     tiles = over(tiles, XY)
     head_all = over(after(head_all, tiles), XY)
 
-    turned = (COLS, TOKENS)
     half = ((HALF, TOKENS), BF)
-    mine, other, context, queries, keys, values, probs, factor_zero = call(
-        attention_kernel,
-        [
-            half,
-            half,
-            (turned, BF),
-            (turned, BF),
-            (turned, BF),
-            (turned, BF),
-            ((COLS // HEAD_DIM, TOKENS, TOKENS), F32),
-            ((8, TOKENS), F32),
-        ],
-        exit_all,
-        tiles,
-        basis,
-    )
+    mine, other = call(attention_kernel, [half, half], exit_all, tiles, basis)
     mine, other = mp_sum(mine, other)
-    mine, other, head_grad, residual, factor_one, loss = call(
+    mine, other, head_grad, residual = call(
         head_kernel,
-        [half, half, groups, ((WIDTH, TOKENS), F32), ((8, TOKENS), F32), ((8, TOKENS), F32)],
+        [half, half, groups, ((WIDTH + 8, TOKENS), F32)],
         exit_all,
         head_all,
         basis,
@@ -496,23 +473,15 @@
         mine,
         other,
         residual,
-        factor_one,
-        factor_zero,
-        context,
-        queries,
-        keys,
-        values,
-        probs,
-        loss,
     )
     totals = over(after(totals, head_grad), XY)
-    head_sum = to_owner(jnp.sum(head_grad.astype(F32), axis=0))
     exit_grad = over(after(exit_grad, totals), XY)
-    total = jnp.sum(totals, axis=0)
-    total = total + along_z(total, FIRST)
-    totals = call(total_kernel, [tiles_like], total, along_z(total, SECOND))[0]
+    totals = z_total(jnp.sum(totals, axis=0))
     totals = over(after(totals, exit_grad), XY)
-    exit_sum = to_owner(jnp.sum(exit_grad.astype(F32), axis=0))
+    rows = (4 * OWN, WIDE)
+    keep, send = call(scatter_kernel, [(rows, F32), (rows, BF)], exit_grad, head_grad)
+    keep = keep + along_z(send, SECOND).astype(F32)
+    sums = keep[: 2 * OWN] + along_z(keep[2 * OWN :].astype(BF), FIRST).astype(F32)
     own = ((OWN, COLS), F32)
     query_grad, key_grad, value_grad, output_grad, head_weight_grad, rest = call(
         last_kernel,
@@ -524,8 +493,7 @@
         asking,
         lookup,
         content,
-        exit_sum,
-        head_sum,
+        sums,
     )
     rest = rest + swapped(rest, "mp_1")
     embed_grad, gains_grad, loss_mean = call(
@@ -559,6 +527,7 @@
         P(MP, DP),
         P(DP, MP),
     )
+
     return jax.shard_map(
         per_device,
         mesh=split,

time: 170 us -> 173 us (1.018)
  blocking collectives: 24.7 us -> 39.2 us
  starting transfers between devices: 73 us -> 58.9 us
  waiting for transfers between devices: 49.1 us -> 55.6 us
  local copies, waits for them, and re-layouts: 4.99 us -> 3.05 us
    all_to_all x2 -> x3, blocking collectives: 24.7 us -> 39.2 us  [over(): return lax.all_to_all(x, axis, 0, 0, tiled=True)]
    all_to_all x6 -> x5, starting transfers between devices: 30.9 us -> 21.9 us  [over(): return lax.all_to_all(x, axis, 0, 0, tiled=True)]
    ppermute x10 -> x9, starting transfers between devices: 26.9 us -> 20.2 us  [along_z(): return lax.ppermute(x, Z, pairs)]
    all_to_all x6 -> x5, waiting for transfers between devices: 26.7 us -> 31.4 us  [over(): return lax.all_to_all(x, axis, 0, 0, tiled=True)]
    unnamed x42 -> x28, local copies, waits for them, and re-layouts: 4.73 us -> 2.82 us
    ppermute x10 -> x9, waiting for transfers between devices: 8.12 us -> 9.26 us  [along_z(): return lax.ppermute(x, Z, pairs)]
    pallas_call x9 -> x10, Pallas kernels: 13.6 us -> 13.1 us  [call(): pl.pallas_call(body, out_shape=[jax.ShapeDtypeStruct(s, d) for s, d in ou...]
  transfers between devices with their start and end apart: 24 -> 22, of which waited for: 16 -> 15; matrix products, arithmetic and copies ran while one was open for 2% -> 1% of each run, Pallas kernels for 2% -> 2%
where the time goes in v4:
time: 173 us
  starting transfers between devices  58.9 us (34%)
  waiting for transfers between devices  55.6 us (32%)
  blocking collectives  39.2 us (23%)
  Pallas kernels  13.1 us (8%)
  local copies, waits for them, and re-layouts  3.05 us (2%)
    all_to_all x3, blocking collectives, over(): return lax.all_to_all(x, axis, 0, 0, tiled=True)  39.2 us
    all_to_all x5, waiting for transfers between devices, over(): return lax.all_to_all(x, axis, 0, 0, tiled=True)  31.4 us
    all_to_all x5, starting transfers between devices, over(): return lax.all_to_all(x, axis, 0, 0, tiled=True)  21.9 us
    ppermute x9, starting transfers between devices, along_z(): return lax.ppermute(x, Z, pairs)  20.2 us
    ppermute x8, starting transfers between devices, swapped(): return lax.ppermute(x, axis, [(0, 1), (1, 0)])  16.8 us
    ppermute x8, waiting for transfers between devices, swapped(): return lax.ppermute(x, axis, [(0, 1), (1, 0)])  15 us
    pallas_call x10, Pallas kernels, call(): pl.pallas_call(body, out_shape=[jax.ShapeDtypeStruct(s, d) for s, d in ou...  13.1 us
    ppermute x9, waiting for transfers between devices, along_z(): return lax.ppermute(x, Z, pairs)  9.26 us
  transfers between devices with their start and end apart: 22, of which 15 were waited for; matrix products, arithmetic and copies ran while one was open for 1% of the time, Pallas kernels for 2%

profile of v4, /device:TPU:1, one launch (start us, length us, event | category | flops | bytes accessed | tf_op | source)
XLA Modules:
  0.0 172.5 jit_solution(4067848502526602800)
XLA Ops:
  0.6 2.3 %shard_map.179 = (f32[16,32,128]{2,1,0:T(8,128)}, bf16[64,384]{1,0:T(8,128)(2,1)}) custom-call(bf16[20,32]{1,0:T(8,128)(2,1)} %bitcast.10, bf16[2,20]{1,0:T(2,128)(2,1)} %gains_ref.3, f32[64,16,20]{2,1,0:T(8,128)} %constant.29.clone.table_ref, bf16[64,20,32]{2,1,0:T(8,128)(2,1)} %constant.30.clone.turned_ref, bf16[20,320]{1,0:T(8,128)(2,1)} %wq_ref.3, ...), custom_call_target="tpu_custom_call" | custom-call | tf_op jit(solution)/shard_map/pallas_call | solution.py:81
  2.9 7.7 %collective-permute-start.2 = (bf16[64,384]{1,0:T(8,128)(2,1)}, bf16[64,384]{1,0:T(8,128)(2,1)S(1)}, u32[]{:S(2)}, u32[]{:S(2)}) collective-permute-start(bf16[64,384]{1,0:T(8,128)(2,1)} %get-tuple-element.41.own_ref), channel_id=1, source_target_pairs={{0,32},{32,0},{16,48},{48,16},{1,33},{33,1},{17,49},{49,17},{2,34}... | collective-permute-start | bytes 147464 | tf_op jit(solution)/shard_map/ppermute | solution.py:391
  11.9 6.9 %all-to-all-start = ((f32[16,32,128]{2,1,0:T(8,128)}), f32[16,32,128]{2,1,0:T(8,128)S(1)}, u32[]{:S(2)}, u32[]{:S(2)}) async-start(f32[16,32,128]{2,1,0:T(8,128)} %get-tuple-element.40), calls=%async_computation | async-start | bytes 524288 | tf_op jit(solution)/shard_map/all_to_all | solution.py:387
  19.1 7.0 %all-to-all-done.tiles_ref = f32[16,32,128]{2,1,0:T(8,128)S(1)} async-done(((f32[16,32,128]{2,1,0:T(8,128)}), f32[16,32,128]{2,1,0:T(8,128)S(1)}, u32[]{:S(2)}, u32[]{:S(2)}) %all-to-all-start) | async-done | bytes 262176 | tf_op jit(solution)/shard_map/all_to_all | solution.py:387
  26.1 1.5 shard_map.180
  27.6 3.8 %all-to-all-start.1 = ((bf16[16,80,384]{2,1,0:T(8,128)(2,1)}), bf16[16,80,384]{2,1,0:T(8,128)(2,1)S(1)}, u32[]{:S(2)}, u32[]{:S(2)}) async-start(bf16[16,80,384]{2,1,0:T(8,128)(2,1)} %get-tuple-element.43), calls=%async_computation.1 | async-start | bytes 1966080 | tf_op jit(solution)/shard_map/all_to_all | solution.py:387
  33.0 2.2 %collective-permute-done.3 = f32[32,128]{1,0:T(8,128)S(1)} collective-permute-done((f32[32,128]{1,0:T(8,128)S(1)}, f32[32,128]{1,0:T(8,128)S(1)}, u32[]{:S(2)}, u32[]{:S(2)}) %collective-permute-start.3) | collective-permute-done | bytes 16416 | tf_op jit(solution)/shard_map/ppermute | solution.py:391
  35.2 3.6 %collective-permute-start.4 = (f32[32,128]{1,0:T(8,128)S(1)}, f32[32,128]{1,0:T(8,128)S(1)}, u32[]{:S(2)}, u32[]{:S(2)}) collective-permute-start(f32[32,128]{1,0:T(8,128)S(1)} %add.46.one_ref), channel_id=1, source_target_pairs={{0,48},{48,0},{16,32},{32,16},{1,49},{49,1},{17,33},{33,17},{2,50}... | collective-permute-start | bytes 49160 | tf_op jit(solution)/shard_map/ppermute | solution.py:391
  38.9 1.3 collective-permute-done.4.other_ref
  40.2 4.8 %all-to-all-done.1.exit_ref = bf16[16,80,384]{2,1,0:T(8,128)(2,1)S(1)} async-done(((bf16[16,80,384]{2,1,0:T(8,128)(2,1)}), bf16[16,80,384]{2,1,0:T(8,128)(2,1)S(1)}, u32[]{:S(2)}, u32[]{:S(2)}) %all-to-all-start.1) | async-done | bytes 983072 | tf_op jit(solution)/shard_map/all_to_all | solution.py:387
  45.0 12.1 %all_to_all.40.tiles_ref = f32[16,32,128]{2,1,0:T(8,128)S(1)} all-to-all(f32[16,32,128]{2,1,0:T(8,128)S(1)} %shard_map.181), channel_id=1, replica_groups=mesh['dp_0'=4,'dp_1'=4,'dp_2'=4,'mp_0'=2,'mp_1'=2] {'dp_0','dp_2'}, dimensions={0} | all-to-all | bytes 524288 | tf_op jit(solution)/shard_map/all_to_all | solution.py:387
  57.1 1.4 shard_map.182
  58.5 3.5 %collective-permute-start.5 = (bf16[640,128]{1,0:T(8,128)(2,1)S(1)}, bf16[640,128]{1,0:T(8,128)(2,1)S(1)}, u32[]{:S(2)}, u32[]{:S(2)}) collective-permute-start(bf16[640,128]{1,0:T(8,128)(2,1)S(1)} %get-tuple-element.50), channel_id=1, source_target_pairs={{0,1},{1,0},{2,3},{3,2},{4,5},{5,4},{6,7},{7,6},{8,9},{9,8},{10,11... | collective-permute-start | bytes 491528 | tf_op jit(solution)/shard_map/ppermute | solution.py:377
  62.0 3.6 %all-to-all-start.3 = ((bf16[16,80,384]{2,1,0:T(8,128)(2,1)}), bf16[16,80,384]{2,1,0:T(8,128)(2,1)S(1)}, u32[]{:S(2)}, u32[]{:S(2)}) async-start(bf16[16,80,384]{2,1,0:T(8,128)(2,1)} %get-tuple-element.47), calls=%async_computation.3 | async-start | bytes 1966080 | tf_op jit(solution)/shard_map/all_to_all | solution.py:387
  66.5 5.0 %collective-permute-done.6 = bf16[640,128]{1,0:T(8,128)(2,1)S(1)} collective-permute-done((bf16[640,128]{1,0:T(8,128)(2,1)S(1)}, bf16[640,128]{1,0:T(8,128)(2,1)S(1)}, u32[]{:S(2)}, u32[]{:S(2)}) %collective-permute-start.6) | collective-permute-done | bytes 163872 | tf_op jit(solution)/shard_map/ppermute | solution.py:377
  73.6 8.6 %all-to-all-done.3.head_ref = bf16[16,80,384]{2,1,0:T(8,128)(2,1)S(1)} async-done(((bf16[16,80,384]{2,1,0:T(8,128)(2,1)}), bf16[16,80,384]{2,1,0:T(8,128)(2,1)S(1)}, u32[]{:S(2)}, u32[]{:S(2)}) %all-to-all-start.3) | async-done | bytes 983072 | tf_op jit(solution)/shard_map/all_to_all | solution.py:387
  82.2 1.9 %shard_map.183 = (bf16[640,128]{1,0:T(8,128)(2,1)S(1)}, bf16[640,128]{1,0:T(8,128)(2,1)S(1)}, bf16[16,80,384]{2,1,0:T(8,128)(2,1)S(1)}, f32[1288,128]{1,0:T(8,128)S(1)}) custom-call(bf16[16,80,384]{2,1,0:T(8,128)(2,1)S(1)} %all-to-all-done.1.exit_ref, bf16[16,80,384]{2,1,0:T(8,128)(2,1)S(1)} %all-to-all-done.3.head_ref, ...), custom_call_target="tpu_custom_call" | custom-call | tf_op jit(solution)/shard_map/pallas_call | solution.py:81
  85.9 1.4 collective-permute-start.8
  87.3 3.6 %all-to-all-start.4 = ((bf16[16,80,384]{2,1,0:T(8,128)(2,1)}), bf16[16,80,384]{2,1,0:T(8,128)(2,1)S(1)}, u32[]{:S(2)}, u32[]{:S(2)}) async-start(bf16[16,80,384]{2,1,0:T(8,128)(2,1)} %copy-done.1), calls=%async_computation.4 | async-start | bytes 1966080 | tf_op jit(solution)/shard_map/all_to_all | solution.py:387
  92.9 5.0 %collective-permute-done.9 = bf16[640,128]{1,0:T(8,128)(2,1)S(1)} collective-permute-done((bf16[640,128]{1,0:T(8,128)(2,1)S(1)}, bf16[640,128]{1,0:T(8,128)(2,1)S(1)}, u32[]{:S(2)}, u32[]{:S(2)}) %collective-permute-start.9) | collective-permute-done | bytes 163872 | tf_op jit(solution)/shard_map/ppermute | solution.py:377
  100.1 3.0 %shard_map.184 = (bf16[16,80,384]{2,1,0:T(8,128)(2,1)S(1)}, f32[16,32,128]{2,1,0:T(8,128)S(1)}) custom-call(bf16[16,80,384]{2,1,0:T(8,128)(2,1)S(1)} %all-to-all-done.1.exit_ref, bf16[16,80,384]{2,1,0:T(8,128)(2,1)S(1)} %all-to-all-done.3.head_ref, f32[16,32,128]{2,1,0:T(8,128)S(1)} %all_to_all.40.tiles_ref, ...), custom_call_target="tpu_custom_call" | custom-call | tf_op jit(solution)/shard_map/pallas_call | solution.py:81
  104.1 3.8 %all-to-all-done.4.head_ref = bf16[16,80,384]{2,1,0:T(8,128)(2,1)S(1)} async-done(((bf16[16,80,384]{2,1,0:T(8,128)(2,1)}), bf16[16,80,384]{2,1,0:T(8,128)(2,1)S(1)}, u32[]{:S(2)}, u32[]{:S(2)}) %all-to-all-start.4) | async-done | bytes 983072 | tf_op jit(solution)/shard_map/all_to_all | solution.py:387
  107.9 10.2 %all_to_all.41 = f32[16,32,128]{2,1,0:T(8,128)S(1)} all-to-all(f32[16,32,128]{2,1,0:T(8,128)S(1)} %get-tuple-element.57), channel_id=1, replica_groups=mesh['dp_0'=4,'dp_1'=4,'dp_2'=4,'mp_0'=2,'mp_1'=2] {'dp_0','dp_2'}, dimensions={0} | all-to-all | bytes 524288 | tf_op jit(solution)/shard_map/all_to_all | solution.py:387
  118.1 16.9 %all_to_all.42.exit_ref = bf16[16,80,384]{2,1,0:T(8,128)(2,1)S(1)} all-to-all(bf16[16,80,384]{2,1,0:T(8,128)(2,1)} %copy-done.2), channel_id=1, replica_groups=mesh['dp_0'=4,'dp_1'=4,'dp_2'=4,'mp_0'=2,'mp_1'=2] {'dp_0','dp_2'}, dimensions={0} | all-to-all | bytes 1966080 | tf_op jit(solution)/shard_map/all_to_all | solution.py:387
  135.2 3.8 %collective-permute-start.13 = (bf16[80,384]{1,0:T(8,128)(2,1)S(1)}, bf16[80,384]{1,0:T(8,128)(2,1)S(1)}, u32[]{:S(2)}, u32[]{:S(2)}) collective-permute-start(bf16[80,384]{1,0:T(8,128)(2,1)S(1)} %get-tuple-element.62), channel_id=1, source_target_pairs={{0,48},{48,0},{16,32},{32,16},{1,49},{49,1},{17,33},{33,17},{2,50}... | collective-permute-start | bytes 184328 | tf_op jit(solution)/shard_map/ppermute | solution.py:391
  140.4 2.3 %collective-permute-done.11 = f32[32,128]{1,0:T(8,128)S(1)} collective-permute-done((f32[32,128]{1,0:T(8,128)S(1)}, f32[32,128]{1,0:T(8,128)S(1)}, u32[]{:S(2)}, u32[]{:S(2)}) %collective-permute-start.11) | collective-permute-done | bytes 16416 | tf_op jit(solution)/shard_map/ppermute | solution.py:391
  144.0 3.4 %collective-permute-done.12.other_ref = f32[32,128]{1,0:T(8,128)S(1)} collective-permute-done((f32[32,128]{1,0:T(8,128)S(1)}, f32[32,128]{1,0:T(8,128)S(1)}, u32[]{:S(2)}, u32[]{:S(2)}) %collective-permute-start.12) | collective-permute-done | bytes 16416 | tf_op jit(solution)/shard_map/ppermute | solution.py:391
  148.1 4.0 %all-to-all-start.7 = ((f32[16,32,128]{2,1,0:T(8,128)}), f32[16,32,128]{2,1,0:T(8,128)S(1)}, u32[]{:S(2)}, u32[]{:S(2)}) async-start(f32[16,32,128]{2,1,0:T(8,128)} %shard_map.185), calls=%async_computation.7 | async-start | bytes 524288 | tf_op jit(solution)/shard_map/all_to_all | solution.py:387
  152.2 7.2 %all-to-all-done.7.tiles_ref = f32[16,32,128]{2,1,0:T(8,128)S(1)} async-done(((f32[16,32,128]{2,1,0:T(8,128)}), f32[16,32,128]{2,1,0:T(8,128)S(1)}, u32[]{:S(2)}, u32[]{:S(2)}) %all-to-all-start.7) | async-done | bytes 262176 | tf_op jit(solution)/shard_map/all_to_all | solution.py:387
  159.5 1.3 shard_map.187
  160.8 7.7 %collective-permute-start.15 = (f32[24,128]{1,0:T(8,128)S(1)}, f32[24,128]{1,0:T(8,128)S(1)}, u32[]{:S(2)}, u32[]{:S(2)}) collective-permute-start(f32[24,128]{1,0:T(8,128)S(1)} %get-tuple-element.63), channel_id=1, source_target_pairs={{0,1},{1,0},{2,3},{3,2},{4,5},{5,4},{6,7},{7,6},{8,9},{9,8},{10,11... | collective-permute-start | bytes 36872 | tf_op jit(solution)/shard_map/ppermute | solution.py:377
  169.8 2.1 %collective-permute-done.16.other_ref = f32[24,128]{1,0:T(8,128)S(1)} collective-permute-done((f32[24,128]{1,0:T(8,128)S(1)}, f32[24,128]{1,0:T(8,128)S(1)}, u32[]{:S(2)}, u32[]{:S(2)}) %collective-permute-start.16) | collective-permute-done | bytes 12320 | tf_op jit(solution)/shard_map/ppermute | solution.py:377
  (77 shorter events, 18.6 us)
Async XLA Ops:
  2.9 16.2 %collective-permute-start.2 = (bf16[64,384]{1,0:T(8,128)(2,1)}, bf16[64,384]{1,0:T(8,128)(2,1)S(1)}, u32[]{:S(2)}, u32[]{:S(2)}) collective-permute-start(bf16[64,384]{1,0:T(8,128)(2,1)} %get-tuple-element.41.own_ref), channel_id=1, source_target_pairs={{0,32},{32,0},{16,48},{48,16},{1,33},{33,1},{17,49},{49,17},{2,34}... | collective-permute-start | bytes 147464 | tf_op jit(solution)/shard_map/ppermute | solution.py:391
  10.7 8.4 %collective-permute-start.1 = (bf16[64,384]{1,0:T(8,128)(2,1)}, bf16[64,384]{1,0:T(8,128)(2,1)S(1)}, u32[]{:S(2)}, u32[]{:S(2)}) collective-permute-start(bf16[64,384]{1,0:T(8,128)(2,1)} %get-tuple-element.41.own_ref), channel_id=1, source_target_pairs={{0,48},{48,0},{16,32},{32,16},{1,49},{49,1},{17,33},{33,17},{2,50}... | collective-permute-start | bytes 147464 | tf_op jit(solution)/shard_map/ppermute | solution.py:391
  10.7 8.4 %collective-permute-start = (bf16[64,384]{1,0:T(8,128)(2,1)}, bf16[64,384]{1,0:T(8,128)(2,1)S(1)}, u32[]{:S(2)}, u32[]{:S(2)}) collective-permute-start(bf16[64,384]{1,0:T(8,128)(2,1)} %get-tuple-element.41.own_ref), channel_id=1, source_target_pairs={{0,16},{16,0},{32,48},{48,32},{1,17},{17,1},{33,49},{49,33},{2,18}... | collective-permute-start | bytes 147464 | tf_op jit(solution)/shard_map/ppermute | solution.py:391
  11.9 6.9 %copy-start.11 = (f32[8,512]{1,0:T(8,128)S(1)}, f32[8,512]{1,0:T(8,128)}, u32[]{:S(2)}) copy-start(f32[8,512]{1,0:T(8,128)} %param.12) | copy-start | bytes 49156
  11.9 14.2 %all-to-all-start = ((f32[16,32,128]{2,1,0:T(8,128)}), f32[16,32,128]{2,1,0:T(8,128)S(1)}, u32[]{:S(2)}, u32[]{:S(2)}) async-start(f32[16,32,128]{2,1,0:T(8,128)} %get-tuple-element.40), calls=%async_computation | async-start | bytes 524288 | tf_op jit(solution)/shard_map/all_to_all | solution.py:387
  18.8 7.3 %copy-start.8 = (bf16[64,384]{1,0:T(8,128)(2,1)S(1)}, bf16[64,384]{1,0:T(8,128)(2,1)}, u32[]{:S(2)}) copy-start(bf16[64,384]{1,0:T(8,128)(2,1)} %get-tuple-element.41.own_ref) | copy-start | bytes 147460
  27.6 3.8 %copy-start.13 = (f32[8,128]{1,0:T(8,128)S(1)}, f32[8,128]{1,0:T(8,128)}, u32[]{:S(2)}) copy-start(f32[8,128]{1,0:T(8,128)} %param.13) | copy-start | bytes 12292
  27.6 17.5 %all-to-all-start.1 = ((bf16[16,80,384]{2,1,0:T(8,128)(2,1)}), bf16[16,80,384]{2,1,0:T(8,128)(2,1)S(1)}, u32[]{:S(2)}, u32[]{:S(2)}) async-start(bf16[16,80,384]{2,1,0:T(8,128)(2,1)} %get-tuple-element.43), calls=%async_computation.1 | async-start | bytes 1966080 | tf_op jit(solution)/shard_map/all_to_all | solution.py:387
  31.6 3.6 %collective-permute-start.3 = (f32[32,128]{1,0:T(8,128)S(1)}, f32[32,128]{1,0:T(8,128)S(1)}, u32[]{:S(2)}, u32[]{:S(2)}) collective-permute-start(f32[32,128]{1,0:T(8,128)S(1)} %get-tuple-element.42), channel_id=1, source_target_pairs={{0,16},{16,0},{32,48},{48,32},{1,17},{17,1},{33,49},{49,33},{2,18}... | collective-permute-start | bytes 49160 | tf_op jit(solution)/shard_map/ppermute | solution.py:391
  35.2 5.0 %collective-permute-start.4 = (f32[32,128]{1,0:T(8,128)S(1)}, f32[32,128]{1,0:T(8,128)S(1)}, u32[]{:S(2)}, u32[]{:S(2)}) collective-permute-start(f32[32,128]{1,0:T(8,128)S(1)} %add.46.one_ref), channel_id=1, source_target_pairs={{0,48},{48,0},{16,32},{32,16},{1,49},{49,1},{17,33},{33,17},{2,50}... | collective-permute-start | bytes 49160 | tf_op jit(solution)/shard_map/ppermute | solution.py:391
  58.5 7.1 %collective-permute-start.5 = (bf16[640,128]{1,0:T(8,128)(2,1)S(1)}, bf16[640,128]{1,0:T(8,128)(2,1)S(1)}, u32[]{:S(2)}, u32[]{:S(2)}) collective-permute-start(bf16[640,128]{1,0:T(8,128)(2,1)S(1)} %get-tuple-element.50), channel_id=1, source_target_pairs={{0,1},{1,0},{2,3},{3,2},{4,5},{5,4},{6,7},{7,6},{8,9},{9,8},{10,11... | collective-permute-start | bytes 491528 | tf_op jit(solution)/shard_map/ppermute | solution.py:377
  62.0 20.1 %all-to-all-start.3 = ((bf16[16,80,384]{2,1,0:T(8,128)(2,1)}), bf16[16,80,384]{2,1,0:T(8,128)(2,1)S(1)}, u32[]{:S(2)}, u32[]{:S(2)}) async-start(bf16[16,80,384]{2,1,0:T(8,128)(2,1)} %get-tuple-element.47), calls=%async_computation.3 | async-start | bytes 1966080 | tf_op jit(solution)/shard_map/all_to_all | solution.py:387
  65.7 5.8 %collective-permute-start.6 = (bf16[640,128]{1,0:T(8,128)(2,1)S(1)}, bf16[640,128]{1,0:T(8,128)(2,1)S(1)}, u32[]{:S(2)}, u32[]{:S(2)}) collective-permute-start(bf16[640,128]{1,0:T(8,128)(2,1)S(1)} %add_convert_fusion.3), channel_id=1, source_target_pairs={{0,2},{2,0},{1,3},{3,1},{4,6},{6,4},{5,7},{7,5},{8,10},{10,8},{9,1... | collective-permute-start | bytes 491528 | tf_op jit(solution)/shard_map/ppermute | solution.py:377
  71.6 2.0 %collective-permute-start.7 = (bf16[640,128]{1,0:T(8,128)(2,1)S(1)}, bf16[640,128]{1,0:T(8,128)(2,1)S(1)}, u32[]{:S(2)}, u32[]{:S(2)}) collective-permute-start(bf16[640,128]{1,0:T(8,128)(2,1)S(1)} %add_convert_fusion.2.half_ref), channel_id=1, source_target_pairs={{0,1},{1,0},{2,3},{3,2},{4,5},{5,4},{6,7},{7,6},{8,9},{9,8},{10,11... | collective-permute-start | bytes 491528 | tf_op jit(solution)/shard_map/ppermute | solution.py:377
  85.9 5.1 %collective-permute-start.8 = (bf16[640,128]{1,0:T(8,128)(2,1)S(1)}, bf16[640,128]{1,0:T(8,128)(2,1)}, u32[]{:S(2)}, u32[]{:S(2)}) collective-permute-start(bf16[640,128]{1,0:T(8,128)(2,1)S(1)} %get-tuple-element.53), channel_id=1, source_target_pairs={{0,1},{1,0},{2,3},{3,2},{4,5},{5,4},{6,7},{7,6},{8,9},{9,8},{10,11... | collective-permute-start | bytes 491528 | tf_op jit(solution)/shard_map/ppermute | solution.py:377
  87.3 20.5 %all-to-all-start.4 = ((bf16[16,80,384]{2,1,0:T(8,128)(2,1)}), bf16[16,80,384]{2,1,0:T(8,128)(2,1)S(1)}, u32[]{:S(2)}, u32[]{:S(2)}) async-start(bf16[16,80,384]{2,1,0:T(8,128)(2,1)} %copy-done.1), calls=%async_computation.4 | async-start | bytes 1966080 | tf_op jit(solution)/shard_map/all_to_all | solution.py:387
  91.0 9.1 %copy-start.4 = (f32[1288,128]{1,0:T(8,128)S(1)}, f32[1288,128]{1,0:T(8,128)}, u32[]{:S(2)}) copy-start(f32[1288,128]{1,0:T(8,128)} %copy-done.3) | copy-start | bytes 1978372
  92.0 5.8 %collective-permute-start.9 = (bf16[640,128]{1,0:T(8,128)(2,1)S(1)}, bf16[640,128]{1,0:T(8,128)(2,1)S(1)}, u32[]{:S(2)}, u32[]{:S(2)}) collective-permute-start(bf16[640,128]{1,0:T(8,128)(2,1)S(1)} %add_convert_fusion.1), channel_id=1, source_target_pairs={{0,2},{2,0},{1,3},{3,1},{4,6},{6,4},{5,7},{7,5},{8,10},{10,8},{9,1... | collective-permute-start | bytes 491528 | tf_op jit(solution)/shard_map/ppermute | solution.py:377
  97.9 2.2 %collective-permute-start.10 = (bf16[640,128]{1,0:T(8,128)(2,1)S(1)}, bf16[640,128]{1,0:T(8,128)(2,1)S(1)}, u32[]{:S(2)}, u32[]{:S(2)}) collective-permute-start(bf16[640,128]{1,0:T(8,128)(2,1)S(1)} %add_convert_fusion.half_ref), channel_id=1, source_target_pairs={{0,1},{1,0},{2,3},{3,2},{4,5},{5,4},{6,7},{7,6},{8,9},{9,8},{10,11... | collective-permute-start | bytes 491528 | tf_op jit(solution)/shard_map/ppermute | solution.py:377
  135.2 7.5 %collective-permute-start.13 = (bf16[80,384]{1,0:T(8,128)(2,1)S(1)}, bf16[80,384]{1,0:T(8,128)(2,1)S(1)}, u32[]{:S(2)}, u32[]{:S(2)}) collective-permute-start(bf16[80,384]{1,0:T(8,128)(2,1)S(1)} %get-tuple-element.62), channel_id=1, source_target_pairs={{0,48},{48,0},{16,32},{32,16},{1,49},{49,1},{17,33},{33,17},{2,50}... | collective-permute-start | bytes 184328 | tf_op jit(solution)/shard_map/ppermute | solution.py:391
  139.1 3.6 %collective-permute-start.11 = (f32[32,128]{1,0:T(8,128)S(1)}, f32[32,128]{1,0:T(8,128)S(1)}, u32[]{:S(2)}, u32[]{:S(2)}) collective-permute-start(f32[32,128]{1,0:T(8,128)S(1)} %reduce_sum.29), channel_id=1, source_target_pairs={{0,16},{16,0},{32,48},{48,32},{1,17},{17,1},{33,49},{49,33},{2,18}... | collective-permute-start | bytes 49160 | tf_op jit(solution)/shard_map/ppermute | solution.py:391
  142.7 4.7 %collective-permute-start.12 = (f32[32,128]{1,0:T(8,128)S(1)}, f32[32,128]{1,0:T(8,128)S(1)}, u32[]{:S(2)}, u32[]{:S(2)}) collective-permute-start(f32[32,128]{1,0:T(8,128)S(1)} %add.55.one_ref), channel_id=1, source_target_pairs={{0,48},{48,0},{16,32},{32,16},{1,49},{49,1},{17,33},{33,17},{2,50}... | collective-permute-start | bytes 49160 | tf_op jit(solution)/shard_map/ppermute | solution.py:391
  142.7 16.7 %copy-start = (f32[64,16,20]{2,1,0:T(8,128)S(1)}, f32[64,16,20]{2,1,0:T(8,128)}, u32[]{:S(2)}) copy-start(f32[64,16,20]{2,1,0:T(8,128)} %constant.29.clone.table_ref) | copy-start | bytes 245764
  142.8 9.4 %collective-permute-start.14 = (bf16[40,384]{1,0:T(8,128)(2,1)S(1)}, bf16[40,384]{1,0:T(8,128)(2,1)S(1)}, u32[]{:S(2)}, u32[]{:S(2)}) collective-permute-start(bf16[40,384]{1,0:T(8,128)(2,1)S(1)} %slice.21), channel_id=1, source_target_pairs={{0,16},{16,0},{32,48},{48,32},{1,17},{17,1},{33,49},{49,33},{2,18}... | collective-permute-start | bytes 92168 | tf_op jit(solution)/shard_map/ppermute | solution.py:391
  148.1 11.3 %all-to-all-start.7 = ((f32[16,32,128]{2,1,0:T(8,128)}), f32[16,32,128]{2,1,0:T(8,128)S(1)}, u32[]{:S(2)}, u32[]{:S(2)}) async-start(f32[16,32,128]{2,1,0:T(8,128)} %shard_map.185), calls=%async_computation.7 | async-start | bytes 524288 | tf_op jit(solution)/shard_map/all_to_all | solution.py:387
  152.1 7.3 %copy-start.5 = (bf16[20,320]{1,0:T(8,128)(2,1)S(1)}, bf16[20,320]{1,0:T(8,128)(2,1)}, u32[]{:S(2)}) copy-start(bf16[20,320]{1,0:T(8,128)(2,1)} %wq_ref.3) | copy-start | bytes 38404
  152.1 7.3 %copy-start.6 = (bf16[20,320]{1,0:T(8,128)(2,1)S(1)}, bf16[20,320]{1,0:T(8,128)(2,1)}, u32[]{:S(2)}) copy-start(bf16[20,320]{1,0:T(8,128)(2,1)} %wk_ref.3) | copy-start | bytes 38404
  152.1 7.3 %copy-start.7 = (bf16[20,320]{1,0:T(8,128)(2,1)S(1)}, bf16[20,320]{1,0:T(8,128)(2,1)}, u32[]{:S(2)}) copy-start(bf16[20,320]{1,0:T(8,128)(2,1)} %wv_ref.3) | copy-start | bytes 38404
  152.1 7.3 %copy-start.9 = (bf16[32,20]{0,1:T(8,128)(2,1)S(1)}, bf16[32,20]{0,1:T(8,128)(2,1)}, u32[]{:S(2)}) copy-start(bf16[32,20]{0,1:T(8,128)(2,1)} %param.14) | copy-start | bytes 3844
  152.1 7.3 %copy-start.10 = (bf16[2,20]{1,0:T(2,128)(2,1)S(1)}, bf16[2,20]{1,0:T(2,128)(2,1)}, u32[]{:S(2)}) copy-start(bf16[2,20]{1,0:T(2,128)(2,1)} %gains_ref.3) | copy-start | bytes 244
  160.8 8.5 %collective-permute-start.15 = (f32[24,128]{1,0:T(8,128)S(1)}, f32[24,128]{1,0:T(8,128)S(1)}, u32[]{:S(2)}, u32[]{:S(2)}) collective-permute-start(f32[24,128]{1,0:T(8,128)S(1)} %get-tuple-element.63), channel_id=1, source_target_pairs={{0,1},{1,0},{2,3},{3,2},{4,5},{5,4},{6,7},{7,6},{8,9},{9,8},{10,11... | collective-permute-start | bytes 36872 | tf_op jit(solution)/shard_map/ppermute | solution.py:377
  169.3 2.5 %collective-permute-start.16 = (f32[24,128]{1,0:T(8,128)S(1)}, f32[24,128]{1,0:T(8,128)S(1)}, u32[]{:S(2)}, u32[]{:S(2)}) collective-permute-start(f32[24,128]{1,0:T(8,128)S(1)} %add.58.one_ref), channel_id=1, source_target_pairs={{0,2},{2,0},{1,3},{3,1},{4,6},{6,4},{5,7},{7,5},{8,10},{10,8},{9,1... | collective-permute-start | bytes 36872 | tf_op jit(solution)/shard_map/ppermute | solution.py:377
  (4 other events, 6.4 us)

commit v5 on v4

--- a/solution.py
+++ b/solution.py
@@ -30,6 +30,8 @@
 GROUP_ROWS = DEPTH * OWN
 SMALL = 8 * BLOCKS // GROUPS
 LINED = 32
+PACKED = 5 * GROUP_ROWS // 2
+GAIN_LANE = COLS + PATCH + PATCHES
 FIRST = [(0, 1), (1, 0), (2, 3), (3, 2)]
 SECOND = [(0, 3), (3, 0), (1, 2), (2, 1)]
 FOURTH = [(0, 2), (2, 0), (1, 3), (3, 1)]
@@ -77,10 +79,13 @@
     return np.concatenate([high, low], axis=2)
 
 
-def call(body, outs, *args, grant=GRANT):
+def call(body, outs, *args, grant=GRANT, far=(), scratch=()):
+    spaces = [pltpu.HBM if at in far else pltpu.VMEM for at in range(len(outs))]
     return pl.pallas_call(
         body,
         out_shape=[jax.ShapeDtypeStruct(s, d) for s, d in outs],
+        **({"out_specs": [pl.BlockSpec(memory_space=space) for space in spaces]} if far else {}),
+        scratch_shapes=scratch,
         compiler_params=pltpu.CompilerParams(vmem_limit_bytes=grant),
     )(*args)
 
@@ -106,13 +111,13 @@
                 lanes = rows[:, 128 * j : min(128 * j + 128, COLS)]
                 k, t = at // DEPTH, 8 * (at % DEPTH)
                 out_ref[k, t : t + 8, 0 : lanes.shape[1]] = lanes
-    pair_eye = lax.broadcasted_iota(jnp.int32, (2, 2), 0) == lax.broadcasted_iota(jnp.int32, (2, 2), 1)
+    second = lax.broadcasted_iota(jnp.int32, (2, 1), 0).astype(F32).astype(BF)
     block_ref[...] = jnp.zeros_like(block_ref)
     block_ref[0:OWN, 0:COLS] = exit_ref[...]
     block_ref[0:OWN, COLS : COLS + PATCH] = embed_ref[...]
     block_ref[0:OWN, COLS + PATCH : WIDE] = turned_ref[lax.axis_index(DP)]
+    block_ref[0:OWN, GAIN_LANE : GAIN_LANE + 1] = tn(gains_ref[...], second).astype(BF)
     block_ref[LINED : LINED + OWN, 0:COLS] = head_ref[...]
-    block_ref[LINED : LINED + OWN, COLS : COLS + 2] = tn(gains_ref[...], pair_eye.astype(F32).astype(BF)).astype(BF)
 
 
 def from_tiles(ref):
@@ -181,6 +186,16 @@
     spread_halves(nn(blocks(exit_ref), context), mine_ref, other_ref)
 
 
+def gain_column(exit_ref):
+    return blocks(exit_ref, slice(256, 384))[:, GAIN_LANE - 256 : GAIN_LANE - 255].astype(F32)
+
+
+def lower_upper(x):
+    grouped = x.reshape(GROUPS, GROUP_ROWS, TOKENS)
+    half = GROUP_ROWS // 2
+    return [part.reshape(WIDTH // 2, TOKENS) for part in (grouped[:, :half], grouped[:, half:])]
+
+
 def head_kernel(
     exit_ref,
     head_ref,
@@ -190,16 +205,24 @@
     target_ref,
     mine_ref,
     other_ref,
+    grad_out_ref,
+    residual_out_ref,
     grad_ref,
     residual_ref,
+    grad_sem,
+    residual_sem,
 ):
-    head = blocks(head_ref)
     residual = first_residual(exit_ref, basis_ref) + joined_halves(half_ref, rest_ref)
     residual_ref[0:WIDTH, :] = residual
     factor = lax.rsqrt(jnp.sum(residual * residual, axis=0, keepdims=True) / WIDTH + EPS)
-    scaled = residual * factor
-    normed = (scaled * head[:, COLS + 1 : COLS + 2].astype(F32)).astype(BF)
-    forecast = tn(head, normed)[0:COLS]
+    scaled = residual * factor * gain_column(exit_ref)
+    normed = scaled.astype(BF)
+    low, high = (part.astype(BF) for part in lower_upper(scaled))
+    wide = jnp.concatenate(
+        [head_ref[:, GROUP_ROWS * at : GROUP_ROWS * (at + 1), :].reshape(WIDTH, 128) for at in range(2)], axis=1
+    )
+    narrow = head_ref[:, 2 * GROUP_ROWS :, :].reshape(WIDTH // 2, 128)
+    forecast = jnp.concatenate([tn(wide, normed), tn(narrow, low)[0:64] + tn(narrow, high)[64:128]], axis=0)
     column = lax.broadcasted_iota(jnp.int32, (COLS, 1), 0).astype(F32)
     step = jnp.floor((column + 0.5) * 0.1)
     channel = column - CHANNELS * step
@@ -218,27 +241,39 @@
     sigmoid = jnp.where(inside >= 0.0, 1.0, tail) / (1.0 + tail)
     terms = jnp.where(mean_channel, error * error, share * error + RADIUS * softplus)
     residual_ref[WIDTH:, :] = jnp.broadcast_to(jnp.sum(terms, axis=0, keepdims=True), (8, TOKENS))
+    residual_copy = pltpu.make_async_copy(residual_ref, residual_out_ref, residual_sem)
+    residual_copy.start()
     slope = (jnp.where(mean_channel, -2.0 * error, sigmoid - share) * (1.0 / 128.0)).astype(BF)
-    slope = jnp.concatenate([slope, jnp.zeros((WIDE - COLS, TOKENS), BF)], axis=0)
-    back = nn(head, slope)
+    blank = jnp.zeros((64, TOKENS), BF)
+    below = jnp.concatenate([slope[256:], blank], axis=0)
+    above = jnp.concatenate([blank, slope[256:]], axis=0)
+    grad = nt(normed, slope[0:256]).astype(BF)
+    for at in range(2):
+        grad_ref[:, GROUP_ROWS * at : GROUP_ROWS * (at + 1), :] = grad[:, 128 * at : 128 * at + 128].reshape(
+            GROUPS, GROUP_ROWS, 128
+        )
+    grad = nt(low, below) + nt(high, above)
+    grad_ref[:, 2 * GROUP_ROWS :, :] = grad.reshape(GROUPS, GROUP_ROWS // 2, 128).astype(BF)
+    grad_copy = pltpu.make_async_copy(grad_ref, grad_out_ref, grad_sem)
+    grad_copy.start()
+    ends = [nn(narrow, part).reshape(GROUPS, GROUP_ROWS // 2, TOKENS) for part in (below, above)]
+    back = nn(wide, slope[0:256]) + jnp.concatenate(ends, axis=1).reshape(WIDTH, TOKENS)
     spread_halves(back, mine_ref, other_ref)
-    high, low = two(jnp.sum(back * scaled, axis=1, keepdims=True))
-    lane = lax.broadcasted_iota(jnp.int32, (1, WIDE), 1)
-    grad = nt(normed, slope)
-    grad = jnp.where(lane == COLS, high.astype(F32), jnp.where(lane == COLS + 1, low.astype(F32), grad))
-    grad_ref[...] = grad.astype(BF).reshape(GROUPS, GROUP_ROWS, WIDE)
+    residual_copy.wait()
+    grad_copy.wait()
 
 
 def backward_kernel(
     exit_ref,
-    head_ref,
     tiles_ref,
     basis_ref,
     half_ref,
     rest_ref,
     residual_ref,
+    grad_out_ref,
+    out_ref,
     grad_ref,
-    out_ref,
+    grad_sem,
 ):
     factor_zero, raw, queries, keys, values, all_probs, context = attention(exit_ref, tiles_ref, basis_ref)
     basis = basis_ref[0:BASIS, :]
@@ -246,13 +281,17 @@
     upstream = joined_halves(half_ref, rest_ref)
     residual = residual_ref[0:WIDTH, :]
     factor = lax.rsqrt(jnp.sum(residual * residual, axis=0, keepdims=True) / WIDTH + EPS)
-    weighted = blocks(head_ref, slice(256, 384))[:, COLS - 255 : COLS - 254].astype(F32) * upstream
+    weighted = gain_column(exit_ref) * upstream
     inner = jnp.sum(weighted * residual, axis=0, keepdims=True) / WIDTH
     low = (factor * weighted - residual * (factor * factor * factor * inner)).astype(BF)
-    grad = nt(low, jnp.concatenate([*context, patches, patches], axis=0))
+    grad = nt(low, jnp.concatenate([*context, patches, jnp.zeros_like(patches)], axis=0))
     lane = lax.broadcasted_iota(jnp.int32, (1, WIDE), 1)
-    grad = jnp.where(lane >= COLS + PATCH, grad - grad.astype(BF).astype(F32), grad)
+    gain_high, gain_low = two(jnp.sum(upstream * residual * factor, axis=1, keepdims=True))
+    grad = jnp.where(lane == COLS + PATCH, gain_high.astype(F32), grad)
+    grad = jnp.where(lane == COLS + PATCH + 1, gain_low.astype(F32), grad)
     grad_ref[...] = grad.astype(BF).reshape(GROUPS, GROUP_ROWS, WIDE)
+    grad_copy = pltpu.make_async_copy(grad_ref, grad_out_ref, grad_sem)
+    grad_copy.start()
     context_grad = tn(blocks(exit_ref), low)[0:COLS].astype(BF)
     backs = ([], [], [])
     for at, probs in zip(HEADS, all_probs):
@@ -280,6 +319,7 @@
     tiles += [jnp.zeros((8, 128), F32)] * (BLOCKS - len(tiles))
     for k in range(GROUPS):
         out_ref[k] = jnp.concatenate(tiles[DEPTH * k : DEPTH * k + DEPTH], axis=0)
+    grad_copy.wait()
 
 
 def group_sum(ref):
@@ -293,7 +333,10 @@
     total_ref[...] = group_sum(tiles_ref)
     parts = [ref[...].astype(F32) for ref in (own_ref, first_ref, second_ref, fourth_ref)]
     exits = jnp.concatenate([p[0:OWN] for p in parts], axis=0).astype(BF)
-    heads = jnp.concatenate([p[LINED : LINED + OWN] for p in parts], axis=0).astype(BF)
+    heads = jnp.concatenate([p[LINED : LINED + OWN] for p in parts], axis=0)
+    half = GROUP_ROWS // 2
+    narrow = jnp.concatenate([heads[:half, 256:320], heads[half:, 256:320]], axis=1)
+    heads = jnp.concatenate([heads[:, 0:128], heads[:, 128:256], narrow], axis=0).astype(BF)
     for k in range(GROUPS):
         exit_ref[k] = exits
         head_ref[k] = heads
@@ -307,6 +350,9 @@
 
 def scatter_kernel(exit_ref, head_ref, keep_ref, send_ref):
     exits, heads = group_sum(exit_ref), group_sum(head_ref)
+    narrow = heads[2 * GROUP_ROWS :]
+    narrow = jnp.concatenate([narrow, jnp.concatenate([narrow[:, 64:], narrow[:, :64]], axis=1)], axis=0)
+    heads = jnp.concatenate([heads[:GROUP_ROWS], heads[GROUP_ROWS : 2 * GROUP_ROWS], narrow], axis=1)
     rows = [x[OWN * at : OWN * at + OWN] for at in range(DEPTH) for x in (exits, heads)]
     keep_ref[...] = jnp.concatenate(rows[:DEPTH], axis=0)
     send_ref[...] = jnp.concatenate(rows[DEPTH:], axis=0).astype(BF)
@@ -327,12 +373,9 @@
     wq_ref,
     wk_ref,
     wv_ref,
-    sums_ref,
     q_ref,
     k_ref,
     v_ref,
-    exit_grad_ref,
-    head_grad_ref,
     rest_ref,
 ):
     basis = own_basis(embed_ref, table_ref)
@@ -354,23 +397,23 @@
 
     mixed = jnp.concatenate([small(TILES + i) for i in range(BASIS // 8)], axis=0)[:, 0:PATCH]
     embed = embed - exact(((0,), (0,)))(basis, mixed)
+    rest_ref[...] = jnp.zeros_like(rest_ref)
+    rest_ref[0:OWN, 0:PATCH] = embed
+    rest_ref[0:OWN, PATCH : PATCH + 1] = gain_zero
+    rest_ref[0:1, PATCH + 2 : PATCH + 3] = jnp.sum(small(TILES + BASIS // 8)[0:1, :], axis=1, keepdims=True)
+
+
+def end_kernel(one_ref, other_ref, sums_ref, embed_ref, gains_ref, loss_ref, exit_grad_ref, head_grad_ref):
     exit_ref, head_ref = sums_ref[0:OWN, :], sums_ref[OWN : 2 * OWN, :]
-    ends = exit_ref[:, COLS : COLS + PATCH] + exit_ref[:, COLS + PATCH : WIDE]
-    gain_one = head_ref[:, COLS : COLS + 1] + head_ref[:, COLS + 1 : COLS + 2]
     exit_grad_ref[...] = exit_ref[:, 0:COLS]
     head_grad_ref[...] = head_ref[:, 0:COLS]
-    rest_ref[...] = jnp.zeros_like(rest_ref)
-    rest_ref[0:OWN, 0:PATCH] = embed + 0.25 * ends
-    rest_ref[0:OWN, PATCH : PATCH + 1] = gain_zero
-    rest_ref[0:OWN, PATCH + 1 : PATCH + 2] = gain_one
-    rest_ref[0:1, PATCH + 2 : PATCH + 3] = jnp.sum(small(TILES + BASIS // 8)[0:1, :], axis=1, keepdims=True)
-
-
-def end_kernel(one_ref, other_ref, embed_ref, gains_ref, loss_ref):
     rest = one_ref[...] + other_ref[...]
-    embed_ref[...] = rest[0:OWN, 0:PATCH]
-    gains_ref[...] = rest.T[PATCH : PATCH + 2, 0:OWN]
+    embed_ref[...] = rest[0:OWN, 0:PATCH] + exit_ref[:, COLS : COLS + PATCH]
     loss_ref[...] = rest[0:1, PATCH + 2 : PATCH + 3] / 1048576.0
+    gain_one = exit_ref[:, COLS + PATCH : COLS + PATCH + 1] + exit_ref[:, COLS + PATCH + 1 : COLS + PATCH + 2]
+    gain_one = jnp.concatenate([gain_one, jnp.zeros((24 - OWN, 1), F32)], axis=0)
+    lane = lax.broadcasted_iota(jnp.int32, rest.shape, 1)
+    gains_ref[...] = jnp.where(lane == PATCH + 1, gain_one, rest).T[PATCH : PATCH + 2, 0:OWN]
 
 
 def swapped(x, axis):
@@ -434,8 +477,9 @@
     )
     tiles = over(tiles, XY)
     column = [along_z(block, pairs) for pairs in (FIRST, SECOND, FOURTH)]
+    packed = ((GROUPS, PACKED, 128), BF)
     total, exit_all, head_all = call(
-        gather_kernel, [((SMALL, 128), F32), groups, groups], tiles, block, *column
+        gather_kernel, [((SMALL, 128), F32), groups, packed], tiles, block, *column
     )
     exit_all = over(exit_all, XY)
     tiles = z_total(total)
@@ -443,7 +487,8 @@
     patches, target = prepare(history, later)
     number = np.arange(TOKENS) % PATCHES
     place_hot = jnp.asarray((np.arange(PATCHES)[:, None] == number[None, :]), dtype=BF)
-    basis = jnp.concatenate([patches, place_hot, place_hot], axis=0)
+    low_hot = jnp.asarray((np.arange(PATCHES)[:, None] == number[None, :]) & (number[None, :] > 0), dtype=BF)
+    basis = jnp.concatenate([patches, place_hot, low_hot], axis=0)
     tiles, exit_all, basis, target = lax.optimization_barrier((tiles, exit_all, basis, target))
     tiles = over(tiles, XY)
     head_all = over(after(head_all, tiles), XY)
@@ -453,13 +498,20 @@
     mine, other = mp_sum(mine, other)
     mine, other, head_grad, residual = call(
         head_kernel,
-        [half, half, groups, ((WIDTH + 8, TOKENS), F32)],
+        [half, half, packed, ((WIDTH + 8, TOKENS), F32)],
         exit_all,
         head_all,
         basis,
         mine,
         other,
         target,
+        far=(2, 3),
+        scratch=[
+            pltpu.VMEM(*packed),
+            pltpu.VMEM((WIDTH + 8, TOKENS), F32),
+            pltpu.SemaphoreType.DMA,
+            pltpu.SemaphoreType.DMA,
+        ],
     )
     head_grad = over(head_grad, XY)
     mine, other = mp_sum(mine, other)
@@ -467,12 +519,13 @@
         backward_kernel,
         [groups, tiles_like],
         exit_all,
-        head_all,
         tiles,
         basis,
         mine,
         other,
         residual,
+        far=(0,),
+        scratch=[pltpu.VMEM(*groups), pltpu.SemaphoreType.DMA],
     )
     totals = over(after(totals, head_grad), XY)
     exit_grad = over(after(exit_grad, totals), XY)
@@ -483,9 +536,9 @@
     keep = keep + along_z(send, SECOND).astype(F32)
     sums = keep[: 2 * OWN] + along_z(keep[2 * OWN :].astype(BF), FIRST).astype(F32)
     own = ((OWN, COLS), F32)
-    query_grad, key_grad, value_grad, output_grad, head_weight_grad, rest = call(
+    query_grad, key_grad, value_grad, rest = call(
         last_kernel,
-        [own, own, own, own, own, ((24, 128), F32)],
+        [own, own, own, ((24, 128), F32)],
         totals,
         embed_turned,
         gains,
@@ -493,14 +546,14 @@
         asking,
         lookup,
         content,
-        sums,
     )
     rest = rest + swapped(rest, "mp_1")
-    embed_grad, gains_grad, loss_mean = call(
+    embed_grad, gains_grad, loss_mean, output_grad, head_weight_grad = call(
         end_kernel,
-        [((OWN, PATCH), F32), ((2, OWN), F32), ((1, 1), F32)],
+        [((OWN, PATCH), F32), ((2, OWN), F32), ((1, 1), F32), own, own],
         rest,
         swapped(rest, "mp_0"),
+        sums,
     )
     return (
         loss_mean[0, 0],

time: 173 us -> 169 us (0.977)
  waiting for transfers between devices: 55.6 us -> 51.9 us
  local copies, waits for them, and re-layouts: 3.05 us -> 1.15 us
    all_to_all x5, waiting for transfers between devices: 31.4 us -> 26.8 us  [over(): return lax.all_to_all(x, axis, 0, 0, tiled=True)]
    unnamed x28 -> x26, local copies, waits for them, and re-layouts: 2.82 us -> 0.91 us
  transfers between devices with their start and end apart: 22 -> 22, of which waited for: 15 -> 15; matrix products, arithmetic and copies ran while one was open for 1% -> 1% of each run, Pallas kernels for 2% -> 3%
where the time goes in v5:
time: 169 us; the launch traced here: 168 us
  starting transfers between devices  58.1 us (34%)
  waiting for transfers between devices  51.9 us (31%)
  blocking collectives  40.9 us (24%)
  Pallas kernels  14.3 us (8%)
    all_to_all x3, blocking collectives, over(): return lax.all_to_all(x, axis, 0, 0, tiled=True)  40.9 us
    all_to_all x5, waiting for transfers between devices, over(): return lax.all_to_all(x, axis, 0, 0, tiled=True)  26.8 us
    all_to_all x5, starting transfers between devices, over(): return lax.all_to_all(x, axis, 0, 0, tiled=True)  21.4 us
    ppermute x9, starting transfers between devices, along_z(): return lax.ppermute(x, Z, pairs)  20.4 us
    ppermute x8, starting transfers between devices, swapped(): return lax.ppermute(x, axis, [(0, 1), (1, 0)])  16.3 us
    ppermute x8, waiting for transfers between devices, swapped(): return lax.ppermute(x, axis, [(0, 1), (1, 0)])  14.7 us
    pallas_call x10, Pallas kernels, call(): pl.pallas_call(body, out_shape=[jax.ShapeDtypeStruct(s, d) for s, d in ou...  14.3 us
    ppermute x9, waiting for transfers between devices, along_z(): return lax.ppermute(x, Z, pairs)  10.5 us
  transfers between devices with their start and end apart: 22, of which 15 were waited for; matrix products, arithmetic and copies ran while one was open for 1% of the time, Pallas kernels for 3%

profile of v5, /device:TPU:1, one launch (start us, length us, event | category | flops | bytes accessed | tf_op | source)
XLA Modules:
  0.0 168.1 jit_solution(2571505750302838138)
XLA Ops:
  0.6 2.3 %shard_map.188 = (f32[16,32,128]{2,1,0:T(8,128)}, bf16[64,384]{1,0:T(8,128)(2,1)}) custom-call(bf16[20,32]{1,0:T(8,128)(2,1)} %bitcast.10, bf16[2,20]{1,0:T(2,128)(2,1)} %gains_ref.3, f32[64,16,20]{2,1,0:T(8,128)} %constant.31.clone.table_ref, bf16[64,20,32]{2,1,0:T(8,128)(2,1)} %constant.32.clone.turned_ref, bf16[20,320]{1,0:T(8,128)(2,1)} %wq_ref.3, ...), custom_call_target="tpu_custom_call" | custom-call | tf_op jit(solution)/shard_map/pallas_call | solution.py:84
  2.9 7.7 %collective-permute-start.2 = (bf16[64,384]{1,0:T(8,128)(2,1)}, bf16[64,384]{1,0:T(8,128)(2,1)S(1)}, u32[]{:S(2)}, u32[]{:S(2)}) collective-permute-start(bf16[64,384]{1,0:T(8,128)(2,1)} %get-tuple-element.41.own_ref), channel_id=1, source_target_pairs={{0,32},{32,0},{16,48},{48,16},{1,33},{33,1},{17,49},{49,17},{2,34}... | collective-permute-start | bytes 147464 | tf_op jit(solution)/shard_map/ppermute | solution.py:434
  11.9 6.9 %all-to-all-start = ((f32[16,32,128]{2,1,0:T(8,128)}), f32[16,32,128]{2,1,0:T(8,128)S(1)}, u32[]{:S(2)}, u32[]{:S(2)}) async-start(f32[16,32,128]{2,1,0:T(8,128)} %get-tuple-element.40), calls=%async_computation | async-start | bytes 524288 | tf_op jit(solution)/shard_map/all_to_all | solution.py:430
  19.1 7.0 %all-to-all-done.tiles_ref = f32[16,32,128]{2,1,0:T(8,128)S(1)} async-done(((f32[16,32,128]{2,1,0:T(8,128)}), f32[16,32,128]{2,1,0:T(8,128)S(1)}, u32[]{:S(2)}, u32[]{:S(2)}) %all-to-all-start) | async-done | bytes 262176 | tf_op jit(solution)/shard_map/all_to_all | solution.py:430
  26.1 1.3 shard_map.189
  27.4 3.8 %all-to-all-start.1 = ((bf16[16,80,384]{2,1,0:T(8,128)(2,1)}), bf16[16,80,384]{2,1,0:T(8,128)(2,1)S(1)}, u32[]{:S(2)}, u32[]{:S(2)}) async-start(bf16[16,80,384]{2,1,0:T(8,128)(2,1)} %get-tuple-element.43), calls=%async_computation.1 | async-start | bytes 1966080 | tf_op jit(solution)/shard_map/all_to_all | solution.py:430
  32.8 2.2 %collective-permute-done.3 = f32[32,128]{1,0:T(8,128)S(1)} collective-permute-done((f32[32,128]{1,0:T(8,128)S(1)}, f32[32,128]{1,0:T(8,128)S(1)}, u32[]{:S(2)}, u32[]{:S(2)}) %collective-permute-start.3) | collective-permute-done | bytes 16416 | tf_op jit(solution)/shard_map/ppermute | solution.py:434
  35.1 3.7 %collective-permute-start.4 = (f32[32,128]{1,0:T(8,128)S(1)}, f32[32,128]{1,0:T(8,128)S(1)}, u32[]{:S(2)}, u32[]{:S(2)}) collective-permute-start(f32[32,128]{1,0:T(8,128)S(1)} %add.46.one_ref), channel_id=1, source_target_pairs={{0,48},{48,0},{16,32},{32,16},{1,49},{49,1},{17,33},{33,17},{2,50}... | collective-permute-start | bytes 49160 | tf_op jit(solution)/shard_map/ppermute | solution.py:434
  40.1 4.8 %all-to-all-done.1.exit_ref = bf16[16,80,384]{2,1,0:T(8,128)(2,1)S(1)} async-done(((bf16[16,80,384]{2,1,0:T(8,128)(2,1)}), bf16[16,80,384]{2,1,0:T(8,128)(2,1)S(1)}, u32[]{:S(2)}, u32[]{:S(2)}) %all-to-all-start.1) | async-done | bytes 983072 | tf_op jit(solution)/shard_map/all_to_all | solution.py:430
  44.9 12.1 %all_to_all.40.tiles_ref = f32[16,32,128]{2,1,0:T(8,128)S(1)} all-to-all(f32[16,32,128]{2,1,0:T(8,128)S(1)} %shard_map.190), channel_id=1, replica_groups=mesh['dp_0'=4,'dp_1'=4,'dp_2'=4,'mp_0'=2,'mp_1'=2] {'dp_0','dp_2'}, dimensions={0} | all-to-all | bytes 524288 | tf_op jit(solution)/shard_map/all_to_all | solution.py:430
  57.0 1.4 shard_map.191
  58.4 3.5 %collective-permute-start.5 = (bf16[640,128]{1,0:T(8,128)(2,1)S(1)}, bf16[640,128]{1,0:T(8,128)(2,1)S(1)}, u32[]{:S(2)}, u32[]{:S(2)}) collective-permute-start(bf16[640,128]{1,0:T(8,128)(2,1)S(1)} %get-tuple-element.50), channel_id=1, source_target_pairs={{0,1},{1,0},{2,3},{3,2},{4,5},{5,4},{6,7},{7,6},{8,9},{9,8},{10,11... | collective-permute-start | bytes 491528 | tf_op jit(solution)/shard_map/ppermute | solution.py:420
  61.9 3.6 %all-to-all-start.3 = ((bf16[16,200,128]{2,1,0:T(8,128)(2,1)}), bf16[16,200,128]{2,1,0:T(8,128)(2,1)S(1)}, u32[]{:S(2)}, u32[]{:S(2)}) async-start(bf16[16,200,128]{2,1,0:T(8,128)(2,1)} %get-tuple-element.48), calls=%async_computation.3 | async-start | bytes 1638400 | tf_op jit(solution)/shard_map/all_to_all | solution.py:430
  66.4 4.9 %collective-permute-done.6 = bf16[640,128]{1,0:T(8,128)(2,1)S(1)} collective-permute-done((bf16[640,128]{1,0:T(8,128)(2,1)S(1)}, bf16[640,128]{1,0:T(8,128)(2,1)S(1)}, u32[]{:S(2)}, u32[]{:S(2)}) %collective-permute-start.6) | collective-permute-done | bytes 163872 | tf_op jit(solution)/shard_map/ppermute | solution.py:420
  73.4 6.3 %all-to-all-done.3.head_ref = bf16[16,200,128]{2,1,0:T(8,128)(2,1)S(1)} async-done(((bf16[16,200,128]{2,1,0:T(8,128)(2,1)}), bf16[16,200,128]{2,1,0:T(8,128)(2,1)S(1)}, u32[]{:S(2)}, u32[]{:S(2)}) %all-to-all-start.3) | async-done | bytes 819232 | tf_op jit(solution)/shard_map/all_to_all | solution.py:430
  79.8 2.6 %shard_map.192 = (bf16[640,128]{1,0:T(8,128)(2,1)S(1)}, bf16[640,128]{1,0:T(8,128)(2,1)S(1)}, bf16[16,200,128]{2,1,0:T(8,128)(2,1)}, f32[1288,128]{1,0:T(8,128)S(1)}) custom-call(bf16[16,80,384]{2,1,0:T(8,128)(2,1)S(1)} %all-to-all-done.1.exit_ref, bf16[16,200,128]{2,1,0:T(8,128)(2,1)S(1)} %all-to-all-done.3.head_ref, ...), custom_call_target="tpu_custom_call" | custom-call | tf_op jit(solution)/shard_map/pallas_call | solution.py:84
  83.2 1.6 collective-permute-start.8
  84.9 3.6 %all-to-all-start.4 = ((bf16[16,200,128]{2,1,0:T(8,128)(2,1)}), bf16[16,200,128]{2,1,0:T(8,128)(2,1)S(1)}, u32[]{:S(2)}, u32[]{:S(2)}) async-start(bf16[16,200,128]{2,1,0:T(8,128)(2,1)} %get-tuple-element.56), calls=%async_computation.4 | async-start | bytes 1638400 | tf_op jit(solution)/shard_map/all_to_all | solution.py:430
  89.4 5.0 %collective-permute-done.9 = bf16[640,128]{1,0:T(8,128)(2,1)S(1)} collective-permute-done((bf16[640,128]{1,0:T(8,128)(2,1)S(1)}, bf16[640,128]{1,0:T(8,128)(2,1)S(1)}, u32[]{:S(2)}, u32[]{:S(2)}) %collective-permute-start.9) | collective-permute-done | bytes 163872 | tf_op jit(solution)/shard_map/ppermute | solution.py:420
  96.6 3.7 %shard_map.193 = (bf16[16,80,384]{2,1,0:T(8,128)(2,1)S(1)}, f32[16,32,128]{2,1,0:T(8,128)S(1)}) custom-call(bf16[16,80,384]{2,1,0:T(8,128)(2,1)S(1)} %all-to-all-done.1.exit_ref, f32[16,32,128]{2,1,0:T(8,128)S(1)} %all_to_all.40.tiles_ref, bf16[64,128]{1,0:T(8,128)(2,1)S(1)} %pad_maximum_fusion.1.basis_ref, bf16[640,128]{1,0:T(8,128)(2,1)S(1)} %add_convert_fusion.half_ref, ...), custom_call_target="tpu_custom_call" | custom-call | tf_op jit(solution)/shard_map/pallas_call | solution.py:84
  100.3 2.8 %all-to-all-done.4.head_ref = bf16[16,200,128]{2,1,0:T(8,128)(2,1)S(1)} async-done(((bf16[16,200,128]{2,1,0:T(8,128)(2,1)}), bf16[16,200,128]{2,1,0:T(8,128)(2,1)S(1)}, u32[]{:S(2)}, u32[]{:S(2)}) %all-to-all-start.4) | async-done | bytes 819232 | tf_op jit(solution)/shard_map/all_to_all | solution.py:430
  103.1 11.0 %all_to_all.41 = f32[16,32,128]{2,1,0:T(8,128)S(1)} all-to-all(f32[16,32,128]{2,1,0:T(8,128)S(1)} %get-tuple-element.57), channel_id=1, replica_groups=mesh['dp_0'=4,'dp_1'=4,'dp_2'=4,'mp_0'=2,'mp_1'=2] {'dp_0','dp_2'}, dimensions={0} | all-to-all | bytes 524288 | tf_op jit(solution)/shard_map/all_to_all | solution.py:430
  114.1 17.8 %all_to_all.42.exit_ref = bf16[16,80,384]{2,1,0:T(8,128)(2,1)S(1)} all-to-all(bf16[16,80,384]{2,1,0:T(8,128)(2,1)S(1)} %get-tuple-element.59), channel_id=1, replica_groups=mesh['dp_0'=4,'dp_1'=4,'dp_2'=4,'mp_0'=2,'mp_1'=2] {'dp_0','dp_2'}, dimensions={0} | all-to-all | bytes 1966080 | tf_op jit(solution)/shard_map/all_to_all | solution.py:430
  132.2 3.9 %collective-permute-start.15 = (bf16[80,384]{1,0:T(8,128)(2,1)S(1)}, bf16[80,384]{1,0:T(8,128)(2,1)S(1)}, u32[]{:S(2)}, u32[]{:S(2)}) collective-permute-start(bf16[80,384]{1,0:T(8,128)(2,1)S(1)} %get-tuple-element.63), channel_id=1, source_target_pairs={{0,48},{48,0},{16,32},{32,16},{1,49},{49,1},{17,33},{33,17},{2,50}... | collective-permute-start | bytes 184328 | tf_op jit(solution)/shard_map/ppermute | solution.py:434
  136.1 1.3 collective-permute-start.11
  137.4 2.3 %collective-permute-done.11 = f32[32,128]{1,0:T(8,128)S(1)} collective-permute-done((f32[32,128]{1,0:T(8,128)S(1)}, f32[32,128]{1,0:T(8,128)S(1)}, u32[]{:S(2)}, u32[]{:S(2)}) %collective-permute-start.11) | collective-permute-done | bytes 16416 | tf_op jit(solution)/shard_map/ppermute | solution.py:434
  139.7 4.7 %collective-permute-done.12.other_ref = f32[32,128]{1,0:T(8,128)S(1)} collective-permute-done((f32[32,128]{1,0:T(8,128)S(1)}, f32[32,128]{1,0:T(8,128)S(1)}, u32[]{:S(2)}, u32[]{:S(2)}) %collective-permute-start.12) | collective-permute-done | bytes 16416 | tf_op jit(solution)/shard_map/ppermute | solution.py:434
  145.1 3.5 %all-to-all-start.7 = ((f32[16,32,128]{2,1,0:T(8,128)}), f32[16,32,128]{2,1,0:T(8,128)S(1)}, u32[]{:S(2)}, u32[]{:S(2)}) async-start(f32[16,32,128]{2,1,0:T(8,128)} %shard_map.194), calls=%async_computation.7 | async-start | bytes 524288 | tf_op jit(solution)/shard_map/all_to_all | solution.py:430
  148.8 1.3 collective-permute-start.16
  150.1 5.9 %all-to-all-done.7.tiles_ref = f32[16,32,128]{2,1,0:T(8,128)S(1)} async-done(((f32[16,32,128]{2,1,0:T(8,128)}), f32[16,32,128]{2,1,0:T(8,128)S(1)}, u32[]{:S(2)}, u32[]{:S(2)}) %all-to-all-start.7) | async-done | bytes 262176 | tf_op jit(solution)/shard_map/all_to_all | solution.py:430
  157.2 6.7 %collective-permute-start.13 = (f32[24,128]{1,0:T(8,128)S(1)}, f32[24,128]{1,0:T(8,128)S(1)}, u32[]{:S(2)}, u32[]{:S(2)}) collective-permute-start(f32[24,128]{1,0:T(8,128)S(1)} %get-tuple-element.61), channel_id=1, source_target_pairs={{0,1},{1,0},{2,3},{3,2},{4,5},{5,4},{6,7},{7,6},{8,9},{9,8},{10,11... | collective-permute-start | bytes 36872 | tf_op jit(solution)/shard_map/ppermute | solution.py:420
  165.5 1.8 %collective-permute-done.14.other_ref = f32[24,128]{1,0:T(8,128)S(1)} collective-permute-done((f32[24,128]{1,0:T(8,128)S(1)}, f32[24,128]{1,0:T(8,128)S(1)}, u32[]{:S(2)}, u32[]{:S(2)}) %collective-permute-start.14) | collective-permute-done | bytes 12320 | tf_op jit(solution)/shard_map/ppermute | solution.py:420
  (75 shorter events, 16.1 us)
Async XLA Ops:
  2.9 16.2 %collective-permute-start.2 = (bf16[64,384]{1,0:T(8,128)(2,1)}, bf16[64,384]{1,0:T(8,128)(2,1)S(1)}, u32[]{:S(2)}, u32[]{:S(2)}) collective-permute-start(bf16[64,384]{1,0:T(8,128)(2,1)} %get-tuple-element.41.own_ref), channel_id=1, source_target_pairs={{0,32},{32,0},{16,48},{48,16},{1,33},{33,1},{17,49},{49,17},{2,34}... | collective-permute-start | bytes 147464 | tf_op jit(solution)/shard_map/ppermute | solution.py:434
  10.7 8.4 %collective-permute-start.1 = (bf16[64,384]{1,0:T(8,128)(2,1)}, bf16[64,384]{1,0:T(8,128)(2,1)S(1)}, u32[]{:S(2)}, u32[]{:S(2)}) collective-permute-start(bf16[64,384]{1,0:T(8,128)(2,1)} %get-tuple-element.41.own_ref), channel_id=1, source_target_pairs={{0,48},{48,0},{16,32},{32,16},{1,49},{49,1},{17,33},{33,17},{2,50}... | collective-permute-start | bytes 147464 | tf_op jit(solution)/shard_map/ppermute | solution.py:434
  10.7 8.4 %collective-permute-start = (bf16[64,384]{1,0:T(8,128)(2,1)}, bf16[64,384]{1,0:T(8,128)(2,1)S(1)}, u32[]{:S(2)}, u32[]{:S(2)}) collective-permute-start(bf16[64,384]{1,0:T(8,128)(2,1)} %get-tuple-element.41.own_ref), channel_id=1, source_target_pairs={{0,16},{16,0},{32,48},{48,32},{1,17},{17,1},{33,49},{49,33},{2,18}... | collective-permute-start | bytes 147464 | tf_op jit(solution)/shard_map/ppermute | solution.py:434
  11.8 6.9 %copy-start.9 = (f32[8,512]{1,0:T(8,128)S(1)}, f32[8,512]{1,0:T(8,128)}, u32[]{:S(2)}) copy-start(f32[8,512]{1,0:T(8,128)} %param.13) | copy-start | bytes 49156
  11.9 14.2 %all-to-all-start = ((f32[16,32,128]{2,1,0:T(8,128)}), f32[16,32,128]{2,1,0:T(8,128)S(1)}, u32[]{:S(2)}, u32[]{:S(2)}) async-start(f32[16,32,128]{2,1,0:T(8,128)} %get-tuple-element.40), calls=%async_computation | async-start | bytes 524288 | tf_op jit(solution)/shard_map/all_to_all | solution.py:430
  18.8 7.3 %copy-start.6 = (bf16[64,384]{1,0:T(8,128)(2,1)S(1)}, bf16[64,384]{1,0:T(8,128)(2,1)}, u32[]{:S(2)}) copy-start(bf16[64,384]{1,0:T(8,128)(2,1)} %get-tuple-element.41.own_ref) | copy-start | bytes 147460
  27.4 3.8 %copy-start.10 = (f32[8,128]{1,0:T(8,128)S(1)}, f32[8,128]{1,0:T(8,128)}, u32[]{:S(2)}) copy-start(f32[8,128]{1,0:T(8,128)} %param.14) | copy-start | bytes 12292
  27.4 17.5 %all-to-all-start.1 = ((bf16[16,80,384]{2,1,0:T(8,128)(2,1)}), bf16[16,80,384]{2,1,0:T(8,128)(2,1)S(1)}, u32[]{:S(2)}, u32[]{:S(2)}) async-start(bf16[16,80,384]{2,1,0:T(8,128)(2,1)} %get-tuple-element.43), calls=%async_computation.1 | async-start | bytes 1966080 | tf_op jit(solution)/shard_map/all_to_all | solution.py:430
  31.5 3.6 %collective-permute-start.3 = (f32[32,128]{1,0:T(8,128)S(1)}, f32[32,128]{1,0:T(8,128)S(1)}, u32[]{:S(2)}, u32[]{:S(2)}) collective-permute-start(f32[32,128]{1,0:T(8,128)S(1)} %get-tuple-element.42), channel_id=1, source_target_pairs={{0,16},{16,0},{32,48},{48,32},{1,17},{17,1},{33,49},{49,33},{2,18}... | collective-permute-start | bytes 49160 | tf_op jit(solution)/shard_map/ppermute | solution.py:434
  35.1 5.0 %collective-permute-start.4 = (f32[32,128]{1,0:T(8,128)S(1)}, f32[32,128]{1,0:T(8,128)S(1)}, u32[]{:S(2)}, u32[]{:S(2)}) collective-permute-start(f32[32,128]{1,0:T(8,128)S(1)} %add.46.one_ref), channel_id=1, source_target_pairs={{0,48},{48,0},{16,32},{32,16},{1,49},{49,1},{17,33},{33,17},{2,50}... | collective-permute-start | bytes 49160 | tf_op jit(solution)/shard_map/ppermute | solution.py:434
  58.4 7.1 %collective-permute-start.5 = (bf16[640,128]{1,0:T(8,128)(2,1)S(1)}, bf16[640,128]{1,0:T(8,128)(2,1)S(1)}, u32[]{:S(2)}, u32[]{:S(2)}) collective-permute-start(bf16[640,128]{1,0:T(8,128)(2,1)S(1)} %get-tuple-element.50), channel_id=1, source_target_pairs={{0,1},{1,0},{2,3},{3,2},{4,5},{5,4},{6,7},{7,6},{8,9},{9,8},{10,11... | collective-permute-start | bytes 491528 | tf_op jit(solution)/shard_map/ppermute | solution.py:420
  61.9 17.9 %all-to-all-start.3 = ((bf16[16,200,128]{2,1,0:T(8,128)(2,1)}), bf16[16,200,128]{2,1,0:T(8,128)(2,1)S(1)}, u32[]{:S(2)}, u32[]{:S(2)}) async-start(bf16[16,200,128]{2,1,0:T(8,128)(2,1)} %get-tuple-element.48), calls=%async_computation.3 | async-start | bytes 1638400 | tf_op jit(solution)/shard_map/all_to_all | solution.py:430
  65.5 5.8 %collective-permute-start.6 = (bf16[640,128]{1,0:T(8,128)(2,1)S(1)}, bf16[640,128]{1,0:T(8,128)(2,1)S(1)}, u32[]{:S(2)}, u32[]{:S(2)}) collective-permute-start(bf16[640,128]{1,0:T(8,128)(2,1)S(1)} %add_convert_fusion.3), channel_id=1, source_target_pairs={{0,2},{2,0},{1,3},{3,1},{4,6},{6,4},{5,7},{7,5},{8,10},{10,8},{9,1... | collective-permute-start | bytes 491528 | tf_op jit(solution)/shard_map/ppermute | solution.py:420
  71.4 2.1 %collective-permute-start.7 = (bf16[640,128]{1,0:T(8,128)(2,1)S(1)}, bf16[640,128]{1,0:T(8,128)(2,1)S(1)}, u32[]{:S(2)}, u32[]{:S(2)}) collective-permute-start(bf16[640,128]{1,0:T(8,128)(2,1)S(1)} %add_convert_fusion.2.half_ref), channel_id=1, source_target_pairs={{0,1},{1,0},{2,3},{3,2},{4,5},{5,4},{6,7},{7,6},{8,9},{9,8},{10,11... | collective-permute-start | bytes 491528 | tf_op jit(solution)/shard_map/ppermute | solution.py:420
  83.2 5.3 %collective-permute-start.8 = (bf16[640,128]{1,0:T(8,128)(2,1)S(1)}, bf16[640,128]{1,0:T(8,128)(2,1)S(1)}, u32[]{:S(2)}, u32[]{:S(2)}) collective-permute-start(bf16[640,128]{1,0:T(8,128)(2,1)S(1)} %get-tuple-element.53), channel_id=1, source_target_pairs={{0,1},{1,0},{2,3},{3,2},{4,5},{5,4},{6,7},{7,6},{8,9},{9,8},{10,11... | collective-permute-start | bytes 491528 | tf_op jit(solution)/shard_map/ppermute | solution.py:420
  84.9 18.2 %all-to-all-start.4 = ((bf16[16,200,128]{2,1,0:T(8,128)(2,1)}), bf16[16,200,128]{2,1,0:T(8,128)(2,1)S(1)}, u32[]{:S(2)}, u32[]{:S(2)}) async-start(bf16[16,200,128]{2,1,0:T(8,128)(2,1)} %get-tuple-element.56), calls=%async_computation.4 | async-start | bytes 1638400 | tf_op jit(solution)/shard_map/all_to_all | solution.py:430
  88.5 8.1 %copy-start.2 = (f32[1288,128]{1,0:T(8,128)S(1)}, f32[1288,128]{1,0:T(8,128)}, u32[]{:S(2)}) copy-start(f32[1288,128]{1,0:T(8,128)} %copy-done.1) | copy-start | bytes 1978372
  88.6 5.8 %collective-permute-start.9 = (bf16[640,128]{1,0:T(8,128)(2,1)S(1)}, bf16[640,128]{1,0:T(8,128)(2,1)S(1)}, u32[]{:S(2)}, u32[]{:S(2)}) collective-permute-start(bf16[640,128]{1,0:T(8,128)(2,1)S(1)} %add_convert_fusion.1), channel_id=1, source_target_pairs={{0,2},{2,0},{1,3},{3,1},{4,6},{6,4},{5,7},{7,5},{8,10},{10,8},{9,1... | collective-permute-start | bytes 491528 | tf_op jit(solution)/shard_map/ppermute | solution.py:420
  94.5 2.2 %collective-permute-start.10 = (bf16[640,128]{1,0:T(8,128)(2,1)S(1)}, bf16[640,128]{1,0:T(8,128)(2,1)S(1)}, u32[]{:S(2)}, u32[]{:S(2)}) collective-permute-start(bf16[640,128]{1,0:T(8,128)(2,1)S(1)} %add_convert_fusion.half_ref), channel_id=1, source_target_pairs={{0,1},{1,0},{2,3},{3,2},{4,5},{5,4},{6,7},{7,6},{8,9},{9,8},{10,11... | collective-permute-start | bytes 491528 | tf_op jit(solution)/shard_map/ppermute | solution.py:420
  132.2 16.5 %collective-permute-start.15 = (bf16[80,384]{1,0:T(8,128)(2,1)S(1)}, bf16[80,384]{1,0:T(8,128)(2,1)S(1)}, u32[]{:S(2)}, u32[]{:S(2)}) collective-permute-start(bf16[80,384]{1,0:T(8,128)(2,1)S(1)} %get-tuple-element.63), channel_id=1, source_target_pairs={{0,48},{48,0},{16,32},{32,16},{1,49},{49,1},{17,33},{33,17},{2,50}... | collective-permute-start | bytes 184328 | tf_op jit(solution)/shard_map/ppermute | solution.py:434
  136.1 3.6 %collective-permute-start.11 = (f32[32,128]{1,0:T(8,128)S(1)}, f32[32,128]{1,0:T(8,128)S(1)}, u32[]{:S(2)}, u32[]{:S(2)}) collective-permute-start(f32[32,128]{1,0:T(8,128)S(1)} %reduce_sum.29), channel_id=1, source_target_pairs={{0,16},{16,0},{32,48},{48,32},{1,17},{17,1},{33,49},{49,33},{2,18}... | collective-permute-start | bytes 49160 | tf_op jit(solution)/shard_map/ppermute | solution.py:434
  139.7 16.3 %copy-start = (f32[64,16,20]{2,1,0:T(8,128)S(1)}, f32[64,16,20]{2,1,0:T(8,128)}, u32[]{:S(2)}) copy-start(f32[64,16,20]{2,1,0:T(8,128)} %constant.31.clone.table_ref) | copy-start | bytes 245764
  139.7 4.7 %collective-permute-start.12 = (f32[32,128]{1,0:T(8,128)S(1)}, f32[32,128]{1,0:T(8,128)S(1)}, u32[]{:S(2)}, u32[]{:S(2)}) collective-permute-start(f32[32,128]{1,0:T(8,128)S(1)} %add.55.one_ref), channel_id=1, source_target_pairs={{0,48},{48,0},{16,32},{32,16},{1,49},{49,1},{17,33},{33,17},{2,50}... | collective-permute-start | bytes 49160 | tf_op jit(solution)/shard_map/ppermute | solution.py:434
  145.1 10.8 %all-to-all-start.7 = ((f32[16,32,128]{2,1,0:T(8,128)}), f32[16,32,128]{2,1,0:T(8,128)S(1)}, u32[]{:S(2)}, u32[]{:S(2)}) async-start(f32[16,32,128]{2,1,0:T(8,128)} %shard_map.194), calls=%async_computation.7 | async-start | bytes 524288 | tf_op jit(solution)/shard_map/all_to_all | solution.py:430
  148.7 7.3 %copy-start.8 = (bf16[2,20]{1,0:T(2,128)(2,1)S(1)}, bf16[2,20]{1,0:T(2,128)(2,1)}, u32[]{:S(2)}) copy-start(bf16[2,20]{1,0:T(2,128)(2,1)} %gains_ref.3) | copy-start | bytes 244
  148.7 7.3 %copy-start.3 = (bf16[20,320]{1,0:T(8,128)(2,1)S(1)}, bf16[20,320]{1,0:T(8,128)(2,1)}, u32[]{:S(2)}) copy-start(bf16[20,320]{1,0:T(8,128)(2,1)} %wq_ref.3) | copy-start | bytes 38404
  148.7 7.2 %copy-start.4 = (bf16[20,320]{1,0:T(8,128)(2,1)S(1)}, bf16[20,320]{1,0:T(8,128)(2,1)}, u32[]{:S(2)}) copy-start(bf16[20,320]{1,0:T(8,128)(2,1)} %wk_ref.3) | copy-start | bytes 38404
  148.8 7.2 %copy-start.5 = (bf16[20,320]{1,0:T(8,128)(2,1)S(1)}, bf16[20,320]{1,0:T(8,128)(2,1)}, u32[]{:S(2)}) copy-start(bf16[20,320]{1,0:T(8,128)(2,1)} %wv_ref.3) | copy-start | bytes 38404
  148.8 7.2 %copy-start.7 = (bf16[32,20]{0,1:T(8,128)(2,1)S(1)}, bf16[32,20]{0,1:T(8,128)(2,1)}, u32[]{:S(2)}) copy-start(bf16[32,20]{0,1:T(8,128)(2,1)} %param.15) | copy-start | bytes 3844
  148.8 16.7 %collective-permute-start.16 = (bf16[40,384]{1,0:T(8,128)(2,1)S(1)}, bf16[40,384]{1,0:T(8,128)(2,1)S(1)}, u32[]{:S(2)}, u32[]{:S(2)}) collective-permute-start(bf16[40,384]{1,0:T(8,128)(2,1)S(1)} %slice.21), channel_id=1, source_target_pairs={{0,16},{16,0},{32,48},{48,32},{1,17},{17,1},{33,49},{49,33},{2,18}... | collective-permute-start | bytes 92168 | tf_op jit(solution)/shard_map/ppermute | solution.py:434
  157.2 7.5 %collective-permute-start.13 = (f32[24,128]{1,0:T(8,128)S(1)}, f32[24,128]{1,0:T(8,128)S(1)}, u32[]{:S(2)}, u32[]{:S(2)}) collective-permute-start(f32[24,128]{1,0:T(8,128)S(1)} %get-tuple-element.61), channel_id=1, source_target_pairs={{0,1},{1,0},{2,3},{3,2},{4,5},{5,4},{6,7},{7,6},{8,9},{9,8},{10,11... | collective-permute-start | bytes 36872 | tf_op jit(solution)/shard_map/ppermute | solution.py:420
  164.8 2.5 %collective-permute-start.14 = (f32[24,128]{1,0:T(8,128)S(1)}, f32[24,128]{1,0:T(8,128)S(1)}, u32[]{:S(2)}, u32[]{:S(2)}) collective-permute-start(f32[24,128]{1,0:T(8,128)S(1)} %add.56.one_ref), channel_id=1, source_target_pairs={{0,2},{2,0},{1,3},{3,1},{4,6},{6,4},{5,7},{7,5},{8,10},{10,8},{9,1... | collective-permute-start | bytes 36872 | tf_op jit(solution)/shard_map/ppermute | solution.py:420
  (3 other events, 8.3 us)
